TPU v7x, 256 devices: a whole 4x4x8 slice. The times are simulated.
256 devices in a mesh: seq: 32 (over x, y, core), head: 8 (over z).
Axes of the slice: x: 4, y: 4, z: 8, core: 2. Of those that a mesh axis runs over, the one named last changes fastest.
Arguments:
- queries: bfloat16 [8192, 16, 128], P('seq', 'head'), may hold values from -30 to 30
- keys: bfloat16 [8192, 16, 128], P('seq', 'head'), may hold values from -12 to 12
- values: bfloat16 [8192, 16, 128], P('seq', 'head'), may hold values from -6 to 6
- log_forget: float32 [16, 8192], P('head', 'seq'), may hold values from -1.6 to 0
- strength: float32 [16, 8192], P('head', 'seq'), may hold values from 0.05 to 1
- out_weight: bfloat16 [2048, 2048], P('head'), may hold values from -0.125 to 0.125
Outputs:
- mixed: bfloat16 [8192, 2048], P(('seq', 'head'))
All inputs are finite; a program needn't handle non-finite values.
Results may differ from a plain program's by a relative error of at most 0.018.
Values may be sent and summed in bfloat16 or wider, within the bound.
No kernel may reach another device: no remote copies, remote signals or barrier semaphores. Data moves between devices by JAX's collectives and lax.ppermute only.
A program may use at most 64 MiB of HBM per device.

v0:
```python
import jax
import jax.numpy as jnp
from jax import lax
from jax.sharding import Mesh
from jax.sharding import PartitionSpec as P

WINDOW = 1024
CG_STEPS = 6
SEQ = ("seq_0", "seq_1", "seq_2")
SEQ_HEAD = ("seq_0", "seq_1", "seq_2", "head")


ridge = 0.25
highest = lax.Precision.HIGHEST
tiny_floor = 1e-30


def shifted(x, axis, by):
    devices = lax.axis_size(axis)
    pairs = [(i, i + by) for i in range(devices) if 0 <= i + by < devices]
    return lax.ppermute(x, axis, pairs)


def filled_with(x, identity):
    return jax.tree.map(
        lambda a, e: jnp.broadcast_to(jnp.asarray(e, a.dtype), a.shape), x, identity
    )


def collected_together(x, axis):
    leaves = jax.tree.leaves(x)
    order = sorted(range(len(leaves)), key=lambda k: -leaves[k].size)
    width = (1, *leaves[order[0]].shape)[-1]
    lines = [
        jnp.pad(leaves[k].reshape(-1), (0, -leaves[k].size % width)).reshape(-1, width)
        for k in order
    ]
    both, at, found = (lax.all_gather(jnp.concatenate(lines), axis), 0, {})
    for k, line in zip(order, lines):
        piece = both[:, at : at + len(line)].reshape(len(both), -1)
        found[k] = piece[:, : leaves[k].size].reshape(-1, *leaves[k].shape)
        at += len(line)
    numbers = iter(range(len(leaves)))
    return jax.tree.map(lambda _: found[next(numbers)], x)


def carried_in(x, axes, combine, identity):
    before = start = filled_with(x, identity)
    so_far = x
    for axis in reversed(axes):
        devices, mine = (lax.axis_size(axis), lax.axis_index(axis))
        pieces = collected_together(
            jax.tree.map(
                lambda part, kind: part.astype(kind),
                so_far,
                (jnp.bfloat16, jnp.bfloat16, jnp.bfloat16),
            ),
            axis,
        )
        inside, so_far = (start, start)
        for k in range(devices):
            passed = k < mine
            so_far = combine(
                so_far, jax.tree.map(lambda part, own: part[k].astype(own.dtype), pieces, x)
            )
            inside = jax.tree.map(lambda new, old: jnp.where(passed, new, old), so_far, inside)
        before = combine(inside, before)
    return before


def in_blocks(x, dim, devices):
    lengths = x.shape
    parts = x.reshape(*lengths[:dim], devices, lengths[dim] // devices, *lengths[dim + 1 :])
    return jnp.moveaxis(parts, dim, 0)


def summed_on_arrival(x, axis, dim):
    devices = lax.axis_size(axis)
    parts = lax.all_to_all(in_blocks(x, dim, devices), axis, 0, 0, tiled=True)
    return jnp.sum(parts.astype(jnp.float32), axis=0)


def window_attention(query_rows, key_rows, value_rows, offset):
    count = query_rows.shape[0]
    block = min(512, count)
    reach = WINDOW + block
    scale = query_rows.shape[2] ** (-0.5)
    query_pos = 0 + jnp.arange(block)
    key_pos = 0 - WINDOW + jnp.arange(reach)
    admitted = (
        (key_pos[None, :] <= query_pos[:, None])
        & (key_pos[None, :] > query_pos[:, None] - WINDOW)
        & (key_pos[None, :] + offset >= 0)
    )
    scores = (
        jnp.einsum("qhe,khe->hqk", query_rows, key_rows, preferred_element_type=jnp.float32) * scale
    )
    scores = jnp.where(admitted[None], scores, -jnp.inf)
    largest = jnp.max(scores, axis=-1, keepdims=True)
    expo = jnp.exp(scores - largest)
    weights = (expo / jnp.sum(expo, axis=-1, keepdims=True)).astype(jnp.bfloat16)
    results = jnp.einsum("hqk,khe->qhe", weights, value_rows, preferred_element_type=jnp.float32)
    return results


def group_step(state, inputs):
    key_state, value_state = state
    query_part, key_part, value_part, forget_part, strength_part = inputs
    decay_sum = jnp.cumsum(forget_part, axis=1)
    length = forget_part.shape[1]
    order = jnp.arange(length)
    causal = (order[:, None] >= order[None, :])[None]
    gap = jnp.where(causal, decay_sum[:, :, None] - decay_sum[:, None, :], 0.0)
    mixing = jnp.where(causal, jnp.exp(gap), 0.0) * strength_part[:, None, :]
    leading = jnp.exp(decay_sum)[:, :, None]
    solution = jnp.zeros_like(query_part)
    residual = query_part
    direction = query_part
    norm_now = jnp.sum(residual * residual, axis=-1, keepdims=True)
    for iteration in range(CG_STEPS):
        operator_correlation = jnp.einsum("htf,hsf->hts", direction, key_part, precision=highest)
        carried = jnp.einsum("htf,hef->hte", direction, key_state, precision=highest)
        inside = jnp.einsum(
            "hts,hse->hte", mixing * operator_correlation, key_part, precision=highest
        )
        image = leading * carried + inside + ridge * direction
        alpha = norm_now / jnp.maximum(
            jnp.sum(direction * image, axis=-1, keepdims=True), tiny_floor
        )
        solution = solution + alpha * direction
        residual = residual - alpha * image
        norm_next = jnp.sum(residual * residual, axis=-1, keepdims=True)
        direction = residual + norm_next / jnp.maximum(norm_now, tiny_floor) * direction
        norm_now = norm_next
    correlation = jnp.einsum("htf,hsf->hts", solution, key_part, precision=highest)
    output = leading * jnp.einsum("htf,hef->hte", solution, value_state, precision=highest)
    output = output + jnp.einsum(
        "hts,hse->hte", mixing * correlation, value_part, precision=highest
    )
    tail = jnp.exp(decay_sum[:, -1:] - decay_sum) * strength_part
    end_factor = jnp.exp(decay_sum[:, -1])[:, None, None]
    key_state = end_factor * key_state + jnp.einsum(
        "hse,hsf->hef", tail[:, :, None] * key_part, key_part, precision=highest
    )
    value_state = end_factor * value_state + jnp.einsum(
        "hse,hsf->hef", tail[:, :, None] * value_part, key_part, precision=highest
    )
    return ((key_state, value_state), output)


def normalized(rows):
    wide = rows.astype(jnp.float32)
    return wide * lax.rsqrt(jnp.sum(wide * wide, axis=-1, keepdims=True) + 1e-06)


def mesa_heads(query_rows, key_rows, value_rows, log_forget, strength, key_start, value_start):
    heads_here, count, width = query_rows.shape
    group = min(256, count)
    blocks = count // group

    def blocked(array):
        shaped = array.reshape((heads_here, blocks, group) + array.shape[2:])
        return jnp.moveaxis(shaped, 1, 0)

    inputs = (
        blocked(query_rows),
        blocked(key_rows),
        blocked(value_rows),
        blocked(log_forget),
        blocked(strength),
    )
    final, outputs = lax.scan(group_step, (key_start, value_start), inputs)
    return jnp.moveaxis(outputs, 0, 1).reshape(heads_here, count, width)


def join_states(earlier, later):
    factor = jnp.exp(later[0])[:, None, None]
    return (earlier[0] + later[0], factor * earlier[1] + later[1], factor * earlier[2] + later[2])


def on_device(queries, keys, values, log_forget, strength, out_weight):
    tok_rows, heads_dev, width = queries.shape
    position = lax.axis_index(SEQ)
    halo_rows = min(tok_rows, WINDOW)
    distance_count = WINDOW // halo_rows
    stacked = jnp.stack((keys, values))
    earlier_parts = []
    for distance in range(distance_count, 0, -1):
        earlier_parts.append(shifted(stacked, SEQ, distance))
    earlier_rows = jnp.concatenate(earlier_parts, axis=1)
    key_window = jnp.concatenate((earlier_rows[0], keys), axis=0)
    value_window = jnp.concatenate((earlier_rows[1], values), axis=0)
    attended = window_attention(queries, key_window, value_window, position * tok_rows)
    query_norm = jnp.transpose(normalized(queries), (1, 0, 2))
    key_norm = jnp.transpose(normalized(keys), (1, 0, 2))
    value_wide = jnp.transpose(values.astype(jnp.float32), (1, 0, 2))
    decay_sum = jnp.cumsum(log_forget, axis=1)
    decay_total = decay_sum[:, -1]
    tail = jnp.exp(decay_total[:, None] - decay_sum) * strength
    key_local = jnp.einsum("hse,hsf->hef", tail[:, :, None] * key_norm, key_norm, precision=highest)
    value_local = jnp.einsum(
        "hse,hsf->hef", tail[:, :, None] * value_wide, key_norm, precision=highest
    )
    empty = jnp.zeros((heads_dev, width, width), jnp.float32)
    identity = (jnp.zeros((heads_dev,), jnp.float32), empty, empty)
    prefix_state = carried_in((decay_total, key_local, value_local), SEQ, join_states, identity)
    key_start, value_start = (prefix_state[1], prefix_state[2])
    mesa = mesa_heads(
        query_norm, key_norm, value_wide, log_forget, strength, key_start, value_start
    )
    head_out = (attended + jnp.transpose(mesa, (1, 0, 2))).astype(jnp.bfloat16)
    flat_local = head_out.reshape(tok_rows, heads_dev * width)
    return summed_on_arrival(
        jnp.dot(flat_local, out_weight, preferred_element_type=jnp.float32).astype(jnp.bfloat16),
        "head",
        0,
    ).astype(jnp.bfloat16)


def solution(mesh):
    split = Mesh(
        mesh.devices.reshape(4, 4, 2, mesh.shape["head"]), ("seq_0", "seq_1", "seq_2", "head")
    )
    in_specs = (
        P(SEQ, "head", None),
        P(SEQ, "head", None),
        P(SEQ, "head", None),
        P("head", SEQ),
        P("head", SEQ),
        P("head", None),
    )
    out_specs = P(SEQ_HEAD, None)
    return jax.shard_map(
        on_device, mesh=split, in_specs=in_specs, out_specs=out_specs, check_vma=False
    )
```

profile of v0, /device:TPU:2, one launch (start us, length us, event | category | flops | bytes accessed | tf_op | source)
XLA Modules:
  0.0 118.7 jit_solution(7778877253162754717)
XLA Ops:
  0.0 1.8 %copy_bitcast_fusion.5 = (bf16[1,256,2,128]{3,1,2,0:T(8,128)(2,1)S(1)}, bf16[256,2,128]{2,0,1:T(8,128)(2,1)}, bf16[1,256,2,128]{3,1,2,0:T(8,128)(2,1)S(1)}, bf16[256,2,128]{2,0,1:T(8,128)(2,1)}) fusion(bf16[256,2,128]{2,1,0:T(2,128)(2,1)} %param.7, bf16[256,2,128]{2,1,0:T(2,128)(2,1)} %param.8), kind=kLoop, calls=%fused_computation.316 | loop fusion | bytes 786432 | tf_op jit(solution)/shard_map/stack | solution.py:186
  1.9 0.7 pad_maximum_fusion
  2.6 5.1 %collective-permute-start = (bf16[2,256,2,128]{3,1,2,0:T(8,128)(2,1)}, bf16[2,256,2,128]{3,1,2,0:T(8,128)(2,1)}, u32[]{:S(2)}, u32[]{:S(2)}) collective-permute-start(bf16[2,256,2,128]{3,1,2,0:T(8,128)(2,1)} %pad_maximum_fusion), channel_id=1, source_target_pairs={{0,32},{8,40},{16,48},{24,56},{32,64},{40,72},{48,80},{56,88},{64,... | collective-permute-start | bytes 786440 | tf_op jit(solution)/shard_map/ppermute | solution.py:21
  7.7 1.9 %collective-permute-start.1 = (bf16[2,256,2,128]{3,1,2,0:T(8,128)(2,1)}, bf16[2,256,2,128]{3,1,2,0:T(8,128)(2,1)}, u32[]{:S(2)}, u32[]{:S(2)}) collective-permute-start(bf16[2,256,2,128]{3,1,2,0:T(8,128)(2,1)} %pad_maximum_fusion), channel_id=1, source_target_pairs={{0,24},{8,32},{16,40},{24,48},{32,56},{40,64},{48,72},{56,80},{64,... | collective-permute-start | bytes 786440 | tf_op jit(solution)/shard_map/ppermute | solution.py:21
  9.6 2.6 %collective-permute-start.2 = (bf16[2,256,2,128]{3,1,2,0:T(8,128)(2,1)}, bf16[2,256,2,128]{3,1,2,0:T(8,128)(2,1)}, u32[]{:S(2)}, u32[]{:S(2)}) collective-permute-start(bf16[2,256,2,128]{3,1,2,0:T(8,128)(2,1)} %pad_maximum_fusion), channel_id=1, source_target_pairs={{0,16},{8,24},{16,32},{24,40},{32,48},{40,56},{48,64},{56,72},{64,... | collective-permute-start | bytes 786440 | tf_op jit(solution)/shard_map/ppermute | solution.py:21
  12.2 3.9 %collective-permute-start.3 = (bf16[2,256,2,128]{3,1,2,0:T(8,128)(2,1)}, bf16[2,256,2,128]{3,1,2,0:T(8,128)(2,1)}, u32[]{:S(2)}, u32[]{:S(2)}) collective-permute-start(bf16[2,256,2,128]{3,1,2,0:T(8,128)(2,1)} %pad_maximum_fusion), channel_id=1, source_target_pairs={{0,8},{8,16},{16,24},{24,32},{32,40},{40,48},{48,56},{56,64},{64,7... | collective-permute-start | bytes 786440 | tf_op jit(solution)/shard_map/ppermute | solution.py:21
  16.1 0.6 iota_add_fusion.1
  16.7 0.6 iota_add_fusion
  17.3 0.1 fusion.48
  17.5 0.6 reduce-window.12
  18.1 0.2 slice_reduce_fusion
  18.3 0.2 reduce-window.13
  18.4 0.1 add_bitcast_fusion
  18.5 0.2 slice_reduce_fusion.1
  18.7 0.6 exponential_bitcast_fusion.9
  19.3 0.8 convolution_convert_fusion.1
  20.1 0.9 convolution_convert_fusion.2
  21.0 2.0 %all-gather.3 = bf16[2,513,128]{2,1,0:T(8,128)(2,1)S(1)} all-gather(bf16[1,513,128]{2,1,0:T(8,128)(2,1)S(1)} %maximum_bitcast_fusion), channel_id=2, replica_groups=mesh['seq_0'=4,'seq_1'=4,'seq_2'=2,'head'=8] {'seq_2'}, dimensions={0}, use_global_device_ids=true | all-gather | bytes 393984 | tf_op jit(solution)/shard_map/all_gather | solution.py:38
  23.0 0.8 slice_convert_fusion.9
  23.9 0.1 fusion.93
  24.1 14.1 %all-gather.4 = bf16[4,513,128]{2,1,0:T(8,128)(2,1)S(1)} all-gather(bf16[1,513,128]{2,1,0:T(8,128)(2,1)S(1)} %maximum_bitcast_fusion.1), channel_id=3, replica_groups=mesh['seq_0'=4,'seq_1'=4,'seq_2'=2,'head'=8] {'seq_1'}, dimensions={0}, use_global_device_ids=true | all-gather | bytes 656640 | tf_op jit(solution)/shard_map/all_gather | solution.py:38
  38.2 0.8 slice_convert_fusion.3
  39.4 0.2 fusion.87
  39.7 13.3 %all-gather.5 = bf16[4,513,128]{2,1,0:T(8,128)(2,1)S(1)} all-gather(bf16[1,513,128]{2,1,0:T(8,128)(2,1)S(1)} %maximum_bitcast_fusion.2), channel_id=4, replica_groups=mesh['seq_0'=4,'seq_1'=4,'seq_2'=2,'head'=8] {'seq_0'}, dimensions={0}, use_global_device_ids=true | all-gather | bytes 656640 | tf_op jit(solution)/shard_map/all_gather | solution.py:38
  52.9 0.7 fusion.197
  53.7 0.1 copy.158
  54.0 0.8 convolution_multiply_fusion.7
  54.8 0.3 fusion.78
  55.2 0.4 convolution_multiply_fusion.13
  55.6 0.9 fusion.41
  56.5 0.1 multiply_reduce_fusion.8
  56.6 0.4 convolution_multiply_fusion.12
  57.0 0.8 convolution_multiply_fusion.6
  57.8 0.9 multiply_reduce_fusion.7
  58.7 0.1 multiply_reduce_fusion.6
  58.9 0.4 convolution_multiply_fusion.11
  59.3 0.8 convolution_multiply_fusion.5
  60.1 0.9 multiply_reduce_fusion.5
  61.1 0.4 convolution_multiply_fusion.10
  61.5 0.8 convolution_multiply_fusion.4
  62.3 0.9 multiply_reduce_fusion.3
  63.3 0.4 convolution_multiply_fusion.9
  63.8 0.8 convolution_multiply_fusion.3
  64.6 0.9 multiply_reduce_fusion.1
  65.6 0.6 copy-done.22
  66.2 0.4 convolution_multiply_fusion.8
  66.6 0.8 convolution_multiply_fusion.2
  67.5 1.1 fusion.20
  68.6 0.7 maximum_divide_fusion
  69.5 1.1 fusion.46
  70.6 1.6 %fusion.7 = pred[256,1280]{0,1:T(8,128)(4,1)} fusion(s32[256]{0:T(256)S(1)} %copy-done.55, s32[1280]{0:T(1024)S(1)} %copy-done.18, pred[1280]{0:T(1024)(128)(4,1)S(1)} %add_compare_fusion), kind=kLoop, calls=%fused_computation.11 | loop fusion | flops 1310720 | bytes 335104 | tf_op jit(solution)/shard_map/and | solution.py:91
  72.4 0.6 fusion.9
  73.0 0.8 convolution_multiply_fusion.1
  73.8 1.0 constant_dynamic-update-slice_fusion.3
  74.8 1.0 constant_dynamic-update-slice_fusion.2
  75.8 1.0 constant_dynamic-update-slice_fusion.1
  76.8 1.0 constant_dynamic-update-slice_fusion
  77.9 0.8 copy-done.14
  78.7 1.9 %fusion.199 = f32[2,256]{1,0:T(2,128)S(1)} fusion(bf16[256,2,128]{0,2,1:T(8,128)(2,1)S(1)} %copy.158, pred[256,1280]{0,1:T(8,128)(4,1)} %fusion.7, bf16[256,2,128]{2,0,1:T(8,128)(2,1)S(1)} %copy-done.14, bf16[1024,2,128]{2,0,1:T(8,128)(2,1)S(1)} %get-tuple-element.44), kind=kOutput, calls=%fused_computation.319 | convolution fusion | flops 171705600 | bytes 1116160 | tf_op jit(solution)/shard_map/sub | solution.py:100
  80.6 2.5 %fusion.18 = f32[256,2,128]{0,2,1:T(8,128)S(1)} fusion(f32[2,256]{1,0:T(2,128)S(1)} %fusion.199, bf16[256,2,128]{2,0,1:T(8,128)(2,1)} %get-tuple-element.97, bf16[1024,2,128]{2,0,1:T(8,128)(2,1)S(1)} %get-tuple-element.43, bf16[256,2,128]{0,2,1:T(8,128)(2,1)S(1)} %copy.158, pred[256,1280]{0,1:T(8,128)(4,1)} %fusion.7, ...), kind=kOutput, calls=%fused_computation.43 | convolution fusion | flops 341444352 | bytes 2033664 | tf_op jit(solution)/shard_map/hqk,khe->qhe/dot_general | solution.py:102
  83.1 0.4 fusion.19
  83.5 0.5 convolution_convert_fusion
  84.0 33.9 %all_to_all.5 = bf16[8,32,2048]{2,1,0:T(8,128)(2,1)S(1)} all-to-all(bf16[8,32,2048]{2,1,0:T(8,128)(2,1)S(1)} %bitcast.315), channel_id=1, replica_groups=mesh['seq_0'=4,'seq_1'=4,'seq_2'=2,'head'=8] {'head'}, dimensions={0} | all-to-all | bytes 2097152 | tf_op jit(solution)/shard_map/all_to_all | solution.py:79
  117.9 0.8 reduce_sum.174
  (163 shorter events, 1.4 us)
Async XLA Ops:
  0.0 83.5 %copy-start = (bf16[256,2048]{1,0:T(8,128)(2,1)S(1)}, bf16[256,2048]{1,0:T(8,128)(2,1)}, u32[]{:S(2)}) copy-start(bf16[256,2048]{1,0:T(8,128)(2,1)} %param.11) | copy-start | bytes 3145732
  0.0 17.3 %copy-start.1 = (bf16[256,2,128]{2,1,0:T(2,128)(2,1)S(1)}, bf16[256,2,128]{2,1,0:T(2,128)(2,1)}, u32[]{:S(2)}) copy-start(bf16[256,2,128]{2,1,0:T(2,128)(2,1)} %param.7) | copy-start | bytes 393220
  0.0 19.3 %copy-start.2 = (bf16[256,2,128]{2,1,0:T(2,128)(2,1)S(1)}, bf16[256,2,128]{2,1,0:T(2,128)(2,1)}, u32[]{:S(2)}) copy-start(bf16[256,2,128]{2,1,0:T(2,128)(2,1)} %param.8) | copy-start | bytes 393220
  0.0 17.4 %copy-start.48 = (f32[2,256]{1,0:T(2,128)S(1)}, f32[2,256]{1,0:T(2,128)}, u32[]{:S(2)}) copy-start(f32[2,256]{1,0:T(2,128)} %param.9) | copy-start | bytes 6148
  0.0 18.7 %copy-start.52 = (f32[2,256]{1,0:T(2,128)S(1)}, f32[2,256]{1,0:T(2,128)}, u32[]{:S(2)}) copy-start(f32[2,256]{1,0:T(2,128)} %param.10) | copy-start | bytes 6148
  2.6 71.2 %collective-permute-start = (bf16[2,256,2,128]{3,1,2,0:T(8,128)(2,1)}, bf16[2,256,2,128]{3,1,2,0:T(8,128)(2,1)}, u32[]{:S(2)}, u32[]{:S(2)}) collective-permute-start(bf16[2,256,2,128]{3,1,2,0:T(8,128)(2,1)} %pad_maximum_fusion), channel_id=1, source_target_pairs={{0,32},{8,40},{16,48},{24,56},{32,64},{40,72},{48,80},{56,88},{64,... | collective-permute-start | bytes 786440 | tf_op jit(solution)/shard_map/ppermute | solution.py:21
  7.7 67.1 %collective-permute-start.1 = (bf16[2,256,2,128]{3,1,2,0:T(8,128)(2,1)}, bf16[2,256,2,128]{3,1,2,0:T(8,128)(2,1)}, u32[]{:S(2)}, u32[]{:S(2)}) collective-permute-start(bf16[2,256,2,128]{3,1,2,0:T(8,128)(2,1)} %pad_maximum_fusion), channel_id=1, source_target_pairs={{0,24},{8,32},{16,40},{24,48},{32,56},{40,64},{48,72},{56,80},{64,... | collective-permute-start | bytes 786440 | tf_op jit(solution)/shard_map/ppermute | solution.py:21
  9.6 66.2 %collective-permute-start.2 = (bf16[2,256,2,128]{3,1,2,0:T(8,128)(2,1)}, bf16[2,256,2,128]{3,1,2,0:T(8,128)(2,1)}, u32[]{:S(2)}, u32[]{:S(2)}) collective-permute-start(bf16[2,256,2,128]{3,1,2,0:T(8,128)(2,1)} %pad_maximum_fusion), channel_id=1, source_target_pairs={{0,16},{8,24},{16,32},{24,40},{32,48},{40,56},{48,64},{56,72},{64,... | collective-permute-start | bytes 786440 | tf_op jit(solution)/shard_map/ppermute | solution.py:21
  12.2 64.6 %collective-permute-start.3 = (bf16[2,256,2,128]{3,1,2,0:T(8,128)(2,1)}, bf16[2,256,2,128]{3,1,2,0:T(8,128)(2,1)}, u32[]{:S(2)}, u32[]{:S(2)}) collective-permute-start(bf16[2,256,2,128]{3,1,2,0:T(8,128)(2,1)} %pad_maximum_fusion), channel_id=1, source_target_pairs={{0,8},{8,16},{16,24},{24,32},{32,40},{40,48},{48,56},{56,64},{64,7... | collective-permute-start | bytes 786440 | tf_op jit(solution)/shard_map/ppermute | solution.py:21
  18.5 45.2 %copy-start.49 = (f32[1,2,2,128]{3,1,2,0:T(2,128)}, f32[1,2,2,128]{3,1,2,0:T(2,128)S(1)}, u32[]{:S(2)}) copy-start(f32[1,2,2,128]{3,1,2,0:T(2,128)S(1)} %copy.314) | copy-start | bytes 6148
  23.8 31.0 %copy-start.23 = (f32[2]{0:T(128)}, f32[2]{0:T(128)S(1)}, u32[]{:S(2)}) copy-start(f32[2]{0:T(128)S(1)} %get-tuple-element.84) | copy-start | bytes 28
  23.8 31.0 %copy-start.25 = (f32[2]{0:T(128)}, f32[2]{0:T(128)S(1)}, u32[]{:S(2)}) copy-start(f32[2]{0:T(128)S(1)} %get-tuple-element.86) | copy-start | bytes 28
  39.1 15.7 %copy-start.28 = (f32[2]{0:T(128)}, f32[2]{0:T(128)S(1)}, u32[]{:S(2)}) copy-start(f32[2]{0:T(128)S(1)} %get-tuple-element.40) | copy-start | bytes 28
  39.1 15.7 %copy-start.30 = (f32[2]{0:T(128)}, f32[2]{0:T(128)S(1)}, u32[]{:S(2)}) copy-start(f32[2]{0:T(128)S(1)} %get-tuple-element.80) | copy-start | bytes 28
  39.1 15.7 %copy-start.32 = (f32[2]{0:T(128)}, f32[2]{0:T(128)S(1)}, u32[]{:S(2)}) copy-start(f32[2]{0:T(128)S(1)} %get-tuple-element.81) | copy-start | bytes 28
  39.1 15.7 %copy-start.34 = (f32[2]{0:T(128)}, f32[2]{0:T(128)S(1)}, u32[]{:S(2)}) copy-start(f32[2]{0:T(128)S(1)} %get-tuple-element.82) | copy-start | bytes 28
  39.1 15.7 %copy-start.36 = (f32[2]{0:T(128)}, f32[2]{0:T(128)S(1)}, u32[]{:S(2)}) copy-start(f32[2]{0:T(128)S(1)} %get-tuple-element.83) | copy-start | bytes 28
  39.6 14.0 %copy-start.13 = (bf16[256,2,128]{2,1,0:T(2,128)(2,1)S(1)}, bf16[256,2,128]{2,1,0:T(2,128)(2,1)}, u32[]{:S(2)}) copy-start(bf16[256,2,128]{2,1,0:T(2,128)(2,1)} %param.6) | copy-start | bytes 393220
  53.7 10.1 %copy-start.15 = (pred[256,256]{1,0:T(8,128)(4,1)}, pred[256,256]{1,0:T(8,128)(4,1)S(1)}, u32[]{:S(2)}) copy-start(pred[256,256]{1,0:T(8,128)(4,1)S(1)} %iota_compare_fusion.1) | copy-start | bytes 196612
  53.9 1.2 %copy-start.46 = (f32[2]{0:T(128)}, f32[2]{0:T(128)S(1)}, u32[]{:S(2)}) copy-start(f32[2]{0:T(128)S(1)} %exponential_bitcast_fusion.1) | copy-start | bytes 28
  53.9 1.2 %copy-start.38 = (f32[2]{0:T(128)}, f32[2]{0:T(128)S(1)}, u32[]{:S(2)}) copy-start(f32[2]{0:T(128)S(1)} %get-tuple-element.76) | copy-start | bytes 28
  53.9 1.2 %copy-start.40 = (f32[2]{0:T(128)}, f32[2]{0:T(128)S(1)}, u32[]{:S(2)}) copy-start(f32[2]{0:T(128)S(1)} %get-tuple-element.77) | copy-start | bytes 28
  53.9 1.2 %copy-start.42 = (f32[2]{0:T(128)}, f32[2]{0:T(128)S(1)}, u32[]{:S(2)}) copy-start(f32[2]{0:T(128)S(1)} %get-tuple-element.78) | copy-start | bytes 28
  53.9 1.2 %copy-start.44 = (f32[2]{0:T(128)}, f32[2]{0:T(128)S(1)}, u32[]{:S(2)}) copy-start(f32[2]{0:T(128)S(1)} %get-tuple-element.79) | copy-start | bytes 28
  58.7 2.4 %copy-start.19 = (f32[2,256]{1,0:T(2,128)}, f32[2,256]{1,0:T(2,128)S(1)}, u32[]{:S(2)}) copy-start(f32[2,256]{1,0:T(2,128)S(1)} %maximum_divide_fusion.8) | copy-start | bytes 6148
  61.0 2.4 %copy-start.20 = (f32[2,256]{1,0:T(2,128)}, f32[2,256]{1,0:T(2,128)S(1)}, u32[]{:S(2)}) copy-start(f32[2,256]{1,0:T(2,128)S(1)} %maximum_divide_fusion.6) | copy-start | bytes 6148
  63.2 0.6 copy-start.21
  65.5 1.2 copy-start.16
  65.5 1.2 copy-start.50
  65.5 1.2 copy-start.53
  65.5 0.6 copy-start.22
  68.5 2.0 %copy-start.18 = (s32[1280]{0:T(1024)S(1)}, s32[1280]{0:T(1024)}, u32[]{:S(2)}) copy-start(s32[1280]{0:T(1024)} %iota_add_fusion) | copy-start | bytes 15364
  68.5 2.0 %copy-start.55 = (s32[256]{0:T(256)S(1)}, s32[256]{0:T(256)}, u32[]{:S(2)}) copy-start(s32[256]{0:T(256)} %iota_add_fusion.1) | copy-start | bytes 3076
  69.2 2.9 %copy-start.3 = (f32[1,256,128]{2,1,0:T(8,128)S(1)}, f32[1,256,128]{2,1,0:T(8,128)}, u32[]{:S(2)}) copy-start(f32[1,256,128]{2,1,0:T(8,128)} %get-tuple-element.55) | copy-start | bytes 393220
  69.2 2.9 %copy-start.4 = (f32[1,256,128]{2,1,0:T(8,128)S(1)}, f32[1,256,128]{2,1,0:T(8,128)}, u32[]{:S(2)}) copy-start(f32[1,256,128]{2,1,0:T(8,128)} %get-tuple-element.56) | copy-start | bytes 393220
  69.2 2.9 %copy-start.5 = (f32[1,256,128]{2,1,0:T(8,128)S(1)}, f32[1,256,128]{2,1,0:T(8,128)}, u32[]{:S(2)}) copy-start(f32[1,256,128]{2,1,0:T(8,128)} %get-tuple-element.57) | copy-start | bytes 393220
  69.3 2.9 %copy-start.6 = (f32[1,256,128]{2,1,0:T(8,128)S(1)}, f32[1,256,128]{2,1,0:T(8,128)}, u32[]{:S(2)}) copy-start(f32[1,256,128]{2,1,0:T(8,128)} %get-tuple-element.62) | copy-start | bytes 393220
  69.3 2.9 %copy-start.7 = (f32[1,256,128]{2,1,0:T(8,128)S(1)}, f32[1,256,128]{2,1,0:T(8,128)}, u32[]{:S(2)}) copy-start(f32[1,256,128]{2,1,0:T(8,128)} %get-tuple-element.65) | copy-start | bytes 393220
  69.3 2.9 %copy-start.8 = (f32[1,256,128]{2,1,0:T(8,128)S(1)}, f32[1,256,128]{2,1,0:T(8,128)}, u32[]{:S(2)}) copy-start(f32[1,256,128]{2,1,0:T(8,128)} %get-tuple-element.68) | copy-start | bytes 393220
  69.3 2.9 %copy-start.9 = (bf16[1,256,128]{2,1,0:T(8,128)(2,1)S(1)}, bf16[1,256,128]{2,1,0:T(8,128)(2,1)}, u32[]{:S(2)}) copy-start(bf16[1,256,128]{2,1,0:T(8,128)(2,1)} %get-tuple-element.47) | copy-start | bytes 196612
  69.3 2.9 %copy-start.10 = (bf16[1,256,128]{2,1,0:T(8,128)(2,1)S(1)}, bf16[1,256,128]{2,1,0:T(8,128)(2,1)}, u32[]{:S(2)}) copy-start(bf16[1,256,128]{2,1,0:T(8,128)(2,1)} %get-tuple-element.48) | copy-start | bytes 196612
  69.3 2.9 %copy-start.11 = (bf16[1,256,128]{2,1,0:T(8,128)(2,1)S(1)}, bf16[1,256,128]{2,1,0:T(8,128)(2,1)}, u32[]{:S(2)}) copy-start(bf16[1,256,128]{2,1,0:T(8,128)(2,1)} %get-tuple-element.49) | copy-start | bytes 196612
  69.3 2.9 %copy-start.12 = (bf16[1,256,128]{2,1,0:T(8,128)(2,1)S(1)}, bf16[1,256,128]{2,1,0:T(8,128)(2,1)}, u32[]{:S(2)}) copy-start(bf16[1,256,128]{2,1,0:T(8,128)(2,1)} %get-tuple-element.54) | copy-start | bytes 196612
  69.3 2.9 %copy-start.24 = (f32[2]{0:T(128)S(1)}, f32[2]{0:T(128)}, u32[]{:S(2)}) copy-start(f32[2]{0:T(128)} %copy-done.23) | copy-start | bytes 28
  69.3 2.9 %copy-start.26 = (f32[2]{0:T(128)S(1)}, f32[2]{0:T(128)}, u32[]{:S(2)}) copy-start(f32[2]{0:T(128)} %copy-done.25) | copy-start | bytes 28
  69.3 2.9 %copy-start.27 = (f32[256,2]{0,1:T(2,128)S(1)}, f32[256,2]{0,1:T(2,128)}, u32[]{:S(2)}) copy-start(f32[256,2]{0,1:T(2,128)} %get-tuple-element.73) | copy-start | bytes 6148
  69.4 2.9 %copy-start.29 = (f32[2]{0:T(128)S(1)}, f32[2]{0:T(128)}, u32[]{:S(2)}) copy-start(f32[2]{0:T(128)} %copy-done.28) | copy-start | bytes 28
  69.4 2.9 %copy-start.31 = (f32[2]{0:T(128)S(1)}, f32[2]{0:T(128)}, u32[]{:S(2)}) copy-start(f32[2]{0:T(128)} %copy-done.30) | copy-start | bytes 28
  69.4 2.9 %copy-start.33 = (f32[2]{0:T(128)S(1)}, f32[2]{0:T(128)}, u32[]{:S(2)}) copy-start(f32[2]{0:T(128)} %copy-done.32) | copy-start | bytes 28
  69.4 2.9 %copy-start.35 = (f32[2]{0:T(128)S(1)}, f32[2]{0:T(128)}, u32[]{:S(2)}) copy-start(f32[2]{0:T(128)} %copy-done.34) | copy-start | bytes 28
  69.4 2.9 %copy-start.37 = (f32[2]{0:T(128)S(1)}, f32[2]{0:T(128)}, u32[]{:S(2)}) copy-start(f32[2]{0:T(128)} %copy-done.36) | copy-start | bytes 28
  69.4 2.9 %copy-start.39 = (f32[2]{0:T(128)S(1)}, f32[2]{0:T(128)}, u32[]{:S(2)}) copy-start(f32[2]{0:T(128)} %copy-done.38) | copy-start | bytes 28
  69.4 2.9 %copy-start.41 = (f32[2]{0:T(128)S(1)}, f32[2]{0:T(128)}, u32[]{:S(2)}) copy-start(f32[2]{0:T(128)} %copy-done.40) | copy-start | bytes 28
  69.4 2.9 %copy-start.43 = (f32[2]{0:T(128)S(1)}, f32[2]{0:T(128)}, u32[]{:S(2)}) copy-start(f32[2]{0:T(128)} %copy-done.42) | copy-start | bytes 28
  69.4 2.9 %copy-start.45 = (f32[2]{0:T(128)S(1)}, f32[2]{0:T(128)}, u32[]{:S(2)}) copy-start(f32[2]{0:T(128)} %copy-done.44) | copy-start | bytes 28
  69.4 2.9 %copy-start.47 = (f32[2]{0:T(128)S(1)}, f32[2]{0:T(128)}, u32[]{:S(2)}) copy-start(f32[2]{0:T(128)} %copy-done.46) | copy-start | bytes 28
  70.5 2.4 %copy-start.17 = (pred[256,256]{1,0:T(8,128)(4,1)S(1)}, pred[256,256]{1,0:T(8,128)(4,1)}, u32[]{:S(2)}) copy-start(pred[256,256]{1,0:T(8,128)(4,1)} %copy-done.15) | copy-start | bytes 196612
  70.5 2.4 %copy-start.51 = (f32[1,2,2,128]{3,1,2,0:T(2,128)S(1)}, f32[1,2,2,128]{3,1,2,0:T(2,128)}, u32[]{:S(2)}) copy-start(f32[1,2,2,128]{3,1,2,0:T(2,128)} %copy-done.49) | copy-start | bytes 6148
  70.6 2.4 %copy-start.54 = (f32[2,256]{1,0:T(2,128)S(1)}, f32[2,256]{1,0:T(2,128)}, u32[]{:S(2)}) copy-start(f32[2,256]{1,0:T(2,128)} %param.10) | copy-start | bytes 6148
  77.8 0.9 copy-start.14
where the time goes:
time: 119 us
  blocking collectives  63.2 us (53%)
  matrix products  20.9 us (18%)
  starting transfers between devices  13.5 us (11%)
  other arithmetic  10.7 us (9%)
  local copies, waits for them, and re-layouts  9.07 us (8%)
  between operations  1.3 us (1%)
    all_to_all x1, blocking collectives, summed_on_arrival(): parts = lax.all_to_all(in_blocks(x, dim, devices), axis, 0, 0, tiled=True)  33.9 us
    all_gather x3, blocking collectives, collected_together(): both, at, found = (lax.all_gather(jnp.concatenate(lines), axis), 0, {})  29.3 us
    ppermute x4, starting transfers between devices, shifted(): return lax.ppermute(x, axis, pairs)  13.5 us
    dot_general x6, matrix products, group_step(): jnp.einsum('hts,hse->hte', mixing * operator_correlation, key_part, preci...  5.33 us
    dot_general x6, matrix products, group_step(): jnp.einsum('htf,hsf->hts', direction, key_part, precision=highest)  4.87 us
    unnamed x120, local copies, waits for them, and re-layouts  4.72 us
    dot_general x1, matrix products, window_attention(): jnp.einsum('hqk,khe->qhe', weights, value_rows, preferred_element_type=jn...  2.47 us
  transfers between devices with their start and end apart: 4, of which 0 were waited for; matrix products, arithmetic and copies ran while one was open for 25% of the time, Pallas kernels for 0%

commit v1 on v0

v1 whole, which is shorter than its diff:
```python
import jax
import jax.numpy as jnp
from jax import lax
from jax.experimental import pallas as pl
from jax.experimental.pallas import tpu as pltpu
from jax.sharding import Mesh
from jax.sharding import PartitionSpec as P

WINDOW = 1024
CG_STEPS = 6
RIDGE = 0.25
TINY = 1e-30
LOW = -1e30
HALF = 256
E = 128
CHIP = 2 * HALF
ROWS = 2 * E + 16
SEQ = ("x", "y", "c")
XY = ("x", "y")
f32 = jnp.float32
bf16 = jnp.bfloat16


def spec(kind=pltpu.VMEM):
    return pl.BlockSpec(memory_space=kind)


def call(body, outs, scratch, flops, *args):
    return pl.pallas_call(
        body,
        out_shape=[jax.ShapeDtypeStruct(shape, kind) for shape, kind in outs],
        in_specs=[spec(pltpu.SMEM)] + [spec()] * (len(args) - 1),
        out_specs=[spec()] * len(outs),
        scratch_shapes=[pltpu.VMEM(shape, kind) for shape, kind in scratch],
        cost_estimate=pl.CostEstimate(flops=flops, bytes_accessed=1 << 20, transcendentals=0),
    )(*args)


def split(x):
    high = x.astype(bf16)
    return high, (x - high.astype(f32)).astype(bf16)


def dot(a, b):
    return jnp.dot(a, b, preferred_element_type=f32)


def two_part(a, b):
    high, low = split(b)
    return dot(a, high) + dot(a, low)


def iotas(shape):
    return lax.broadcasted_iota(jnp.int32, shape, 0), lax.broadcasted_iota(jnp.int32, shape, 1)


def payload(state, total):
    high, low = split(total)
    row, _ = iotas((16, E))
    tail = jnp.where(row == 0, high.astype(f32), jnp.where(row == 1, low.astype(f32), 0.0))
    return jnp.concatenate((state, tail), axis=0).astype(bf16)


def decay_row(tail):
    wide = tail.astype(f32)
    return wide[0:1, :] + wide[1:2, :]


def gram_body(pos, keep, recv, gate_keep, gate_recv, q_out, kv_out, gates_out, pay_out, first_out):
    core = pos[0]
    for source, which in ((keep, core), (recv, 1 - core)):
        rows = pl.ds(pl.multiple_of(which * HALF, HALF), HALF)
        q_out[rows, :] = source[0]
        kv_out[0, rows, :] = source[1]
        kv_out[1, rows, :] = source[2]
    a, b = gate_keep[...], gate_recv[...]
    first, second = jnp.where(core == 0, a, b), jnp.where(core == 0, b, a)
    forget = jnp.concatenate((first[0:1], second[0:1], jnp.zeros((6, HALF), f32)), axis=0)
    row, col = iotas((HALF, HALF))
    upto = (row <= col).astype(f32)
    sums = jnp.dot(forget, upto, preferred_element_type=f32, precision=lax.Precision.HIGHEST)
    gates_out[...] = jnp.concatenate(
        (sums[0:2], first[1:2], second[1:2], jnp.zeros((4, HALF), f32)), axis=0
    )
    grams = []
    for j in range(2):
        own = slice(j * HALF, (j + 1) * HALF)
        k = kv_out[0, own, :]
        kt = jnp.transpose(k.astype(f32))
        vt = jnp.transpose(kv_out[1, own, :].astype(f32))
        r = lax.rsqrt(jnp.sum(kt * kt, axis=0, keepdims=True) + 1e-6)
        weight = jnp.exp(sums[j : j + 1, HALF - 1 :] - sums[j : j + 1]) * gates_out[2 + j : 3 + j]
        left = jnp.concatenate((kt * (weight * r * r), vt * (weight * r)), axis=0)
        high, low = split(left)
        grams.append(dot(high, k) + dot(low, k))
    first_out[...] = grams[0]
    later = sums[1:2, HALF - 1 :]
    local = jnp.exp(later) * grams[0] + grams[1]
    pay_out[...] = payload(local, jnp.broadcast_to(sums[0:1, HALF - 1 :] + later, (1, E)))


def row_body(pos, own, r1, r2, r3, pay_out, state_out, lead_out, place):
    mine = pos[2]
    place[mine] = own[...]
    for distance, received in ((1, r1), (2, r2), (3, r3)):
        place[lax.rem(mine + 4 - distance, 4)] = received[...]
    decays = [decay_row(place[m, 2 * E :, :]) for m in range(4)]
    zero = jnp.zeros((1, E), f32)
    total = before = jnp.zeros((2 * E, E), f32)
    lead = zero
    for m in range(4):
        block = place[m, : 2 * E, :].astype(f32)
        step = jnp.exp(decays[m])
        total = step * total + block
        earlier = m < mine
        before = jnp.where(earlier, step * before + block, before)
        lead = jnp.where(earlier, lead + decays[m], lead)
    pay_out[...] = payload(total, decays[0] + decays[1] + decays[2] + decays[3])
    state_out[...] = before
    lead_out[...] = jnp.broadcast_to(lead, (8, E))


def solve_body(
    pos, q, kv, gates, first, state, lead, t1, t2, t3, out, left, keys_t, mix, mix_v, xs, rs, ds, rr
):
    line = pos[1]
    start = jnp.zeros((2 * E, E), f32)
    passed = jnp.zeros((1, E), f32)
    for distance, received in ((1, t1), (2, t2), (3, t3)):
        block = received[: 2 * E, :].astype(f32)
        start = jnp.where(line >= distance, start + jnp.exp(passed) * block, start)
        passed = passed + decay_row(received[2 * E :, :])
    start = jnp.exp(lead[0:1, :]) * start + state[...]
    starts = [start, jnp.exp(gates[0:1, HALF - 1 :]) * start + first[...]]
    row, col = iotas((HALF, HALF))
    causal = row <= col
    leads = []
    for j in range(2):
        own = slice(j * HALF, (j + 1) * HALF)
        k = kv[0, own, :]
        kt = jnp.transpose(k.astype(f32))
        keys_t[j] = kt.astype(bf16)
        r = lax.rsqrt(jnp.sum(kt * kt, axis=0, keepdims=True) + 1e-6)
        c = gates[j : j + 1, :]
        strength = gates[2 + j : 3 + j, :]
        line_of, _ = iotas((E, HALF))
        columns = jnp.transpose(
            jnp.where(
                line_of == 0, c, jnp.where(line_of == 1, strength * r * r, strength * r)
            )
        )
        gap = jnp.where(causal, c - columns[:, 0:1], 0.0)
        decay = jnp.where(causal, jnp.exp(gap), 0.0)
        mix[j] = decay * columns[:, 1:2]
        mix_v[j] = decay * columns[:, 2:3]
        leads.append(jnp.exp(c))
        left[j, :HALF, :E] = k
        left[j, :HALF, E:] = k
        high, low = split(starts[j][:E])
        left[j, HALF : HALF + E, :E] = high
        left[j, HALF : HALF + E, E:] = high
        left[j, HALF + E :, :E] = low
        left[j, HALF + E :, E:] = jnp.zeros((E, E), bf16)
        qt = jnp.transpose(q[own, :].astype(f32))
        qn = qt * lax.rsqrt(jnp.sum(qt * qt, axis=0, keepdims=True) + 1e-6)
        xs[j] = jnp.zeros((E, HALF), f32)
        rs[j] = qn
        ds[j] = qn
        rr[j] = jnp.sum(qn * qn, axis=0, keepdims=True)

    def products(j, vector, weights, right):
        high, low = split(vector)
        y = dot(left[j], jnp.concatenate((high, low), axis=0))
        inside = two_part(right, weights * y[:HALF])
        return leads[j] * (y[HALF : HALF + E] + y[HALF + E :]) + inside

    def iteration(_, carry):
        for j in range(2):
            d = ds[j]
            image = products(j, d, mix[j], keys_t[j]) + RIDGE * d
            now = rr[j]
            alpha = now / jnp.maximum(jnp.sum(d * image, axis=0, keepdims=True), TINY)
            xs[j] = xs[j] + alpha * d
            r = rs[j] - alpha * image
            rs[j] = r
            new = jnp.sum(r * r, axis=0, keepdims=True)
            ds[j] = r + new / jnp.maximum(now, TINY) * d
            rr[j] = new
        return carry

    lax.fori_loop(0, CG_STEPS, iteration, 0)
    for j in range(2):
        own = slice(j * HALF, (j + 1) * HALF)
        high, low = split(starts[j][E:])
        left[j, HALF : HALF + E, :E] = high
        left[j, HALF : HALF + E, E:] = high
        left[j, HALF + E :, :E] = low
        vt = jnp.transpose(kv[1, own, :].astype(f32)).astype(bf16)
        out[:, own] = products(j, xs[j], mix_v[j], vt)


def attend_body(pos, q, kv, near, far, mesa, keep_out, send_out):
    core, chip = pos[0], pos[1] * 4 + pos[2]
    scale = E ** (-0.5)
    row, col = iotas((HALF, HALF))
    parts = [(far, 0, 2), (far, 1, 2), (near, 0, 1), (near, 1, 1), (kv, 0, 0), (kv, 1, 0)]

    def rows_of(b, which):
        source, half, _ = parts[b]
        return source[which, half * HALF : (half + 1) * HALF, :]

    values_t = [jnp.transpose(rows_of(b, 1).astype(f32)).astype(bf16) for b in range(6)]
    for j in range(2):
        own = slice(j * HALF, (j + 1) * HALF)
        qj = q[own, :]
        scores = []
        for b in range(j, j + 5):
            s = lax.dot_general(
                rows_of(b, 0), qj, (((1,), (1,)), ((), ())), preferred_element_type=f32
            )
            if b == j:
                s = jnp.where(row > col, s, LOW)
            if b == j + 4:
                s = jnp.where(row <= col, s, LOW)
            if parts[b][2]:
                s = jnp.where(chip >= parts[b][2], s, LOW)
            scores.append(s)
        largest = scores[0]
        for s in scores[1:]:
            largest = jnp.maximum(largest, s)
        largest = jnp.max(largest, axis=0, keepdims=True)
        total = jnp.zeros((1, HALF), f32)
        result = jnp.zeros((E, HALF), f32)
        for b, s in zip(range(j, j + 5), scores):
            expo = jnp.exp((s - largest) * scale)
            total = total + jnp.sum(expo, axis=0, keepdims=True)
            result = result + dot(values_t[b], expo.astype(bf16))
        both = jnp.transpose(result / total + mesa[:, own]).astype(bf16)

        @pl.when(core == j)
        def _():
            keep_out[...] = both

        @pl.when(core != j)
        def _():
            send_out[...] = both


def swapped(x):
    return lax.ppermute(x, "c", [(0, 1), (1, 0)])


def turned(x, axis, by):
    return lax.ppermute(x, axis, [(i, (i + by) % 4) for i in range(4)])


def on_device(queries, keys, values, log_forget, strength, out_weight):
    core, x, y = (lax.axis_index(a) for a in ("c", "x", "y"))
    pos = jnp.stack((core, x, y)).astype(jnp.int32)
    rows = jnp.stack((queries, keys, values))
    gates = jnp.stack((log_forget, strength), axis=1)
    front = core == 0
    keep = jnp.where(front, rows[:, :, 0], rows[:, :, 1])
    send = jnp.where(front, rows[:, :, 1], rows[:, :, 0])
    gate_keep = jnp.where(front, gates[0], gates[1])
    gate_send = jnp.where(front, gates[1], gates[0])
    q, kv, gates, local, first = call(
        gram_body,
        [
            ((CHIP, E), bf16),
            ((2, CHIP, E), bf16),
            ((8, HALF), f32),
            ((ROWS, E), bf16),
            ((2 * E, E), f32),
        ],
        [],
        1 << 26,
        pos,
        keep,
        swapped(send),
        gate_keep,
        swapped(gate_send),
    )
    near, far = (
        lax.ppermute(kv, XY, [(i, i + by) for i in range(16) if i + by < 16]) for by in (1, 2)
    )
    row_total, state, lead = call(
        row_body,
        [((ROWS, E), bf16), ((2 * E, E), f32), ((8, E), f32)],
        [((4, ROWS, E), bf16)],
        1 << 20,
        pos,
        local,
        *(turned(local, "y", by) for by in (1, 2, 3)),
    )
    (mesa,) = call(
        solve_body,
        [((E, CHIP), f32)],
        [
            ((2, CHIP, CHIP // 2), bf16),
            ((2, E, HALF), bf16),
            ((2, HALF, HALF), f32),
            ((2, HALF, HALF), f32),
            ((2, E, HALF), f32),
            ((2, E, HALF), f32),
            ((2, E, HALF), f32),
            ((2, 1, HALF), f32),
        ],
        1 << 30,
        pos,
        q,
        kv,
        gates,
        first,
        state,
        lead,
        *(turned(row_total, "x", by) for by in (1, 2, 3)),
    )
    kept, sent = call(
        attend_body, [((HALF, E), bf16)] * 2, [], 1 << 29, pos, q, kv, near, far, mesa
    )
    other = swapped(sent)
    flat = jnp.concatenate(
        (jnp.where(front, kept, other), jnp.where(front, other, kept)), axis=1
    )
    shares = jnp.dot(flat, out_weight, preferred_element_type=f32).astype(bf16)
    parts = lax.all_to_all(shares.reshape(8, 32, 2048), "z", 0, 0, tiled=True)
    return jnp.sum(parts.astype(f32), axis=0).astype(bf16)


def solution(mesh):
    grid = Mesh(mesh.devices.reshape(4, 4, 2, mesh.shape["head"]), ("x", "y", "c", "z"))
    in_specs = (
        P(SEQ, "z", None),
        P(SEQ, "z", None),
        P(SEQ, "z", None),
        P("z", SEQ),
        P("z", SEQ),
        P("z", None),
    )
    return jax.shard_map(
        on_device, mesh=grid, in_specs=in_specs, out_specs=P((*SEQ, "z"), None), check_vma=False
    )
```

time: 119 us -> 96.9 us (0.81); the launches traced: 119 us -> 95 us
  blocking collectives: 63.2 us -> 37.3 us
  matrix products: 20.9 us -> 0.44 us
  Pallas kernels: 0 us -> 15.9 us
  waiting for transfers between devices: 0.01 us -> 15.2 us
  other arithmetic: 10.7 us -> 3.69 us
  local copies, waits for them, and re-layouts: 9.07 us -> 5.42 us
  starting transfers between devices: 13.5 us -> 16.9 us
    all_gather x3 -> x0, blocking collectives: 29.3 us -> none  [collected_together(): both, at, found = (lax.all_gather(jnp.concatenate(lines), axis), 0, {})]
    dot_general x25 -> x1, matrix products: 18.9 us -> 0.44 us  [on_device(): shares = jnp.dot(flat, out_weight, preferred_element_type=f32).astype(bf16)]
    pallas_call x0 -> x4, Pallas kernels: none -> 15.9 us  [call(): pl.pallas_call(body, out_shape=[jax.ShapeDtypeStruct(shape, kind) for sha...]
    ppermute x4 -> x11, waiting for transfers between devices: 0.01 us -> 15.2 us  [the longest x6 13.6 us: turned(): return lax.ppermute(x, axis, [(i, (i + by) % 4) for i in range(4)])]
    all_to_all x1, blocking collectives: 33.9 us -> 37.3 us  [on_device(): parts = lax.all_to_all(shares.reshape(8, 32, 2048), 'z', 0, 0, tiled=True)]
    ppermute x4 -> x11, starting transfers between devices: 13.5 us -> 16.9 us  [the longest x6 8.72 us: turned(): return lax.ppermute(x, axis, [(i, (i + by) % 4) for i in range(4)])]
    select_n x0 -> x3, other arithmetic: none -> 2.17 us  [the longest x1 0.86 us: on_device(): jnp.where(front, kept, other)]
    add x8 -> x0, other arithmetic: 2.15 us -> none  [the longest x1 1.05 us: group_step(): solution = solution + alpha * direction]
  transfers between devices with their start and end apart: 4 -> 11, of which waited for: 0 -> 8; matrix products, arithmetic and copies ran while one was open for 25% -> 1% of each run, Pallas kernels for 0% -> 10%
where the time goes in v1:
time: 96.9 us; the launch traced here: 95 us
  blocking collectives  37.3 us (38%)
  starting transfers between devices  16.9 us (17%)
  Pallas kernels  15.9 us (16%)
  waiting for transfers between devices  15.2 us (16%)
  local copies, waits for them, and re-layouts  5.42 us (6%)
  other arithmetic  3.69 us (4%)
    all_to_all x1, blocking collectives, on_device(): parts = lax.all_to_all(shares.reshape(8, 32, 2048), 'z', 0, 0, tiled=True)  37.3 us
    pallas_call x4, Pallas kernels, call(): pl.pallas_call(body, out_shape=[jax.ShapeDtypeStruct(shape, kind) for sha...  15.9 us
    ppermute x6, waiting for transfers between devices, turned(): return lax.ppermute(x, axis, [(i, (i + by) % 4) for i in range(4)])  13.6 us
    ppermute x6, starting transfers between devices, turned(): return lax.ppermute(x, axis, [(i, (i + by) % 4) for i in range(4)])  8.72 us
    ppermute x2, starting transfers between devices, on_device(): lax.ppermute(kv, XY, [(i, i + by) for i in range(16) if i + by < 16])  7.68 us
    unnamed x27, local copies, waits for them, and re-layouts  4.4 us
  transfers between devices with their start and end apart: 11, of which 8 were waited for; matrix products, arithmetic and copies ran while one was open for 1% of the time, Pallas kernels for 10%

profile of v1, /device:TPU:2, one launch (start us, length us, event | category | flops | bytes accessed | tf_op | source)
XLA Modules:
  0.0 95.0 jit_solution(3863532048532955506)
XLA Ops:
  0.0 0.0 copy-start
  0.0 1.0 %copy.13 = bf16[256,2,128]{2,0,1:T(8,128)(2,1)S(1)} copy(bf16[256,2,128]{2,1,0:T(2,128)(2,1)} %param.6) | data formatting | bytes 262144 | tf_op args[0]
  1.0 0.0 copy-start.6
  1.0 0.0 copy-start.7
  1.0 1.0 %copy_bitcast_fusion = (bf16[1,256,2,128]{3,1,0,2:T(8,128)(2,1)S(1)}, bf16[1,256,2,128]{3,1,0,2:T(8,128)(2,1)S(1)}) fusion(bf16[256,2,128]{2,1,0:T(2,128)(2,1)} %param.8, bf16[256,2,128]{2,1,0:T(2,128)(2,1)} %param.7), kind=kLoop, calls=%fused_computation.7 | loop fusion | bytes 524288 | tf_op jit(solution)/shard_map/stack | solution.py:260
  2.1 0.7 select_bitcast_fusion
  2.8 0.0 collective-permute-start
  2.8 0.0 copy-done.6
  2.8 0.0 copy-done.7
  2.9 0.6 select_bitcast_fusion.2
  3.5 0.5 collective-permute-start.1
  4.0 0.7 pad_add_fusion.pos
  4.6 0.2 collective-permute-done.1.gate_recv
  4.8 0.0 copy-start.5
  4.8 0.0 collective-permute-done.recv
  4.8 0.0 copy-start.1
  4.8 0.6 copy-done.5
  5.4 0.1 copy-done.1
  5.5 2.4 %shard_map.64 = (bf16[512,128]{1,0:T(8,128)(2,1)}, bf16[2,512,128]{2,1,0:T(8,128)(2,1)}, f32[8,256]{1,0:T(8,128)}, bf16[272,128]{1,0:T(8,128)(2,1)}, f32[256,128]{1,0:T(8,128)}) custom-call(s32[3]{0:T(128)} %pad_add_fusion.pos, bf16[3,256,128]{2,1,0:T(8,128)(2,1)} %get-tuple-element.26.keep, bf16[3,256,128]{2,1,0:T(8,128)(2,1)} %copy-done.1, ...), custom_call_target="tpu_custom_call" | custom-call | flops 67108864 | bytes 1048576 | tf_op jit(solution)/shard_map/pallas_call | solution.py:29
  7.9 5.1 %collective-permute-start.3 = (bf16[2,512,128]{2,1,0:T(8,128)(2,1)}, bf16[2,512,128]{2,1,0:T(8,128)(2,1)S(1)}, u32[]{:S(2)}, u32[]{:S(2)}) collective-permute-start(bf16[2,512,128]{2,1,0:T(8,128)(2,1)} %get-tuple-element.16.kv), channel_id=1, source_target_pairs={{0,32},{16,48},{32,64},{48,80},{64,96},{80,112},{96,128},{112,144}... | collective-permute-start | bytes 786440 | tf_op jit(solution)/shard_map/ppermute | solution.py:285
  13.0 2.6 %collective-permute-start.2 = (bf16[2,512,128]{2,1,0:T(8,128)(2,1)}, bf16[2,512,128]{2,1,0:T(8,128)(2,1)S(1)}, u32[]{:S(2)}, u32[]{:S(2)}) collective-permute-start(bf16[2,512,128]{2,1,0:T(8,128)(2,1)} %get-tuple-element.16.kv), channel_id=1, source_target_pairs={{0,16},{16,32},{32,48},{48,64},{64,80},{80,96},{96,112},{112,128},... | collective-permute-start | bytes 786440 | tf_op jit(solution)/shard_map/ppermute | solution.py:285
  15.6 3.6 %collective-permute-start.6 = (bf16[272,128]{1,0:T(8,128)(2,1)}, bf16[272,128]{1,0:T(8,128)(2,1)S(1)}, u32[]{:S(2)}, u32[]{:S(2)}) collective-permute-start(bf16[272,128]{1,0:T(8,128)(2,1)} %get-tuple-element.19.own), channel_id=1, source_target_pairs={{0,48},{16,0},{32,16},{48,32},{1,49},{17,1},{33,17},{49,33},{2,50}... | collective-permute-start | bytes 208904 | tf_op jit(solution)/shard_map/ppermute | solution.py:254
  19.1 0.0 collective-permute-start.5
  19.2 1.0 %collective-permute-start.4 = (bf16[272,128]{1,0:T(8,128)(2,1)}, bf16[272,128]{1,0:T(8,128)(2,1)S(1)}, u32[]{:S(2)}, u32[]{:S(2)}) collective-permute-start(bf16[272,128]{1,0:T(8,128)(2,1)} %get-tuple-element.19.own), channel_id=1, source_target_pairs={{0,16},{16,32},{32,48},{48,0},{1,17},{17,33},{33,49},{49,1},{2,18}... | collective-permute-start | bytes 208904 | tf_op jit(solution)/shard_map/ppermute | solution.py:254
  20.1 2.4 %collective-permute-done.6.r3 = bf16[272,128]{1,0:T(8,128)(2,1)S(1)} collective-permute-done((bf16[272,128]{1,0:T(8,128)(2,1)}, bf16[272,128]{1,0:T(8,128)(2,1)S(1)}, u32[]{:S(2)}, u32[]{:S(2)}) %collective-permute-start.6) | collective-permute-done | bytes 69664 | tf_op jit(solution)/shard_map/ppermute | solution.py:254
  22.5 0.0 copy-start.2
  22.5 6.4 %collective-permute-done.5.r2 = bf16[272,128]{1,0:T(8,128)(2,1)S(1)} collective-permute-done((bf16[272,128]{1,0:T(8,128)(2,1)}, bf16[272,128]{1,0:T(8,128)(2,1)S(1)}, u32[]{:S(2)}, u32[]{:S(2)}) %collective-permute-start.5) | collective-permute-done | bytes 69664 | tf_op jit(solution)/shard_map/ppermute | solution.py:254
  28.9 0.0 copy-start.3
  28.9 1.4 %collective-permute-done.4.r1 = bf16[272,128]{1,0:T(8,128)(2,1)S(1)} collective-permute-done((bf16[272,128]{1,0:T(8,128)(2,1)}, bf16[272,128]{1,0:T(8,128)(2,1)S(1)}, u32[]{:S(2)}, u32[]{:S(2)}) %collective-permute-start.4) | collective-permute-done | bytes 69664 | tf_op jit(solution)/shard_map/ppermute | solution.py:254
  30.3 0.0 copy-done.2
  30.3 0.0 copy-done.3
  30.3 0.0 copy-start.4
  30.3 0.6 copy-done.4
  31.0 1.8 %shard_map.65 = (bf16[272,128]{1,0:T(8,128)(2,1)}, f32[256,128]{1,0:T(8,128)}, f32[8,128]{1,0:T(8,128)}) custom-call(s32[3]{0:T(128)} %pad_add_fusion.pos, bf16[272,128]{1,0:T(8,128)(2,1)} %get-tuple-element.19.own, bf16[272,128]{1,0:T(8,128)(2,1)} %copy-done.4, bf16[272,128]{1,0:T(8,128)(2,1)} %copy-done.3, bf16[272,128]{1,0:T(8,128)(2,1)} %copy-done.2), custom_call_target="tpu_custom_call" | custom-call | flops 1048576 | bytes 1048576 | tf_op jit(solution)/shard_map/pallas_call | solution.py:29
  32.8 0.0 collective-permute-start.9
  32.8 2.9 %collective-permute-start.8 = (bf16[272,128]{1,0:T(8,128)(2,1)}, bf16[272,128]{1,0:T(8,128)(2,1)S(1)}, u32[]{:S(2)}, u32[]{:S(2)}) collective-permute-start(bf16[272,128]{1,0:T(8,128)(2,1)} %get-tuple-element.22), channel_id=1, source_target_pairs={{0,128},{64,192},{128,0},{192,64},{1,129},{65,193},{129,1},{193,65... | collective-permute-start | bytes 208904 | tf_op jit(solution)/shard_map/ppermute | solution.py:254
  35.7 1.3 %collective-permute-start.7 = (bf16[272,128]{1,0:T(8,128)(2,1)}, bf16[272,128]{1,0:T(8,128)(2,1)S(1)}, u32[]{:S(2)}, u32[]{:S(2)}) collective-permute-start(bf16[272,128]{1,0:T(8,128)(2,1)} %get-tuple-element.22), channel_id=1, source_target_pairs={{0,64},{64,128},{128,192},{192,0},{1,65},{65,129},{129,193},{193,1... | collective-permute-start | bytes 208904 | tf_op jit(solution)/shard_map/ppermute | solution.py:254
  37.0 0.3 collective-permute-done.9.t3
  37.3 0.0 copy-start.10
  37.3 2.2 %collective-permute-done.8.t2 = bf16[272,128]{1,0:T(8,128)(2,1)S(1)} collective-permute-done((bf16[272,128]{1,0:T(8,128)(2,1)}, bf16[272,128]{1,0:T(8,128)(2,1)S(1)}, u32[]{:S(2)}, u32[]{:S(2)}) %collective-permute-start.8) | collective-permute-done | bytes 69664 | tf_op jit(solution)/shard_map/ppermute | solution.py:254
  39.5 0.0 copy-start.11
  39.5 0.9 collective-permute-done.7.t1
  40.4 0.0 copy-start.12
  40.4 0.0 copy-done.10
  40.4 0.0 copy-done.11
  40.4 0.6 copy-done.12
  41.0 7.9 %shard_map.66.mesa = f32[128,512]{1,0:T(8,128)} custom-call(s32[3]{0:T(128)} %pad_add_fusion.pos, bf16[512,128]{1,0:T(8,128)(2,1)} %get-tuple-element.15.q, bf16[2,512,128]{2,1,0:T(8,128)(2,1)} %get-tuple-element.16.kv, f32[8,256]{1,0:T(8,128)} %get-tuple-element.17.gates, f32[256,128]{1,0:T(8,128)} %get-tuple-element.18.first, ...), custom_call_target="tpu_custom_call" | custom-call | flops 1073741824 | bytes 1048576 | tf_op jit(solution)/shard_map/pallas_call | solution.py:29
  48.9 0.0 collective-permute-done.3.far
  48.9 0.0 copy-start.8
  48.9 0.0 collective-permute-done.2.near
  48.9 0.7 copy-done.8
  49.7 0.0 copy-start.9
  49.7 0.7 copy-done.9
  50.4 3.7 %shard_map.67 = (bf16[256,128]{1,0:T(8,128)(2,1)}, bf16[256,128]{1,0:T(8,128)(2,1)}) custom-call(s32[3]{0:T(128)} %pad_add_fusion.pos, bf16[512,128]{1,0:T(8,128)(2,1)} %get-tuple-element.15.q, bf16[2,512,128]{2,1,0:T(8,128)(2,1)} %get-tuple-element.16.kv, bf16[2,512,128]{2,1,0:T(8,128)(2,1)} %copy-done.9, bf16[2,512,128]{2,1,0:T(8,128)(2,1)} %copy-done.8, ...), custom_call_target="tpu_custom_call" | custom-call | flops 536870912 | bytes 1048576 | tf_op jit(solution)/shard_map/pallas_call | solution.py:29
  54.1 0.0 collective-permute-start.10
  54.1 1.5 %collective-permute-done.10 = bf16[256,128]{1,0:T(8,128)(2,1)S(1)} collective-permute-done((bf16[256,128]{1,0:T(8,128)(2,1)}, bf16[256,128]{1,0:T(8,128)(2,1)S(1)}, u32[]{:S(2)}, u32[]{:S(2)}) %collective-permute-start.10) | collective-permute-done | bytes 65568 | tf_op jit(solution)/shard_map/ppermute | solution.py:250
  55.5 0.9 broadcast_select_fusion.1
  56.4 0.0 copy-done
  56.4 0.4 convolution_convert_fusion
  56.8 37.3 %all_to_all.5 = bf16[8,32,2048]{2,1,0:T(8,128)(2,1)S(1)} all-to-all(bf16[8,32,2048]{2,1,0:T(8,128)(2,1)S(1)} %bitcast.20), channel_id=1, replica_groups=mesh['x'=4,'y'=4,'c'=2,'z'=8] {'z'}, dimensions={0} | all-to-all | bytes 2097152 | tf_op jit(solution)/shard_map/all_to_all | solution.py:327
  94.2 0.8 reduce_sum.12
  (3 shorter events, 0.1 us)
Async XLA Ops:
  0.0 56.4 %copy-start = (bf16[256,2048]{1,0:T(8,128)(2,1)S(1)}, bf16[256,2048]{1,0:T(8,128)(2,1)}, u32[]{:S(2)}) copy-start(bf16[256,2048]{1,0:T(8,128)(2,1)} %param.11) | copy-start | bytes 3145732
  1.0 1.8 %copy-start.6 = (f32[2,256]{1,0:T(2,128)S(1)}, f32[2,256]{1,0:T(2,128)}, u32[]{:S(2)}) copy-start(f32[2,256]{1,0:T(2,128)} %param.9) | copy-start | bytes 6148
  1.0 1.8 %copy-start.7 = (f32[2,256]{1,0:T(2,128)S(1)}, f32[2,256]{1,0:T(2,128)}, u32[]{:S(2)}) copy-start(f32[2,256]{1,0:T(2,128)} %param.10) | copy-start | bytes 6148
  2.8 1.9 %collective-permute-start = (bf16[3,256,128]{2,1,0:T(8,128)(2,1)S(1)}, bf16[3,256,128]{2,1,0:T(8,128)(2,1)S(1)}, u32[]{:S(2)}, u32[]{:S(2)}) collective-permute-start(bf16[3,256,128]{2,1,0:T(8,128)(2,1)S(1)} %get-tuple-element.25), channel_id=1, source_target_pairs={{0,8},{8,0},{1,9},{9,1},{2,10},{10,2},{3,11},{11,3},{4,12},{12,4},... | collective-permute-start | bytes 589832 | tf_op jit(solution)/shard_map/ppermute | solution.py:250
  3.5 1.3 %collective-permute-start.1 = (f32[2,256]{1,0:T(2,128)S(1)}, f32[2,256]{1,0:T(2,128)S(1)}, u32[]{:S(2)}, u32[]{:S(2)}) collective-permute-start(f32[2,256]{1,0:T(2,128)S(1)} %get-tuple-element.29), channel_id=1, source_target_pairs={{0,8},{8,0},{1,9},{9,1},{2,10},{10,2},{3,11},{11,3},{4,12},{12,4},... | collective-permute-start | bytes 6152 | tf_op jit(solution)/shard_map/ppermute | solution.py:250
  4.8 0.6 copy-start.5
  4.8 0.7 copy-start.1
  7.9 41.0 %collective-permute-start.3 = (bf16[2,512,128]{2,1,0:T(8,128)(2,1)}, bf16[2,512,128]{2,1,0:T(8,128)(2,1)S(1)}, u32[]{:S(2)}, u32[]{:S(2)}) collective-permute-start(bf16[2,512,128]{2,1,0:T(8,128)(2,1)} %get-tuple-element.16.kv), channel_id=1, source_target_pairs={{0,32},{16,48},{32,64},{48,80},{64,96},{80,112},{96,128},{112,144}... | collective-permute-start | bytes 786440 | tf_op jit(solution)/shard_map/ppermute | solution.py:285
  13.0 35.9 %collective-permute-start.2 = (bf16[2,512,128]{2,1,0:T(8,128)(2,1)}, bf16[2,512,128]{2,1,0:T(8,128)(2,1)S(1)}, u32[]{:S(2)}, u32[]{:S(2)}) collective-permute-start(bf16[2,512,128]{2,1,0:T(8,128)(2,1)} %get-tuple-element.16.kv), channel_id=1, source_target_pairs={{0,16},{16,32},{32,48},{48,64},{64,80},{80,96},{96,112},{112,128},... | collective-permute-start | bytes 786440 | tf_op jit(solution)/shard_map/ppermute | solution.py:285
  15.6 6.9 %collective-permute-start.6 = (bf16[272,128]{1,0:T(8,128)(2,1)}, bf16[272,128]{1,0:T(8,128)(2,1)S(1)}, u32[]{:S(2)}, u32[]{:S(2)}) collective-permute-start(bf16[272,128]{1,0:T(8,128)(2,1)} %get-tuple-element.19.own), channel_id=1, source_target_pairs={{0,48},{16,0},{32,16},{48,32},{1,49},{17,1},{33,17},{49,33},{2,50}... | collective-permute-start | bytes 208904 | tf_op jit(solution)/shard_map/ppermute | solution.py:254
  19.1 9.8 %collective-permute-start.5 = (bf16[272,128]{1,0:T(8,128)(2,1)}, bf16[272,128]{1,0:T(8,128)(2,1)S(1)}, u32[]{:S(2)}, u32[]{:S(2)}) collective-permute-start(bf16[272,128]{1,0:T(8,128)(2,1)} %get-tuple-element.19.own), channel_id=1, source_target_pairs={{0,32},{16,48},{32,0},{48,16},{1,33},{17,49},{33,1},{49,17},{2,34}... | collective-permute-start | bytes 208904 | tf_op jit(solution)/shard_map/ppermute | solution.py:254
  19.2 11.2 %collective-permute-start.4 = (bf16[272,128]{1,0:T(8,128)(2,1)}, bf16[272,128]{1,0:T(8,128)(2,1)S(1)}, u32[]{:S(2)}, u32[]{:S(2)}) collective-permute-start(bf16[272,128]{1,0:T(8,128)(2,1)} %get-tuple-element.19.own), channel_id=1, source_target_pairs={{0,16},{16,32},{32,48},{48,0},{1,17},{17,33},{33,49},{49,1},{2,18}... | collective-permute-start | bytes 208904 | tf_op jit(solution)/shard_map/ppermute | solution.py:254
  22.5 7.8 %copy-start.2 = (bf16[272,128]{1,0:T(8,128)(2,1)}, bf16[272,128]{1,0:T(8,128)(2,1)S(1)}, u32[]{:S(2)}) copy-start(bf16[272,128]{1,0:T(8,128)(2,1)S(1)} %collective-permute-done.6.r3) | copy-start | bytes 208900
  28.9 1.4 %copy-start.3 = (bf16[272,128]{1,0:T(8,128)(2,1)}, bf16[272,128]{1,0:T(8,128)(2,1)S(1)}, u32[]{:S(2)}) copy-start(bf16[272,128]{1,0:T(8,128)(2,1)S(1)} %collective-permute-done.5.r2) | copy-start | bytes 208900
  30.3 0.6 copy-start.4
  32.8 4.5 %collective-permute-start.9 = (bf16[272,128]{1,0:T(8,128)(2,1)}, bf16[272,128]{1,0:T(8,128)(2,1)S(1)}, u32[]{:S(2)}, u32[]{:S(2)}) collective-permute-start(bf16[272,128]{1,0:T(8,128)(2,1)} %get-tuple-element.22), channel_id=1, source_target_pairs={{0,192},{64,0},{128,64},{192,128},{1,193},{65,1},{129,65},{193,129... | collective-permute-start | bytes 208904 | tf_op jit(solution)/shard_map/ppermute | solution.py:254
  32.8 6.7 %collective-permute-start.8 = (bf16[272,128]{1,0:T(8,128)(2,1)}, bf16[272,128]{1,0:T(8,128)(2,1)S(1)}, u32[]{:S(2)}, u32[]{:S(2)}) collective-permute-start(bf16[272,128]{1,0:T(8,128)(2,1)} %get-tuple-element.22), channel_id=1, source_target_pairs={{0,128},{64,192},{128,0},{192,64},{1,129},{65,193},{129,1},{193,65... | collective-permute-start | bytes 208904 | tf_op jit(solution)/shard_map/ppermute | solution.py:254
  35.7 4.6 %collective-permute-start.7 = (bf16[272,128]{1,0:T(8,128)(2,1)}, bf16[272,128]{1,0:T(8,128)(2,1)S(1)}, u32[]{:S(2)}, u32[]{:S(2)}) collective-permute-start(bf16[272,128]{1,0:T(8,128)(2,1)} %get-tuple-element.22), channel_id=1, source_target_pairs={{0,64},{64,128},{128,192},{192,0},{1,65},{65,129},{129,193},{193,1... | collective-permute-start | bytes 208904 | tf_op jit(solution)/shard_map/ppermute | solution.py:254
  37.3 3.1 %copy-start.10 = (bf16[272,128]{1,0:T(8,128)(2,1)}, bf16[272,128]{1,0:T(8,128)(2,1)S(1)}, u32[]{:S(2)}) copy-start(bf16[272,128]{1,0:T(8,128)(2,1)S(1)} %collective-permute-done.9.t3) | copy-start | bytes 208900
  39.5 0.9 copy-start.11
  40.4 0.6 copy-start.12
  48.9 0.7 copy-start.8
  49.7 0.7 copy-start.9
  54.1 1.5 %collective-permute-start.10 = (bf16[256,128]{1,0:T(8,128)(2,1)}, bf16[256,128]{1,0:T(8,128)(2,1)S(1)}, u32[]{:S(2)}, u32[]{:S(2)}) collective-permute-start(bf16[256,128]{1,0:T(8,128)(2,1)} %get-tuple-element.24), channel_id=1, source_target_pairs={{0,8},{8,0},{1,9},{9,1},{2,10},{10,2},{3,11},{11,3},{4,12},{12,4},... | collective-permute-start | bytes 196616 | tf_op jit(solution)/shard_map/ppermute | solution.py:250

commit v2 on v1

--- a/solution.py
+++ b/solution.py
@@ -6,7 +6,6 @@
 from jax.sharding import Mesh
 from jax.sharding import PartitionSpec as P
 
-WINDOW = 1024
 CG_STEPS = 6
 RIDGE = 0.25
 TINY = 1e-30
@@ -15,6 +14,8 @@
 E = 128
 CHIP = 2 * HALF
 ROWS = 2 * E + 16
+SLOT = 32
+GRANT = 16 << 20
 SEQ = ("x", "y", "c")
 XY = ("x", "y")
 f32 = jnp.float32
@@ -32,6 +33,7 @@
         in_specs=[spec(pltpu.SMEM)] + [spec()] * (len(args) - 1),
         out_specs=[spec()] * len(outs),
         scratch_shapes=[pltpu.VMEM(shape, kind) for shape, kind in scratch],
+        compiler_params=pltpu.CompilerParams(vmem_limit_bytes=GRANT),
         cost_estimate=pl.CostEstimate(flops=flops, bytes_accessed=1 << 20, transcendentals=0),
     )(*args)
 
@@ -199,7 +201,7 @@
         out[:, own] = products(j, xs[j], mix_v[j], vt)
 
 
-def attend_body(pos, q, kv, near, far, mesa, keep_out, send_out):
+def attend_body(pos, q, kv, near, far, mesa, keep_out, c_out, z_out, cz_out, place):
     core, chip = pos[0], pos[1] * 4 + pos[2]
     scale = E ** (-0.5)
     row, col = iotas((HALF, HALF))
@@ -236,14 +238,36 @@
             total = total + jnp.sum(expo, axis=0, keepdims=True)
             result = result + dot(values_t[b], expo.astype(bf16))
         both = jnp.transpose(result / total + mesa[:, own]).astype(bf16)
-
-        @pl.when(core == j)
-        def _():
-            keep_out[...] = both
-
-        @pl.when(core != j)
-        def _():
-            send_out[...] = both
+        for slot in range(HALF // SLOT):
+            at = slot // 2 * SLOT
+            place[2 * j + slot % 2, at : at + SLOT, :] = both[slot * SLOT : (slot + 1) * SLOT]
+    side = lax.rem(pos[3], 2)
+    keep_out[...] = place[2 * core + side]
+    c_out[...] = place[2 * (1 - core) + side]
+    z_out[...] = place[2 * core + 1 - side]
+    cz_out[...] = place[2 * (1 - core) + 1 - side]
+
+
+def project_body(pos, keep, from_c, from_z, from_cz, own_weight, pair_weight, mine, s1, s2, s3, wide):
+    core, mine_at = pos[0], lax.div(pos[3], 2)
+    for piece, at in (
+        (keep, core),
+        (from_c, 1 - core),
+        (from_z, 2 + core),
+        (from_cz, 3 - core),
+    ):
+        wide[:, pl.ds(pl.multiple_of(at * E, E), E)] = piece[...]
+    rows = jnp.concatenate(
+        [
+            wide[pl.ds(pl.multiple_of(lax.rem(mine_at + d, 4) * SLOT, SLOT), SLOT), :]
+            for d in range(4)
+        ],
+        axis=0,
+    )
+    y = dot(rows[:, : 2 * E], own_weight[...]) + dot(rows[:, 2 * E :], pair_weight[...])
+    mine[...] = y[:SLOT]
+    for d, out in ((1, s1), (2, s2), (3, s3)):
+        out[...] = y[d * SLOT : (d + 1) * SLOT].astype(bf16)
 
 
 def swapped(x):
@@ -254,9 +278,14 @@
     return lax.ppermute(x, axis, [(i, (i + by) % 4) for i in range(4)])
 
 
+def across(x, dc, dz):
+    pairs = [(c * 8 + z, (c ^ dc) * 8 + (z ^ dz)) for c in range(2) for z in range(8)]
+    return lax.ppermute(x, ("c", "z"), pairs)
+
+
 def on_device(queries, keys, values, log_forget, strength, out_weight):
     core, x, y = (lax.axis_index(a) for a in ("c", "x", "y"))
-    pos = jnp.stack((core, x, y)).astype(jnp.int32)
+    pos = jnp.stack((core, x, y, lax.axis_index("z"))).astype(jnp.int32)
     rows = jnp.stack((queries, keys, values))
     gates = jnp.stack((log_forget, strength), axis=1)
     front = core == 0
@@ -281,9 +310,8 @@
         gate_keep,
         swapped(gate_send),
     )
-    near, far = (
-        lax.ppermute(kv, XY, [(i, i + by) for i in range(16) if i + by < 16]) for by in (1, 2)
-    )
+    around_y = [turned(local, "y", by) for by in (1, 2, 3)]
+    pair_weight = across(out_weight, 0, 1)
     row_total, state, lead = call(
         row_body,
         [((ROWS, E), bf16), ((2 * E, E), f32), ((8, E), f32)],
@@ -291,8 +319,15 @@
         1 << 20,
         pos,
         local,
-        *(turned(local, "y", by) for by in (1, 2, 3)),
-    )
+        *around_y,
+    )
+    around_x = [turned(row_total, "x", by) for by in (1, 2, 3)]
+    halo, _ = lax.optimization_barrier((kv, row_total))
+    halos = []
+    for by in (1, 2):
+        halos.append(
+            lax.ppermute(halo, XY, [(i, i + by) for i in range(16) if i + by < 16])
+        )
     (mesa,) = call(
         solve_body,
         [((E, CHIP), f32)],
@@ -314,18 +349,37 @@
         first,
         state,
         lead,
-        *(turned(row_total, "x", by) for by in (1, 2, 3)),
-    )
-    kept, sent = call(
-        attend_body, [((HALF, E), bf16)] * 2, [], 1 << 29, pos, q, kv, near, far, mesa
-    )
-    other = swapped(sent)
-    flat = jnp.concatenate(
-        (jnp.where(front, kept, other), jnp.where(front, other, kept)), axis=1
-    )
-    shares = jnp.dot(flat, out_weight, preferred_element_type=f32).astype(bf16)
-    parts = lax.all_to_all(shares.reshape(8, 32, 2048), "z", 0, 0, tiled=True)
-    return jnp.sum(parts.astype(f32), axis=0).astype(bf16)
+        *around_x,
+    )
+    kept, to_c, to_z, to_cz = call(
+        attend_body,
+        [((HALF // 2, E), bf16)] * 4,
+        [((4, HALF // 2, E), bf16)],
+        1 << 29,
+        pos,
+        q,
+        kv,
+        *halos,
+        mesa,
+    )
+    mine, *sent = call(
+        project_body,
+        [((SLOT, 2048), f32)] + [((SLOT, 2048), bf16)] * 3,
+        [((HALF // 2, 4 * E), bf16)],
+        1 << 28,
+        pos,
+        kept,
+        across(to_c, 1, 0),
+        across(to_z, 0, 1),
+        across(to_cz, 1, 1),
+        out_weight,
+        pair_weight,
+    )
+    total = mine
+    for by, share in zip((2, 4, 6), sent):
+        got = lax.ppermute(share, "z", [(i, (i + by) % 8) for i in range(8)])
+        total = total + got.astype(f32)
+    return total.astype(bf16)
 
 
 def solution(mesh):
@@ -338,6 +392,7 @@
         P("z", SEQ),
         P("z", None),
     )
+
     return jax.shard_map(
         on_device, mesh=grid, in_specs=in_specs, out_specs=P((*SEQ, "z"), None), check_vma=False
     )

time: 96.9 us -> 72.5 us (0.75)
  the two profiles are of different devices: /device:TPU:2 before, /device:TPU:25 now
where the time goes in v2:
time: 72.5 us; the launch traced here: 72.4 us
  starting transfers between devices  33.3 us (46%)
  waiting for transfers between devices  25.3 us (35%)
  Pallas kernels  11.7 us (16%)
  local copies, waits for them, and re-layouts  1.05 us (1%)
  other arithmetic  0.88 us (1%)
    ppermute x6, waiting for transfers between devices, turned(): return lax.ppermute(x, axis, [(i, (i + by) % 4) for i in range(4)])  11.9 us
    pallas_call x5, Pallas kernels, call(): pl.pallas_call(body, out_shape=[jax.ShapeDtypeStruct(shape, kind) for sha...  11.7 us
    ppermute x3, waiting for transfers between devices, on_device(): got = lax.ppermute(share, 'z', [(i, (i + by) % 8) for i in range(8)])  10.5 us
    ppermute x3, starting transfers between devices, on_device(): got = lax.ppermute(share, 'z', [(i, (i + by) % 8) for i in range(8)])  9.95 us
    ppermute x2, starting transfers between devices, on_device(): lax.ppermute(halo, XY, [(i, i + by) for i in range(16) if i + by < 16])  8.28 us
    ppermute x6, starting transfers between devices, turned(): return lax.ppermute(x, axis, [(i, (i + by) % 4) for i in range(4)])  7.38 us
    ppermute x4, starting transfers between devices, across(): return lax.ppermute(x, ('c', 'z'), pairs)  6.02 us
    ppermute x4, waiting for transfers between devices, across(): return lax.ppermute(x, ('c', 'z'), pairs)  2.09 us
  transfers between devices with their start and end apart: 17, of which 10 were waited for; matrix products, arithmetic and copies ran while one was open for 2% of the time, Pallas kernels for 15%

profile of v2, /device:TPU:25, one launch (start us, length us, event | category | flops | bytes accessed | tf_op | source)
XLA Modules:
  0.0 72.4 jit_solution(1373014290553166662)
XLA Ops:
  0.0 0.0 copy-start.1
  0.0 1.6 %collective-permute-start.13 = (bf16[256,2048]{1,0:T(8,128)(2,1)}, bf16[256,2048]{1,0:T(8,128)(2,1)S(1)}, u32[]{:S(2)}, u32[]{:S(2)}) collective-permute-start(bf16[256,2048]{1,0:T(8,128)(2,1)} %own_weight.1), channel_id=1, source_target_pairs={{0,1},{1,0},{2,3},{3,2},{4,5},{5,4},{6,7},{7,6},{8,9},{9,8},{10,11... | collective-permute-start | bytes 3145736 | tf_op jit(solution)/shard_map/ppermute | solution.py:283
  1.6 1.0 %copy_bitcast_fusion = (bf16[1,256,2,128]{3,1,0,2:T(8,128)(2,1)S(1)}, bf16[1,256,2,128]{3,1,0,2:T(8,128)(2,1)S(1)}) fusion(bf16[256,2,128]{2,1,0:T(2,128)(2,1)} %param.8, bf16[256,2,128]{2,1,0:T(2,128)(2,1)} %param.7), kind=kLoop, calls=%fused_computation.4 | loop fusion | bytes 524288 | tf_op jit(solution)/shard_map/stack | solution.py:289
  2.7 0.0 copy-done.1
  2.7 0.0 copy-start.2
  2.8 0.0 copy-start.3
  2.8 1.0 %collective-permute-start = (bf16[3,256,128]{2,1,0:T(8,128)(2,1)S(1)}, bf16[3,256,128]{2,1,0:T(8,128)(2,1)S(1)}, u32[]{:S(2)}, u32[]{:S(2)}) collective-permute-start(bf16[3,256,128]{2,1,0:T(8,128)(2,1)S(1)} %get-tuple-element.39), channel_id=1, source_target_pairs={{0,8},{8,0},{1,9},{9,1},{2,10},{10,2},{3,11},{11,3},{4,12},{12,4},... | collective-permute-start | bytes 589832 | tf_op jit(solution)/shard_map/ppermute | solution.py:274
  3.9 0.0 copy-done.2
  3.9 0.0 copy-done.3
  3.9 0.7 collective-permute-start.1
  4.5 0.1 pad_add_fusion.pos
  4.6 0.7 %collective-permute-done.1.gate_recv = f32[2,256]{1,0:T(2,128)S(1)} collective-permute-done((f32[2,256]{1,0:T(2,128)S(1)}, f32[2,256]{1,0:T(2,128)S(1)}, u32[]{:S(2)}, u32[]{:S(2)}) %collective-permute-start.1) | collective-permute-done | bytes 2080 | tf_op jit(solution)/shard_map/ppermute | solution.py:274
  5.4 0.0 collective-permute-done.recv
  5.4 1.3 %shard_map.64 = (bf16[512,128]{1,0:T(8,128)(2,1)S(1)}, bf16[2,512,128]{2,1,0:T(8,128)(2,1)S(1)}, f32[8,256]{1,0:T(8,128)S(1)}, bf16[272,128]{1,0:T(8,128)(2,1)S(1)}, f32[256,128]{1,0:T(8,128)S(1)}) custom-call(s32[4]{0:T(128)S(1)} %pad_add_fusion.pos, bf16[3,256,128]{2,1,0:T(8,128)(2,1)S(1)} %get-tuple-element.40.keep, ...), custom_call_target="tpu_custom_call" | custom-call | flops 67108864 | bytes 1048576 | tf_op jit(solution)/shard_map/pallas_call | solution.py:30
  6.6 0.5 collective-permute-start.4
  7.2 0.7 collective-permute-start.3
  7.8 1.9 %collective-permute-start.2 = (bf16[272,128]{1,0:T(8,128)(2,1)S(1)}, bf16[272,128]{1,0:T(8,128)(2,1)S(1)}, u32[]{:S(2)}, u32[]{:S(2)}) collective-permute-start(bf16[272,128]{1,0:T(8,128)(2,1)S(1)} %get-tuple-element.24.own), channel_id=1, source_target_pairs={{0,16},{16,32},{32,48},{48,0},{1,17},{17,33},{33,49},{49,1},{2,18}... | collective-permute-start | bytes 208904 | tf_op jit(solution)/shard_map/ppermute | solution.py:278
  9.7 1.3 %collective-permute-done.4.r3 = bf16[272,128]{1,0:T(8,128)(2,1)S(1)} collective-permute-done((bf16[272,128]{1,0:T(8,128)(2,1)S(1)}, bf16[272,128]{1,0:T(8,128)(2,1)S(1)}, u32[]{:S(2)}, u32[]{:S(2)}) %collective-permute-start.4) | collective-permute-done | bytes 69664 | tf_op jit(solution)/shard_map/ppermute | solution.py:278
  11.1 0.8 %collective-permute-done.3.r2 = bf16[272,128]{1,0:T(8,128)(2,1)S(1)} collective-permute-done((bf16[272,128]{1,0:T(8,128)(2,1)S(1)}, bf16[272,128]{1,0:T(8,128)(2,1)S(1)}, u32[]{:S(2)}, u32[]{:S(2)}) %collective-permute-start.3) | collective-permute-done | bytes 69664 | tf_op jit(solution)/shard_map/ppermute | solution.py:278
  11.9 1.2 %collective-permute-done.2.r1 = bf16[272,128]{1,0:T(8,128)(2,1)S(1)} collective-permute-done((bf16[272,128]{1,0:T(8,128)(2,1)S(1)}, bf16[272,128]{1,0:T(8,128)(2,1)S(1)}, u32[]{:S(2)}, u32[]{:S(2)}) %collective-permute-start.2) | collective-permute-done | bytes 69664 | tf_op jit(solution)/shard_map/ppermute | solution.py:278
  13.1 0.7 shard_map.65
  13.8 3.8 %collective-permute-start.6 = (bf16[2,512,128]{2,1,0:T(8,128)(2,1)S(1)}, bf16[2,512,128]{2,1,0:T(8,128)(2,1)S(1)}, u32[]{:S(2)}, u32[]{:S(2)}) collective-permute-start(bf16[2,512,128]{2,1,0:T(8,128)(2,1)S(1)} %get-tuple-element.26.kv), channel_id=1, source_target_pairs={{0,32},{16,48},{32,64},{48,80},{64,96},{80,112},{96,128},{112,144}... | collective-permute-start | bytes 786440 | tf_op jit(solution)/shard_map/ppermute | solution.py:329
  17.6 4.5 %collective-permute-start.5 = (bf16[2,512,128]{2,1,0:T(8,128)(2,1)S(1)}, bf16[2,512,128]{2,1,0:T(8,128)(2,1)S(1)}, u32[]{:S(2)}, u32[]{:S(2)}) collective-permute-start(bf16[2,512,128]{2,1,0:T(8,128)(2,1)S(1)} %get-tuple-element.26.kv), channel_id=1, source_target_pairs={{0,16},{16,32},{32,48},{48,64},{64,80},{80,96},{96,112},{112,128},... | collective-permute-start | bytes 786440 | tf_op jit(solution)/shard_map/ppermute | solution.py:329
  22.1 0.1 collective-permute-start.9
  22.2 3.0 %collective-permute-start.8 = (bf16[272,128]{1,0:T(8,128)(2,1)S(1)}, bf16[272,128]{1,0:T(8,128)(2,1)S(1)}, u32[]{:S(2)}, u32[]{:S(2)}) collective-permute-start(bf16[272,128]{1,0:T(8,128)(2,1)S(1)} %get-tuple-element.25), channel_id=1, source_target_pairs={{0,128},{64,192},{128,0},{192,64},{1,129},{65,193},{129,1},{193,65... | collective-permute-start | bytes 208904 | tf_op jit(solution)/shard_map/ppermute | solution.py:278
  25.2 0.5 collective-permute-done.9.t3
  25.6 1.2 %collective-permute-start.7 = (bf16[272,128]{1,0:T(8,128)(2,1)S(1)}, bf16[272,128]{1,0:T(8,128)(2,1)S(1)}, u32[]{:S(2)}, u32[]{:S(2)}) collective-permute-start(bf16[272,128]{1,0:T(8,128)(2,1)S(1)} %get-tuple-element.25), channel_id=1, source_target_pairs={{0,64},{64,128},{128,192},{192,0},{1,65},{65,129},{129,193},{193,1... | collective-permute-start | bytes 208904 | tf_op jit(solution)/shard_map/ppermute | solution.py:278
  26.9 8.1 %collective-permute-done.8.t2 = bf16[272,128]{1,0:T(8,128)(2,1)S(1)} collective-permute-done((bf16[272,128]{1,0:T(8,128)(2,1)S(1)}, bf16[272,128]{1,0:T(8,128)(2,1)S(1)}, u32[]{:S(2)}, u32[]{:S(2)}) %collective-permute-start.8) | collective-permute-done | bytes 69664 | tf_op jit(solution)/shard_map/ppermute | solution.py:278
  35.0 0.0 collective-permute-done.7.t1
  35.0 6.6 %shard_map.66.mesa = f32[128,512]{1,0:T(8,128)S(1)} custom-call(s32[4]{0:T(128)S(1)} %pad_add_fusion.pos, bf16[512,128]{1,0:T(8,128)(2,1)S(1)} %get-tuple-element.22.q, bf16[2,512,128]{2,1,0:T(8,128)(2,1)S(1)} %get-tuple-element.26.kv, f32[8,256]{1,0:T(8,128)S(1)} %get-tuple-element.27.gates, f32[256,128]{1,0:T(8,128)S(1)} %get-tuple-element.28.first, ...), custom_call_target="tpu_custom_call" | custom-call | flops 1073741824 | bytes 1048576 | tf_op jit(solution)/shard_map/pallas_call | solution.py:30
  41.5 0.0 copy-start
  41.5 0.0 collective-permute-done.6.far
  41.6 0.0 collective-permute-done.5.near
  41.6 2.1 %shard_map.67 = (bf16[128,128]{1,0:T(8,128)(2,1)S(1)}, bf16[128,128]{1,0:T(8,128)(2,1)S(1)}, bf16[128,128]{1,0:T(8,128)(2,1)S(1)}, bf16[128,128]{1,0:T(8,128)(2,1)S(1)}) custom-call(s32[4]{0:T(128)S(1)} %pad_add_fusion.pos, bf16[512,128]{1,0:T(8,128)(2,1)S(1)} %get-tuple-element.22.q, bf16[2,512,128]{2,1,0:T(8,128)(2,1)S(1)} %get-tuple-element.26.kv, ...), custom_call_target="tpu_custom_call" | custom-call | flops 536870912 | bytes 1048576 | tf_op jit(solution)/shard_map/pallas_call | solution.py:30
  43.7 2.6 %collective-permute-start.10 = (bf16[128,128]{1,0:T(8,128)(2,1)S(1)}, bf16[128,128]{1,0:T(8,128)(2,1)S(1)}, u32[]{:S(2)}, u32[]{:S(2)}) collective-permute-start(bf16[128,128]{1,0:T(8,128)(2,1)S(1)} %get-tuple-element.32), channel_id=1, source_target_pairs={{0,8},{1,9},{2,10},{3,11},{4,12},{5,13},{6,14},{7,15},{8,0},{9,1},... | collective-permute-start | bytes 98312 | tf_op jit(solution)/shard_map/ppermute | solution.py:283
  46.3 0.0 collective-permute-start.11
  46.3 1.7 %collective-permute-start.12 = (bf16[128,128]{1,0:T(8,128)(2,1)S(1)}, bf16[128,128]{1,0:T(8,128)(2,1)S(1)}, u32[]{:S(2)}, u32[]{:S(2)}) collective-permute-start(bf16[128,128]{1,0:T(8,128)(2,1)S(1)} %get-tuple-element.34), channel_id=1, source_target_pairs={{0,9},{1,8},{2,11},{3,10},{4,13},{5,12},{6,15},{7,14},{8,1},{9,0},... | collective-permute-start | bytes 98312 | tf_op jit(solution)/shard_map/ppermute | solution.py:283
  48.1 0.0 collective-permute-done.10.from_c
  48.1 1.0 %collective-permute-done.11.from_z = bf16[128,128]{1,0:T(8,128)(2,1)S(1)} collective-permute-done((bf16[128,128]{1,0:T(8,128)(2,1)S(1)}, bf16[128,128]{1,0:T(8,128)(2,1)S(1)}, u32[]{:S(2)}, u32[]{:S(2)}) %collective-permute-start.11) | collective-permute-done | bytes 32800 | tf_op jit(solution)/shard_map/ppermute | solution.py:283
  49.1 1.1 %collective-permute-done.12.from_cz = bf16[128,128]{1,0:T(8,128)(2,1)S(1)} collective-permute-done((bf16[128,128]{1,0:T(8,128)(2,1)S(1)}, bf16[128,128]{1,0:T(8,128)(2,1)S(1)}, u32[]{:S(2)}, u32[]{:S(2)}) %collective-permute-start.12) | collective-permute-done | bytes 32800 | tf_op jit(solution)/shard_map/ppermute | solution.py:283
  50.2 0.0 collective-permute-done.13.pair_weight
  50.2 0.0 copy-done
  50.2 1.0 %shard_map.68 = (f32[32,2048]{1,0:T(8,128)S(1)}, bf16[32,2048]{1,0:T(8,128)(2,1)S(1)}, bf16[32,2048]{1,0:T(8,128)(2,1)S(1)}, bf16[32,2048]{1,0:T(8,128)(2,1)S(1)}) custom-call(s32[4]{0:T(128)S(1)} %pad_add_fusion.pos, bf16[128,128]{1,0:T(8,128)(2,1)S(1)} %get-tuple-element.31.keep, bf16[128,128]{1,0:T(8,128)(2,1)S(1)} %collective-permute-done.10.from_c, ...), custom_call_target="tpu_custom_call" | custom-call | flops 268435456 | bytes 1048576 | tf_op jit(solution)/shard_map/pallas_call | solution.py:30
  51.2 3.1 %collective-permute-start.14 = (bf16[32,2048]{1,0:T(8,128)(2,1)S(1)}, bf16[32,2048]{1,0:T(8,128)(2,1)S(1)}, u32[]{:S(2)}, u32[]{:S(2)}) collective-permute-start(bf16[32,2048]{1,0:T(8,128)(2,1)S(1)} %get-tuple-element.36), channel_id=1, source_target_pairs={{0,2},{1,3},{2,4},{3,5},{4,6},{5,7},{6,0},{7,1},{8,10},{9,11},{10,... | collective-permute-start | bytes 393224 | tf_op jit(solution)/shard_map/ppermute | solution.py:380
  54.2 4.5 %collective-permute-start.15 = (bf16[32,2048]{1,0:T(8,128)(2,1)S(1)}, bf16[32,2048]{1,0:T(8,128)(2,1)S(1)}, u32[]{:S(2)}, u32[]{:S(2)}) collective-permute-start(bf16[32,2048]{1,0:T(8,128)(2,1)S(1)} %get-tuple-element.37), channel_id=1, source_target_pairs={{0,4},{1,5},{2,6},{3,7},{4,0},{5,1},{6,2},{7,3},{8,12},{9,13},{10,... | collective-permute-start | bytes 393224 | tf_op jit(solution)/shard_map/ppermute | solution.py:380
  58.7 2.4 %collective-permute-start.16 = (bf16[32,2048]{1,0:T(8,128)(2,1)S(1)}, bf16[32,2048]{1,0:T(8,128)(2,1)S(1)}, u32[]{:S(2)}, u32[]{:S(2)}) collective-permute-start(bf16[32,2048]{1,0:T(8,128)(2,1)S(1)} %get-tuple-element.38), channel_id=1, source_target_pairs={{0,6},{1,7},{2,0},{3,1},{4,2},{5,3},{6,4},{7,5},{8,14},{9,15},{10,... | collective-permute-start | bytes 393224 | tf_op jit(solution)/shard_map/ppermute | solution.py:380
  61.1 0.0 collective-permute-done.14
  61.1 6.5 %collective-permute-done.15 = bf16[32,2048]{1,0:T(8,128)(2,1)S(1)} collective-permute-done((bf16[32,2048]{1,0:T(8,128)(2,1)S(1)}, bf16[32,2048]{1,0:T(8,128)(2,1)S(1)}, u32[]{:S(2)}, u32[]{:S(2)}) %collective-permute-start.15) | collective-permute-done | bytes 131104 | tf_op jit(solution)/shard_map/ppermute | solution.py:380
  67.6 4.1 %collective-permute-done.16 = bf16[32,2048]{1,0:T(8,128)(2,1)S(1)} collective-permute-done((bf16[32,2048]{1,0:T(8,128)(2,1)S(1)}, bf16[32,2048]{1,0:T(8,128)(2,1)S(1)}, u32[]{:S(2)}, u32[]{:S(2)}) %collective-permute-start.16) | collective-permute-done | bytes 131104 | tf_op jit(solution)/shard_map/ppermute | solution.py:380
  71.7 0.7 add_convert_fusion
  (6 shorter events, 0.1 us)
Async XLA Ops:
  0.0 2.7 %copy-start.1 = (bf16[256,2,128]{2,1,0:T(2,128)(2,1)S(1)}, bf16[256,2,128]{2,1,0:T(2,128)(2,1)}, u32[]{:S(2)}) copy-start(bf16[256,2,128]{2,1,0:T(2,128)(2,1)} %param.6) | copy-start | bytes 393220
  0.0 50.2 %collective-permute-start.13 = (bf16[256,2048]{1,0:T(8,128)(2,1)}, bf16[256,2048]{1,0:T(8,128)(2,1)S(1)}, u32[]{:S(2)}, u32[]{:S(2)}) collective-permute-start(bf16[256,2048]{1,0:T(8,128)(2,1)} %own_weight.1), channel_id=1, source_target_pairs={{0,1},{1,0},{2,3},{3,2},{4,5},{5,4},{6,7},{7,6},{8,9},{9,8},{10,11... | collective-permute-start | bytes 3145736 | tf_op jit(solution)/shard_map/ppermute | solution.py:283
  2.7 1.1 %copy-start.2 = (f32[2,256]{1,0:T(2,128)S(1)}, f32[2,256]{1,0:T(2,128)}, u32[]{:S(2)}) copy-start(f32[2,256]{1,0:T(2,128)} %param.9) | copy-start | bytes 6148
  2.8 1.1 %copy-start.3 = (f32[2,256]{1,0:T(2,128)S(1)}, f32[2,256]{1,0:T(2,128)}, u32[]{:S(2)}) copy-start(f32[2,256]{1,0:T(2,128)} %param.10) | copy-start | bytes 6148
  2.8 2.6 %collective-permute-start = (bf16[3,256,128]{2,1,0:T(8,128)(2,1)S(1)}, bf16[3,256,128]{2,1,0:T(8,128)(2,1)S(1)}, u32[]{:S(2)}, u32[]{:S(2)}) collective-permute-start(bf16[3,256,128]{2,1,0:T(8,128)(2,1)S(1)} %get-tuple-element.39), channel_id=1, source_target_pairs={{0,8},{8,0},{1,9},{9,1},{2,10},{10,2},{3,11},{11,3},{4,12},{12,4},... | collective-permute-start | bytes 589832 | tf_op jit(solution)/shard_map/ppermute | solution.py:274
  3.9 1.5 %collective-permute-start.1 = (f32[2,256]{1,0:T(2,128)S(1)}, f32[2,256]{1,0:T(2,128)S(1)}, u32[]{:S(2)}, u32[]{:S(2)}) collective-permute-start(f32[2,256]{1,0:T(2,128)S(1)} %get-tuple-element.41), channel_id=1, source_target_pairs={{0,8},{8,0},{1,9},{9,1},{2,10},{10,2},{3,11},{11,3},{4,12},{12,4},... | collective-permute-start | bytes 6152 | tf_op jit(solution)/shard_map/ppermute | solution.py:274
  6.6 4.4 %collective-permute-start.4 = (bf16[272,128]{1,0:T(8,128)(2,1)S(1)}, bf16[272,128]{1,0:T(8,128)(2,1)S(1)}, u32[]{:S(2)}, u32[]{:S(2)}) collective-permute-start(bf16[272,128]{1,0:T(8,128)(2,1)S(1)} %get-tuple-element.24.own), channel_id=1, source_target_pairs={{0,48},{16,0},{32,16},{48,32},{1,49},{17,1},{33,17},{49,33},{2,50}... | collective-permute-start | bytes 208904 | tf_op jit(solution)/shard_map/ppermute | solution.py:278
  7.2 4.7 %collective-permute-start.3 = (bf16[272,128]{1,0:T(8,128)(2,1)S(1)}, bf16[272,128]{1,0:T(8,128)(2,1)S(1)}, u32[]{:S(2)}, u32[]{:S(2)}) collective-permute-start(bf16[272,128]{1,0:T(8,128)(2,1)S(1)} %get-tuple-element.24.own), channel_id=1, source_target_pairs={{0,32},{16,48},{32,0},{48,16},{1,33},{17,49},{33,1},{49,17},{2,34}... | collective-permute-start | bytes 208904 | tf_op jit(solution)/shard_map/ppermute | solution.py:278
  7.8 5.3 %collective-permute-start.2 = (bf16[272,128]{1,0:T(8,128)(2,1)S(1)}, bf16[272,128]{1,0:T(8,128)(2,1)S(1)}, u32[]{:S(2)}, u32[]{:S(2)}) collective-permute-start(bf16[272,128]{1,0:T(8,128)(2,1)S(1)} %get-tuple-element.24.own), channel_id=1, source_target_pairs={{0,16},{16,32},{32,48},{48,0},{1,17},{17,33},{33,49},{49,1},{2,18}... | collective-permute-start | bytes 208904 | tf_op jit(solution)/shard_map/ppermute | solution.py:278
  13.8 27.7 %collective-permute-start.6 = (bf16[2,512,128]{2,1,0:T(8,128)(2,1)S(1)}, bf16[2,512,128]{2,1,0:T(8,128)(2,1)S(1)}, u32[]{:S(2)}, u32[]{:S(2)}) collective-permute-start(bf16[2,512,128]{2,1,0:T(8,128)(2,1)S(1)} %get-tuple-element.26.kv), channel_id=1, source_target_pairs={{0,32},{16,48},{32,64},{48,80},{64,96},{80,112},{96,128},{112,144}... | collective-permute-start | bytes 786440 | tf_op jit(solution)/shard_map/ppermute | solution.py:329
  17.6 24.0 %collective-permute-start.5 = (bf16[2,512,128]{2,1,0:T(8,128)(2,1)S(1)}, bf16[2,512,128]{2,1,0:T(8,128)(2,1)S(1)}, u32[]{:S(2)}, u32[]{:S(2)}) collective-permute-start(bf16[2,512,128]{2,1,0:T(8,128)(2,1)S(1)} %get-tuple-element.26.kv), channel_id=1, source_target_pairs={{0,16},{16,32},{32,48},{48,64},{64,80},{80,96},{96,112},{112,128},... | collective-permute-start | bytes 786440 | tf_op jit(solution)/shard_map/ppermute | solution.py:329
  22.1 3.5 %collective-permute-start.9 = (bf16[272,128]{1,0:T(8,128)(2,1)S(1)}, bf16[272,128]{1,0:T(8,128)(2,1)S(1)}, u32[]{:S(2)}, u32[]{:S(2)}) collective-permute-start(bf16[272,128]{1,0:T(8,128)(2,1)S(1)} %get-tuple-element.25), channel_id=1, source_target_pairs={{0,192},{64,0},{128,64},{192,128},{1,193},{65,1},{129,65},{193,129... | collective-permute-start | bytes 208904 | tf_op jit(solution)/shard_map/ppermute | solution.py:278
  22.2 12.7 %collective-permute-start.8 = (bf16[272,128]{1,0:T(8,128)(2,1)S(1)}, bf16[272,128]{1,0:T(8,128)(2,1)S(1)}, u32[]{:S(2)}, u32[]{:S(2)}) collective-permute-start(bf16[272,128]{1,0:T(8,128)(2,1)S(1)} %get-tuple-element.25), channel_id=1, source_target_pairs={{0,128},{64,192},{128,0},{192,64},{1,129},{65,193},{129,1},{193,65... | collective-permute-start | bytes 208904 | tf_op jit(solution)/shard_map/ppermute | solution.py:278
  25.6 9.3 %collective-permute-start.7 = (bf16[272,128]{1,0:T(8,128)(2,1)S(1)}, bf16[272,128]{1,0:T(8,128)(2,1)S(1)}, u32[]{:S(2)}, u32[]{:S(2)}) collective-permute-start(bf16[272,128]{1,0:T(8,128)(2,1)S(1)} %get-tuple-element.25), channel_id=1, source_target_pairs={{0,64},{64,128},{128,192},{192,0},{1,65},{65,129},{129,193},{193,1... | collective-permute-start | bytes 208904 | tf_op jit(solution)/shard_map/ppermute | solution.py:278
  41.5 8.6 %copy-start = (bf16[256,2048]{1,0:T(8,128)(2,1)S(1)}, bf16[256,2048]{1,0:T(8,128)(2,1)}, u32[]{:S(2)}) copy-start(bf16[256,2048]{1,0:T(8,128)(2,1)} %own_weight.1) | copy-start | bytes 3145732
  43.7 4.4 %collective-permute-start.10 = (bf16[128,128]{1,0:T(8,128)(2,1)S(1)}, bf16[128,128]{1,0:T(8,128)(2,1)S(1)}, u32[]{:S(2)}, u32[]{:S(2)}) collective-permute-start(bf16[128,128]{1,0:T(8,128)(2,1)S(1)} %get-tuple-element.32), channel_id=1, source_target_pairs={{0,8},{1,9},{2,10},{3,11},{4,12},{5,13},{6,14},{7,15},{8,0},{9,1},... | collective-permute-start | bytes 98312 | tf_op jit(solution)/shard_map/ppermute | solution.py:283
  46.3 2.8 %collective-permute-start.11 = (bf16[128,128]{1,0:T(8,128)(2,1)S(1)}, bf16[128,128]{1,0:T(8,128)(2,1)S(1)}, u32[]{:S(2)}, u32[]{:S(2)}) collective-permute-start(bf16[128,128]{1,0:T(8,128)(2,1)S(1)} %get-tuple-element.33), channel_id=1, source_target_pairs={{0,1},{1,0},{2,3},{3,2},{4,5},{5,4},{6,7},{7,6},{8,9},{9,8},{10,11... | collective-permute-start | bytes 98312 | tf_op jit(solution)/shard_map/ppermute | solution.py:283
  46.3 3.8 %collective-permute-start.12 = (bf16[128,128]{1,0:T(8,128)(2,1)S(1)}, bf16[128,128]{1,0:T(8,128)(2,1)S(1)}, u32[]{:S(2)}, u32[]{:S(2)}) collective-permute-start(bf16[128,128]{1,0:T(8,128)(2,1)S(1)} %get-tuple-element.34), channel_id=1, source_target_pairs={{0,9},{1,8},{2,11},{3,10},{4,13},{5,12},{6,15},{7,14},{8,1},{9,0},... | collective-permute-start | bytes 98312 | tf_op jit(solution)/shard_map/ppermute | solution.py:283
  51.2 10.0 %collective-permute-start.14 = (bf16[32,2048]{1,0:T(8,128)(2,1)S(1)}, bf16[32,2048]{1,0:T(8,128)(2,1)S(1)}, u32[]{:S(2)}, u32[]{:S(2)}) collective-permute-start(bf16[32,2048]{1,0:T(8,128)(2,1)S(1)} %get-tuple-element.36), channel_id=1, source_target_pairs={{0,2},{1,3},{2,4},{3,5},{4,6},{5,7},{6,0},{7,1},{8,10},{9,11},{10,... | collective-permute-start | bytes 393224 | tf_op jit(solution)/shard_map/ppermute | solution.py:380
  54.2 13.4 %collective-permute-start.15 = (bf16[32,2048]{1,0:T(8,128)(2,1)S(1)}, bf16[32,2048]{1,0:T(8,128)(2,1)S(1)}, u32[]{:S(2)}, u32[]{:S(2)}) collective-permute-start(bf16[32,2048]{1,0:T(8,128)(2,1)S(1)} %get-tuple-element.37), channel_id=1, source_target_pairs={{0,4},{1,5},{2,6},{3,7},{4,0},{5,1},{6,2},{7,3},{8,12},{9,13},{10,... | collective-permute-start | bytes 393224 | tf_op jit(solution)/shard_map/ppermute | solution.py:380
  58.7 12.9 %collective-permute-start.16 = (bf16[32,2048]{1,0:T(8,128)(2,1)S(1)}, bf16[32,2048]{1,0:T(8,128)(2,1)S(1)}, u32[]{:S(2)}, u32[]{:S(2)}) collective-permute-start(bf16[32,2048]{1,0:T(8,128)(2,1)S(1)} %get-tuple-element.38), channel_id=1, source_target_pairs={{0,6},{1,7},{2,0},{3,1},{4,2},{5,3},{6,4},{7,5},{8,14},{9,15},{10,... | collective-permute-start | bytes 393224 | tf_op jit(solution)/shard_map/ppermute | solution.py:380

commit v3 on v2

--- a/solution.py
+++ b/solution.py
@@ -15,6 +15,7 @@
 CHIP = 2 * HALF
 ROWS = 2 * E + 16
 SLOT = 32
+SLOTS = 8
 GRANT = 16 << 20
 SEQ = ("x", "y", "c")
 XY = ("x", "y")
@@ -238,18 +239,29 @@
             total = total + jnp.sum(expo, axis=0, keepdims=True)
             result = result + dot(values_t[b], expo.astype(bf16))
         both = jnp.transpose(result / total + mesa[:, own]).astype(bf16)
-        for slot in range(HALF // SLOT):
-            at = slot // 2 * SLOT
-            place[2 * j + slot % 2, at : at + SLOT, :] = both[slot * SLOT : (slot + 1) * SLOT]
-    side = lax.rem(pos[3], 2)
-    keep_out[...] = place[2 * core + side]
-    c_out[...] = place[2 * (1 - core) + side]
-    z_out[...] = place[2 * core + 1 - side]
-    cz_out[...] = place[2 * (1 - core) + 1 - side]
+        for slot in range(SLOTS):
+            place[SLOTS * j + slot] = both[slot * SLOT : (slot + 1) * SLOT]
+
+    def piece(which, device):
+        way = 2 * lax.rem(device, 2) - 1
+        return jnp.concatenate(
+            [
+                place[SLOTS * which + lax.rem(device + way * away + SLOTS, SLOTS)]
+                for away in range(SLOTS // 2)
+            ],
+            axis=0,
+        )
+
+    here = pos[3]
+    there = here + 1 - 2 * lax.rem(here, 2)
+    keep_out[...] = piece(core, here)
+    c_out[...] = piece(1 - core, here)
+    z_out[...] = piece(core, there)
+    cz_out[...] = piece(1 - core, there)
 
 
 def project_body(pos, keep, from_c, from_z, from_cz, own_weight, pair_weight, mine, s1, s2, s3, wide):
-    core, mine_at = pos[0], lax.div(pos[3], 2)
+    core = pos[0]
     for piece, at in (
         (keep, core),
         (from_c, 1 - core),
@@ -257,21 +269,14 @@
         (from_cz, 3 - core),
     ):
         wide[:, pl.ds(pl.multiple_of(at * E, E), E)] = piece[...]
-    rows = jnp.concatenate(
-        [
-            wide[pl.ds(pl.multiple_of(lax.rem(mine_at + d, 4) * SLOT, SLOT), SLOT), :]
-            for d in range(4)
-        ],
-        axis=0,
-    )
-    y = dot(rows[:, : 2 * E], own_weight[...]) + dot(rows[:, 2 * E :], pair_weight[...])
+    y = dot(wide[:, : 2 * E], own_weight[...]) + dot(wide[:, 2 * E :], pair_weight[...])
     mine[...] = y[:SLOT]
     for d, out in ((1, s1), (2, s2), (3, s3)):
         out[...] = y[d * SLOT : (d + 1) * SLOT].astype(bf16)
 
 
-def swapped(x):
-    return lax.ppermute(x, "c", [(0, 1), (1, 0)])
+def beyond(x, by):
+    return lax.ppermute(x, XY, [(i, (i + by) % 16) for i in range(16)])
 
 
 def turned(x, axis, by):
@@ -284,15 +289,17 @@
 
 
 def on_device(queries, keys, values, log_forget, strength, out_weight):
-    core, x, y = (lax.axis_index(a) for a in ("c", "x", "y"))
-    pos = jnp.stack((core, x, y, lax.axis_index("z"))).astype(jnp.int32)
+    pos = jnp.stack([lax.axis_index(a) for a in ("c", "x", "y", "z")]).astype(jnp.int32)
+    front = lax.axis_index("c") == 0
     rows = jnp.stack((queries, keys, values))
     gates = jnp.stack((log_forget, strength), axis=1)
-    front = core == 0
     keep = jnp.where(front, rows[:, :, 0], rows[:, :, 1])
     send = jnp.where(front, rows[:, :, 1], rows[:, :, 0])
     gate_keep = jnp.where(front, gates[0], gates[1])
     gate_send = jnp.where(front, gates[1], gates[0])
+    received = across(send, 1, 0)
+    gate_received = across(gate_send, 1, 0)
+    pair_weight = across(out_weight, 0, 1)
     q, kv, gates, local, first = call(
         gram_body,
         [
@@ -306,12 +313,12 @@
         1 << 26,
         pos,
         keep,
-        swapped(send),
+        received,
         gate_keep,
-        swapped(gate_send),
+        gate_received,
     )
     around_y = [turned(local, "y", by) for by in (1, 2, 3)]
-    pair_weight = across(out_weight, 0, 1)
+    halos = [beyond(kv, 1), beyond(kv, 2)]
     row_total, state, lead = call(
         row_body,
         [((ROWS, E), bf16), ((2 * E, E), f32), ((8, E), f32)],
@@ -322,12 +329,6 @@
         *around_y,
     )
     around_x = [turned(row_total, "x", by) for by in (1, 2, 3)]
-    halo, _ = lax.optimization_barrier((kv, row_total))
-    halos = []
-    for by in (1, 2):
-        halos.append(
-            lax.ppermute(halo, XY, [(i, i + by) for i in range(16) if i + by < 16])
-        )
     (mesa,) = call(
         solve_body,
         [((E, CHIP), f32)],
@@ -354,7 +355,7 @@
     kept, to_c, to_z, to_cz = call(
         attend_body,
         [((HALF // 2, E), bf16)] * 4,
-        [((4, HALF // 2, E), bf16)],
+        [((2 * SLOTS, SLOT, E), bf16)],
         1 << 29,
         pos,
         q,
@@ -362,6 +363,9 @@
         *halos,
         mesa,
     )
+    from_cz = across(to_cz, 1, 1)
+    from_z = across(to_z, 0, 1)
+    from_c = across(to_c, 1, 0)
     mine, *sent = call(
         project_body,
         [((SLOT, 2048), f32)] + [((SLOT, 2048), bf16)] * 3,
@@ -369,16 +373,16 @@
         1 << 28,
         pos,
         kept,
-        across(to_c, 1, 0),
-        across(to_z, 0, 1),
-        across(to_cz, 1, 1),
+        from_c,
+        from_z,
+        from_cz,
         out_weight,
         pair_weight,
     )
     total = mine
-    for by, share in zip((2, 4, 6), sent):
-        got = lax.ppermute(share, "z", [(i, (i + by) % 8) for i in range(8)])
-        total = total + got.astype(f32)
+    for away, share in reversed(list(enumerate(sent, 1))):
+        pairs = [(z, (z + (2 * (z % 2) - 1) * away) % SLOTS) for z in range(SLOTS)]
+        total = total + lax.ppermute(share, "z", pairs).astype(f32)
     return total.astype(bf16)
 
 

time: 72.5 us -> 70.5 us (0.972)
  the two profiles are of different devices: /device:TPU:25 before, /device:TPU:1 now
where the time goes in v3:
time: 70.5 us; the launch traced here: 70.4 us
  starting transfers between devices  38 us (54%)
  waiting for transfers between devices  18.6 us (26%)
  Pallas kernels  11.7 us (17%)
  local copies, waits for them, and re-layouts  1.05 us (1%)
  other arithmetic  0.88 us (1%)
    ppermute x6, starting transfers between devices, turned(): return lax.ppermute(x, axis, [(i, (i + by) % 4) for i in range(4)])  14.5 us
    pallas_call x5, Pallas kernels, call(): pl.pallas_call(body, out_shape=[jax.ShapeDtypeStruct(shape, kind) for sha...  11.7 us
    ppermute x6, starting transfers between devices, across(): return lax.ppermute(x, ('c', 'z'), pairs)  11.6 us
    ppermute x3, starting transfers between devices, on_device(): total = total + lax.ppermute(share, 'z', pairs).astype(f32)  9.36 us
    ppermute x6, waiting for transfers between devices, turned(): return lax.ppermute(x, axis, [(i, (i + by) % 4) for i in range(4)])  8.14 us
    ppermute x3, waiting for transfers between devices, on_device(): total = total + lax.ppermute(share, 'z', pairs).astype(f32)  7.77 us
    ppermute x6, waiting for transfers between devices, across(): return lax.ppermute(x, ('c', 'z'), pairs)  2.69 us
    ppermute x2, starting transfers between devices, beyond(): return lax.ppermute(x, XY, [(i, (i + by) % 16) for i in range(16)])  2.56 us
  transfers between devices with their start and end apart: 17, of which 11 were waited for; matrix products, arithmetic and copies ran while one was open for 2% of the time, Pallas kernels for 15%

profile of v3, /device:TPU:1, one launch (start us, length us, event | category | flops | bytes accessed | tf_op | source)
XLA Modules:
  0.0 70.4 jit_solution(5791136960995108880)
XLA Ops:
  0.0 0.0 copy-start.1
  0.0 2.5 %collective-permute-start.13 = (bf16[256,2048]{1,0:T(8,128)(2,1)}, bf16[256,2048]{1,0:T(8,128)(2,1)S(1)}, u32[]{:S(2)}, u32[]{:S(2)}) collective-permute-start(bf16[256,2048]{1,0:T(8,128)(2,1)} %own_weight.1), channel_id=1, source_target_pairs={{0,1},{1,0},{2,3},{3,2},{4,5},{5,4},{6,7},{7,6},{8,9},{9,8},{10,11... | collective-permute-start | bytes 3145736 | tf_op jit(solution)/shard_map/ppermute | solution.py:288
  2.5 1.0 %copy_bitcast_fusion = (bf16[1,256,2,128]{3,1,0,2:T(8,128)(2,1)S(1)}, bf16[1,256,2,128]{3,1,0,2:T(8,128)(2,1)S(1)}) fusion(bf16[256,2,128]{2,1,0:T(2,128)(2,1)} %param.8, bf16[256,2,128]{2,1,0:T(2,128)(2,1)} %param.7), kind=kLoop, calls=%fused_computation.4 | loop fusion | bytes 524288 | tf_op jit(solution)/shard_map/stack | solution.py:294
  3.5 0.0 copy-done.1
  3.6 0.0 copy-start.2
  3.6 0.0 copy-start.3
  3.6 1.0 %collective-permute-start = (bf16[3,256,128]{2,1,0:T(8,128)(2,1)S(1)}, bf16[3,256,128]{2,1,0:T(8,128)(2,1)S(1)}, u32[]{:S(2)}, u32[]{:S(2)}) collective-permute-start(bf16[3,256,128]{2,1,0:T(8,128)(2,1)S(1)} %get-tuple-element.37), channel_id=1, source_target_pairs={{0,8},{1,9},{2,10},{3,11},{4,12},{5,13},{6,14},{7,15},{8,0},{9,1},... | collective-permute-start | bytes 589832 | tf_op jit(solution)/shard_map/ppermute | solution.py:288
  4.7 0.0 copy-done.2
  4.7 0.0 copy-done.3
  4.7 0.7 collective-permute-start.1
  5.4 0.1 pad_add_fusion.pos
  5.4 0.7 %collective-permute-done.1.gate_recv = f32[2,256]{1,0:T(2,128)S(1)} collective-permute-done((f32[2,256]{1,0:T(2,128)S(1)}, f32[2,256]{1,0:T(2,128)S(1)}, u32[]{:S(2)}, u32[]{:S(2)}) %collective-permute-start.1) | collective-permute-done | bytes 2080 | tf_op jit(solution)/shard_map/ppermute | solution.py:288
  6.2 0.0 collective-permute-done.recv
  6.2 1.3 %shard_map.64 = (bf16[512,128]{1,0:T(8,128)(2,1)S(1)}, bf16[2,512,128]{2,1,0:T(8,128)(2,1)S(1)}, f32[8,256]{1,0:T(8,128)S(1)}, bf16[272,128]{1,0:T(8,128)(2,1)S(1)}, f32[256,128]{1,0:T(8,128)S(1)}) custom-call(s32[4]{0:T(128)S(1)} %pad_add_fusion.pos, bf16[3,256,128]{2,1,0:T(8,128)(2,1)S(1)} %get-tuple-element.38.keep, ...), custom_call_target="tpu_custom_call" | custom-call | flops 67108864 | bytes 1048576 | tf_op jit(solution)/shard_map/pallas_call | solution.py:31
  7.4 2.8 %collective-permute-start.6 = (bf16[272,128]{1,0:T(8,128)(2,1)S(1)}, bf16[272,128]{1,0:T(8,128)(2,1)S(1)}, u32[]{:S(2)}, u32[]{:S(2)}) collective-permute-start(bf16[272,128]{1,0:T(8,128)(2,1)S(1)} %get-tuple-element.25.own), channel_id=1, source_target_pairs={{0,48},{16,0},{32,16},{48,32},{1,49},{17,1},{33,17},{49,33},{2,50}... | collective-permute-start | bytes 208904 | tf_op jit(solution)/shard_map/ppermute | solution.py:283
  10.3 0.4 collective-permute-start.5
  10.6 0.7 collective-permute-start.4
  11.3 1.9 %collective-permute-start.3 = (bf16[2,512,128]{2,1,0:T(8,128)(2,1)S(1)}, bf16[2,512,128]{2,1,0:T(8,128)(2,1)S(1)}, u32[]{:S(2)}, u32[]{:S(2)}) collective-permute-start(bf16[2,512,128]{2,1,0:T(8,128)(2,1)S(1)} %get-tuple-element.22.kv), channel_id=1, source_target_pairs={{0,32},{16,48},{32,64},{48,80},{64,96},{80,112},{96,128},{112,144}... | collective-permute-start | bytes 786440 | tf_op jit(solution)/shard_map/ppermute | solution.py:279
  13.2 0.0 collective-permute-done.6.r3
  13.2 0.6 collective-permute-start.2
  13.9 1.1 %collective-permute-done.5.r2 = bf16[272,128]{1,0:T(8,128)(2,1)S(1)} collective-permute-done((bf16[272,128]{1,0:T(8,128)(2,1)S(1)}, bf16[272,128]{1,0:T(8,128)(2,1)S(1)}, u32[]{:S(2)}, u32[]{:S(2)}) %collective-permute-start.5) | collective-permute-done | bytes 69664 | tf_op jit(solution)/shard_map/ppermute | solution.py:283
  15.0 2.0 %collective-permute-done.4.r1 = bf16[272,128]{1,0:T(8,128)(2,1)S(1)} collective-permute-done((bf16[272,128]{1,0:T(8,128)(2,1)S(1)}, bf16[272,128]{1,0:T(8,128)(2,1)S(1)}, u32[]{:S(2)}, u32[]{:S(2)}) %collective-permute-start.4) | collective-permute-done | bytes 69664 | tf_op jit(solution)/shard_map/ppermute | solution.py:283
  17.0 0.7 shard_map.65
  17.7 9.3 %collective-permute-start.9 = (bf16[272,128]{1,0:T(8,128)(2,1)S(1)}, bf16[272,128]{1,0:T(8,128)(2,1)S(1)}, u32[]{:S(2)}, u32[]{:S(2)}) collective-permute-start(bf16[272,128]{1,0:T(8,128)(2,1)S(1)} %get-tuple-element.28), channel_id=1, source_target_pairs={{0,192},{64,0},{128,64},{192,128},{1,193},{65,1},{129,65},{193,129... | collective-permute-start | bytes 208904 | tf_op jit(solution)/shard_map/ppermute | solution.py:283
  27.0 0.5 collective-permute-start.8
  27.5 0.9 %collective-permute-done.9.t3 = bf16[272,128]{1,0:T(8,128)(2,1)S(1)} collective-permute-done((bf16[272,128]{1,0:T(8,128)(2,1)S(1)}, bf16[272,128]{1,0:T(8,128)(2,1)S(1)}, u32[]{:S(2)}, u32[]{:S(2)}) %collective-permute-start.9) | collective-permute-done | bytes 69664 | tf_op jit(solution)/shard_map/ppermute | solution.py:283
  28.3 0.8 %collective-permute-start.7 = (bf16[272,128]{1,0:T(8,128)(2,1)S(1)}, bf16[272,128]{1,0:T(8,128)(2,1)S(1)}, u32[]{:S(2)}, u32[]{:S(2)}) collective-permute-start(bf16[272,128]{1,0:T(8,128)(2,1)S(1)} %get-tuple-element.28), channel_id=1, source_target_pairs={{0,64},{64,128},{128,192},{192,0},{1,65},{65,129},{129,193},{193,1... | collective-permute-start | bytes 208904 | tf_op jit(solution)/shard_map/ppermute | solution.py:283
  29.2 2.5 %collective-permute-done.8.t2 = bf16[272,128]{1,0:T(8,128)(2,1)S(1)} collective-permute-done((bf16[272,128]{1,0:T(8,128)(2,1)S(1)}, bf16[272,128]{1,0:T(8,128)(2,1)S(1)}, u32[]{:S(2)}, u32[]{:S(2)}) %collective-permute-start.8) | collective-permute-done | bytes 69664 | tf_op jit(solution)/shard_map/ppermute | solution.py:283
  31.6 1.7 %collective-permute-done.7.t1 = bf16[272,128]{1,0:T(8,128)(2,1)S(1)} collective-permute-done((bf16[272,128]{1,0:T(8,128)(2,1)S(1)}, bf16[272,128]{1,0:T(8,128)(2,1)S(1)}, u32[]{:S(2)}, u32[]{:S(2)}) %collective-permute-start.7) | collective-permute-done | bytes 69664 | tf_op jit(solution)/shard_map/ppermute | solution.py:283
  33.3 6.6 %shard_map.66.mesa = f32[128,512]{1,0:T(8,128)S(1)} custom-call(s32[4]{0:T(128)S(1)} %pad_add_fusion.pos, bf16[512,128]{1,0:T(8,128)(2,1)S(1)} %get-tuple-element.21.q, bf16[2,512,128]{2,1,0:T(8,128)(2,1)S(1)} %get-tuple-element.22.kv, f32[8,256]{1,0:T(8,128)S(1)} %get-tuple-element.23.gates, f32[256,128]{1,0:T(8,128)S(1)} %get-tuple-element.24.first, ...), custom_call_target="tpu_custom_call" | custom-call | flops 1073741824 | bytes 1048576 | tf_op jit(solution)/shard_map/pallas_call | solution.py:31
  39.9 0.0 copy-start
  39.9 0.0 collective-permute-done.3.far
  39.9 0.0 collective-permute-done.2.near
  40.0 2.1 %shard_map.67 = (bf16[128,128]{1,0:T(8,128)(2,1)S(1)}, bf16[128,128]{1,0:T(8,128)(2,1)S(1)}, bf16[128,128]{1,0:T(8,128)(2,1)S(1)}, bf16[128,128]{1,0:T(8,128)(2,1)S(1)}) custom-call(s32[4]{0:T(128)S(1)} %pad_add_fusion.pos, bf16[512,128]{1,0:T(8,128)(2,1)S(1)} %get-tuple-element.21.q, bf16[2,512,128]{2,1,0:T(8,128)(2,1)S(1)} %get-tuple-element.22.kv, ...), custom_call_target="tpu_custom_call" | custom-call | flops 536870912 | bytes 1048576 | tf_op jit(solution)/shard_map/pallas_call | solution.py:31
  42.1 5.5 %collective-permute-start.10 = (bf16[128,128]{1,0:T(8,128)(2,1)S(1)}, bf16[128,128]{1,0:T(8,128)(2,1)S(1)}, u32[]{:S(2)}, u32[]{:S(2)}) collective-permute-start(bf16[128,128]{1,0:T(8,128)(2,1)S(1)} %get-tuple-element.30), channel_id=1, source_target_pairs={{0,8},{1,9},{2,10},{3,11},{4,12},{5,13},{6,14},{7,15},{8,0},{9,1},... | collective-permute-start | bytes 98312 | tf_op jit(solution)/shard_map/ppermute | solution.py:288
  47.6 0.0 collective-permute-start.11
  47.6 1.9 %collective-permute-start.12 = (bf16[128,128]{1,0:T(8,128)(2,1)S(1)}, bf16[128,128]{1,0:T(8,128)(2,1)S(1)}, u32[]{:S(2)}, u32[]{:S(2)}) collective-permute-start(bf16[128,128]{1,0:T(8,128)(2,1)S(1)} %get-tuple-element.32), channel_id=1, source_target_pairs={{0,9},{1,8},{2,11},{3,10},{4,13},{5,12},{6,15},{7,14},{8,1},{9,0},... | collective-permute-start | bytes 98312 | tf_op jit(solution)/shard_map/ppermute | solution.py:288
  49.6 0.0 collective-permute-done.10.from_c
  49.6 0.8 %collective-permute-done.11.from_z = bf16[128,128]{1,0:T(8,128)(2,1)S(1)} collective-permute-done((bf16[128,128]{1,0:T(8,128)(2,1)S(1)}, bf16[128,128]{1,0:T(8,128)(2,1)S(1)}, u32[]{:S(2)}, u32[]{:S(2)}) %collective-permute-start.11) | collective-permute-done | bytes 32800 | tf_op jit(solution)/shard_map/ppermute | solution.py:288
  50.4 1.1 %collective-permute-done.12.from_cz = bf16[128,128]{1,0:T(8,128)(2,1)S(1)} collective-permute-done((bf16[128,128]{1,0:T(8,128)(2,1)S(1)}, bf16[128,128]{1,0:T(8,128)(2,1)S(1)}, u32[]{:S(2)}, u32[]{:S(2)}) %collective-permute-start.12) | collective-permute-done | bytes 32800 | tf_op jit(solution)/shard_map/ppermute | solution.py:288
  51.5 0.0 collective-permute-done.13.pair_weight
  51.5 0.0 copy-done
  51.5 1.0 %shard_map.68 = (f32[32,2048]{1,0:T(8,128)S(1)}, bf16[32,2048]{1,0:T(8,128)(2,1)S(1)}, bf16[32,2048]{1,0:T(8,128)(2,1)S(1)}, bf16[32,2048]{1,0:T(8,128)(2,1)S(1)}) custom-call(s32[4]{0:T(128)S(1)} %pad_add_fusion.pos, bf16[128,128]{1,0:T(8,128)(2,1)S(1)} %get-tuple-element.29.keep, bf16[128,128]{1,0:T(8,128)(2,1)S(1)} %collective-permute-done.10.from_c, ...), custom_call_target="tpu_custom_call" | custom-call | flops 268435456 | bytes 1048576 | tf_op jit(solution)/shard_map/pallas_call | solution.py:31
  52.5 6.2 %collective-permute-start.14 = (bf16[32,2048]{1,0:T(8,128)(2,1)S(1)}, bf16[32,2048]{1,0:T(8,128)(2,1)S(1)}, u32[]{:S(2)}, u32[]{:S(2)}) collective-permute-start(bf16[32,2048]{1,0:T(8,128)(2,1)S(1)} %get-tuple-element.34), channel_id=1, source_target_pairs={{0,5},{1,4},{2,7},{3,6},{4,1},{5,0},{6,3},{7,2},{8,13},{9,12},{10,... | collective-permute-start | bytes 393224 | tf_op jit(solution)/shard_map/ppermute | solution.py:385
  58.8 0.3 collective-permute-start.15
  59.0 2.8 %collective-permute-start.16 = (bf16[32,2048]{1,0:T(8,128)(2,1)S(1)}, bf16[32,2048]{1,0:T(8,128)(2,1)S(1)}, u32[]{:S(2)}, u32[]{:S(2)}) collective-permute-start(bf16[32,2048]{1,0:T(8,128)(2,1)S(1)} %get-tuple-element.36), channel_id=1, source_target_pairs={{0,7},{1,2},{2,1},{3,4},{4,3},{5,6},{6,5},{7,0},{8,15},{9,10},{10,... | collective-permute-start | bytes 393224 | tf_op jit(solution)/shard_map/ppermute | solution.py:385
  61.9 0.4 collective-permute-done.14
  62.2 6.6 %collective-permute-done.15 = bf16[32,2048]{1,0:T(8,128)(2,1)S(1)} collective-permute-done((bf16[32,2048]{1,0:T(8,128)(2,1)S(1)}, bf16[32,2048]{1,0:T(8,128)(2,1)S(1)}, u32[]{:S(2)}, u32[]{:S(2)}) %collective-permute-start.15) | collective-permute-done | bytes 131104 | tf_op jit(solution)/shard_map/ppermute | solution.py:385
  68.8 0.9 %collective-permute-done.16 = bf16[32,2048]{1,0:T(8,128)(2,1)S(1)} collective-permute-done((bf16[32,2048]{1,0:T(8,128)(2,1)S(1)}, bf16[32,2048]{1,0:T(8,128)(2,1)S(1)}, u32[]{:S(2)}, u32[]{:S(2)}) %collective-permute-start.16) | collective-permute-done | bytes 131104 | tf_op jit(solution)/shard_map/ppermute | solution.py:385
  69.7 0.7 %add_convert_fusion = bf16[32,2048]{1,0:T(8,128)(2,1)} fusion(bf16[32,2048]{1,0:T(8,128)(2,1)S(1)} %collective-permute-done.16, bf16[32,2048]{1,0:T(8,128)(2,1)S(1)} %collective-permute-done.15, f32[32,2048]{1,0:T(8,128)S(1)} %get-tuple-element.33, bf16[32,2048]{1,0:T(8,128)(2,1)S(1)} %collective-permute-done.14), kind=kLoop, calls=%fused_computation.1 | loop fusion | flops 458752 | bytes 786432 | tf_op jit(solution)/shard_map/convert_element_type | solution.py:386
  (6 shorter events, 0.1 us)
Async XLA Ops:
  0.0 3.5 %copy-start.1 = (bf16[256,2,128]{2,1,0:T(2,128)(2,1)S(1)}, bf16[256,2,128]{2,1,0:T(2,128)(2,1)}, u32[]{:S(2)}) copy-start(bf16[256,2,128]{2,1,0:T(2,128)(2,1)} %param.6) | copy-start | bytes 393220
  0.0 51.5 %collective-permute-start.13 = (bf16[256,2048]{1,0:T(8,128)(2,1)}, bf16[256,2048]{1,0:T(8,128)(2,1)S(1)}, u32[]{:S(2)}, u32[]{:S(2)}) collective-permute-start(bf16[256,2048]{1,0:T(8,128)(2,1)} %own_weight.1), channel_id=1, source_target_pairs={{0,1},{1,0},{2,3},{3,2},{4,5},{5,4},{6,7},{7,6},{8,9},{9,8},{10,11... | collective-permute-start | bytes 3145736 | tf_op jit(solution)/shard_map/ppermute | solution.py:288
  3.6 1.1 %copy-start.2 = (f32[2,256]{1,0:T(2,128)S(1)}, f32[2,256]{1,0:T(2,128)}, u32[]{:S(2)}) copy-start(f32[2,256]{1,0:T(2,128)} %param.9) | copy-start | bytes 6148
  3.6 1.1 %copy-start.3 = (f32[2,256]{1,0:T(2,128)S(1)}, f32[2,256]{1,0:T(2,128)}, u32[]{:S(2)}) copy-start(f32[2,256]{1,0:T(2,128)} %param.10) | copy-start | bytes 6148
  3.6 2.6 %collective-permute-start = (bf16[3,256,128]{2,1,0:T(8,128)(2,1)S(1)}, bf16[3,256,128]{2,1,0:T(8,128)(2,1)S(1)}, u32[]{:S(2)}, u32[]{:S(2)}) collective-permute-start(bf16[3,256,128]{2,1,0:T(8,128)(2,1)S(1)} %get-tuple-element.37), channel_id=1, source_target_pairs={{0,8},{1,9},{2,10},{3,11},{4,12},{5,13},{6,14},{7,15},{8,0},{9,1},... | collective-permute-start | bytes 589832 | tf_op jit(solution)/shard_map/ppermute | solution.py:288
  4.7 1.5 %collective-permute-start.1 = (f32[2,256]{1,0:T(2,128)S(1)}, f32[2,256]{1,0:T(2,128)S(1)}, u32[]{:S(2)}, u32[]{:S(2)}) collective-permute-start(f32[2,256]{1,0:T(2,128)S(1)} %get-tuple-element.39), channel_id=1, source_target_pairs={{0,8},{1,9},{2,10},{3,11},{4,12},{5,13},{6,14},{7,15},{8,0},{9,1},... | collective-permute-start | bytes 6152 | tf_op jit(solution)/shard_map/ppermute | solution.py:288
  7.4 5.8 %collective-permute-start.6 = (bf16[272,128]{1,0:T(8,128)(2,1)S(1)}, bf16[272,128]{1,0:T(8,128)(2,1)S(1)}, u32[]{:S(2)}, u32[]{:S(2)}) collective-permute-start(bf16[272,128]{1,0:T(8,128)(2,1)S(1)} %get-tuple-element.25.own), channel_id=1, source_target_pairs={{0,48},{16,0},{32,16},{48,32},{1,49},{17,1},{33,17},{49,33},{2,50}... | collective-permute-start | bytes 208904 | tf_op jit(solution)/shard_map/ppermute | solution.py:283
  10.3 4.7 %collective-permute-start.5 = (bf16[272,128]{1,0:T(8,128)(2,1)S(1)}, bf16[272,128]{1,0:T(8,128)(2,1)S(1)}, u32[]{:S(2)}, u32[]{:S(2)}) collective-permute-start(bf16[272,128]{1,0:T(8,128)(2,1)S(1)} %get-tuple-element.25.own), channel_id=1, source_target_pairs={{0,32},{16,48},{32,0},{48,16},{1,33},{17,49},{33,1},{49,17},{2,34}... | collective-permute-start | bytes 208904 | tf_op jit(solution)/shard_map/ppermute | solution.py:283
  10.6 6.3 %collective-permute-start.4 = (bf16[272,128]{1,0:T(8,128)(2,1)S(1)}, bf16[272,128]{1,0:T(8,128)(2,1)S(1)}, u32[]{:S(2)}, u32[]{:S(2)}) collective-permute-start(bf16[272,128]{1,0:T(8,128)(2,1)S(1)} %get-tuple-element.25.own), channel_id=1, source_target_pairs={{0,16},{16,32},{32,48},{48,0},{1,17},{17,33},{33,49},{49,1},{2,18}... | collective-permute-start | bytes 208904 | tf_op jit(solution)/shard_map/ppermute | solution.py:283
  11.3 28.6 %collective-permute-start.3 = (bf16[2,512,128]{2,1,0:T(8,128)(2,1)S(1)}, bf16[2,512,128]{2,1,0:T(8,128)(2,1)S(1)}, u32[]{:S(2)}, u32[]{:S(2)}) collective-permute-start(bf16[2,512,128]{2,1,0:T(8,128)(2,1)S(1)} %get-tuple-element.22.kv), channel_id=1, source_target_pairs={{0,32},{16,48},{32,64},{48,80},{64,96},{80,112},{96,128},{112,144}... | collective-permute-start | bytes 786440 | tf_op jit(solution)/shard_map/ppermute | solution.py:279
  13.2 26.7 %collective-permute-start.2 = (bf16[2,512,128]{2,1,0:T(8,128)(2,1)S(1)}, bf16[2,512,128]{2,1,0:T(8,128)(2,1)S(1)}, u32[]{:S(2)}, u32[]{:S(2)}) collective-permute-start(bf16[2,512,128]{2,1,0:T(8,128)(2,1)S(1)} %get-tuple-element.22.kv), channel_id=1, source_target_pairs={{0,16},{16,32},{32,48},{48,64},{64,80},{80,96},{96,112},{112,128},... | collective-permute-start | bytes 786440 | tf_op jit(solution)/shard_map/ppermute | solution.py:279
  17.7 10.7 %collective-permute-start.9 = (bf16[272,128]{1,0:T(8,128)(2,1)S(1)}, bf16[272,128]{1,0:T(8,128)(2,1)S(1)}, u32[]{:S(2)}, u32[]{:S(2)}) collective-permute-start(bf16[272,128]{1,0:T(8,128)(2,1)S(1)} %get-tuple-element.28), channel_id=1, source_target_pairs={{0,192},{64,0},{128,64},{192,128},{1,193},{65,1},{129,65},{193,129... | collective-permute-start | bytes 208904 | tf_op jit(solution)/shard_map/ppermute | solution.py:283
  27.0 4.7 %collective-permute-start.8 = (bf16[272,128]{1,0:T(8,128)(2,1)S(1)}, bf16[272,128]{1,0:T(8,128)(2,1)S(1)}, u32[]{:S(2)}, u32[]{:S(2)}) collective-permute-start(bf16[272,128]{1,0:T(8,128)(2,1)S(1)} %get-tuple-element.28), channel_id=1, source_target_pairs={{0,128},{64,192},{128,0},{192,64},{1,129},{65,193},{129,1},{193,65... | collective-permute-start | bytes 208904 | tf_op jit(solution)/shard_map/ppermute | solution.py:283
  28.3 5.0 %collective-permute-start.7 = (bf16[272,128]{1,0:T(8,128)(2,1)S(1)}, bf16[272,128]{1,0:T(8,128)(2,1)S(1)}, u32[]{:S(2)}, u32[]{:S(2)}) collective-permute-start(bf16[272,128]{1,0:T(8,128)(2,1)S(1)} %get-tuple-element.28), channel_id=1, source_target_pairs={{0,64},{64,128},{128,192},{192,0},{1,65},{65,129},{129,193},{193,1... | collective-permute-start | bytes 208904 | tf_op jit(solution)/shard_map/ppermute | solution.py:283
  39.9 11.6 %copy-start = (bf16[256,2048]{1,0:T(8,128)(2,1)S(1)}, bf16[256,2048]{1,0:T(8,128)(2,1)}, u32[]{:S(2)}) copy-start(bf16[256,2048]{1,0:T(8,128)(2,1)} %own_weight.1) | copy-start | bytes 3145732
  42.1 7.5 %collective-permute-start.10 = (bf16[128,128]{1,0:T(8,128)(2,1)S(1)}, bf16[128,128]{1,0:T(8,128)(2,1)S(1)}, u32[]{:S(2)}, u32[]{:S(2)}) collective-permute-start(bf16[128,128]{1,0:T(8,128)(2,1)S(1)} %get-tuple-element.30), channel_id=1, source_target_pairs={{0,8},{1,9},{2,10},{3,11},{4,12},{5,13},{6,14},{7,15},{8,0},{9,1},... | collective-permute-start | bytes 98312 | tf_op jit(solution)/shard_map/ppermute | solution.py:288
  47.6 2.8 %collective-permute-start.11 = (bf16[128,128]{1,0:T(8,128)(2,1)S(1)}, bf16[128,128]{1,0:T(8,128)(2,1)S(1)}, u32[]{:S(2)}, u32[]{:S(2)}) collective-permute-start(bf16[128,128]{1,0:T(8,128)(2,1)S(1)} %get-tuple-element.31), channel_id=1, source_target_pairs={{0,1},{1,0},{2,3},{3,2},{4,5},{5,4},{6,7},{7,6},{8,9},{9,8},{10,11... | collective-permute-start | bytes 98312 | tf_op jit(solution)/shard_map/ppermute | solution.py:288
  47.6 3.9 %collective-permute-start.12 = (bf16[128,128]{1,0:T(8,128)(2,1)S(1)}, bf16[128,128]{1,0:T(8,128)(2,1)S(1)}, u32[]{:S(2)}, u32[]{:S(2)}) collective-permute-start(bf16[128,128]{1,0:T(8,128)(2,1)S(1)} %get-tuple-element.32), channel_id=1, source_target_pairs={{0,9},{1,8},{2,11},{3,10},{4,13},{5,12},{6,15},{7,14},{8,1},{9,0},... | collective-permute-start | bytes 98312 | tf_op jit(solution)/shard_map/ppermute | solution.py:288
  52.5 9.7 %collective-permute-start.14 = (bf16[32,2048]{1,0:T(8,128)(2,1)S(1)}, bf16[32,2048]{1,0:T(8,128)(2,1)S(1)}, u32[]{:S(2)}, u32[]{:S(2)}) collective-permute-start(bf16[32,2048]{1,0:T(8,128)(2,1)S(1)} %get-tuple-element.34), channel_id=1, source_target_pairs={{0,5},{1,4},{2,7},{3,6},{4,1},{5,0},{6,3},{7,2},{8,13},{9,12},{10,... | collective-permute-start | bytes 393224 | tf_op jit(solution)/shard_map/ppermute | solution.py:385
  58.8 10.0 %collective-permute-start.15 = (bf16[32,2048]{1,0:T(8,128)(2,1)S(1)}, bf16[32,2048]{1,0:T(8,128)(2,1)S(1)}, u32[]{:S(2)}, u32[]{:S(2)}) collective-permute-start(bf16[32,2048]{1,0:T(8,128)(2,1)S(1)} %get-tuple-element.35), channel_id=1, source_target_pairs={{0,6},{1,3},{2,0},{3,5},{4,2},{5,7},{6,4},{7,1},{8,14},{9,11},{10,... | collective-permute-start | bytes 393224 | tf_op jit(solution)/shard_map/ppermute | solution.py:385
  59.0 10.6 %collective-permute-start.16 = (bf16[32,2048]{1,0:T(8,128)(2,1)S(1)}, bf16[32,2048]{1,0:T(8,128)(2,1)S(1)}, u32[]{:S(2)}, u32[]{:S(2)}) collective-permute-start(bf16[32,2048]{1,0:T(8,128)(2,1)S(1)} %get-tuple-element.36), channel_id=1, source_target_pairs={{0,7},{1,2},{2,1},{3,4},{4,3},{5,6},{6,5},{7,0},{8,15},{9,10},{10,... | collective-permute-start | bytes 393224 | tf_op jit(solution)/shard_map/ppermute | solution.py:385

commit v4 on v3

--- a/solution.py
+++ b/solution.py
@@ -31,7 +31,7 @@
     return pl.pallas_call(
         body,
         out_shape=[jax.ShapeDtypeStruct(shape, kind) for shape, kind in outs],
-        in_specs=[spec(pltpu.SMEM)] + [spec()] * (len(args) - 1),
+        in_specs=[spec()] * len(args),
         out_specs=[spec()] * len(outs),
         scratch_shapes=[pltpu.VMEM(shape, kind) for shape, kind in scratch],
         compiler_params=pltpu.CompilerParams(vmem_limit_bytes=GRANT),
@@ -69,8 +69,8 @@
     return wide[0:1, :] + wide[1:2, :]
 
 
-def gram_body(pos, keep, recv, gate_keep, gate_recv, q_out, kv_out, gates_out, pay_out, first_out):
-    core = pos[0]
+def gram_body(keep, recv, gate_keep, gate_recv, q_out, kv_out, gates_out, pay_out, first_out):
+    core = lax.axis_index("c")
     for source, which in ((keep, core), (recv, 1 - core)):
         rows = pl.ds(pl.multiple_of(which * HALF, HALF), HALF)
         q_out[rows, :] = source[0]
@@ -102,8 +102,8 @@
     pay_out[...] = payload(local, jnp.broadcast_to(sums[0:1, HALF - 1 :] + later, (1, E)))
 
 
-def row_body(pos, own, r1, r2, r3, pay_out, state_out, lead_out, place):
-    mine = pos[2]
+def row_body(own, r1, r2, r3, pay_out, state_out, lead_out, place):
+    mine = lax.axis_index("y")
     place[mine] = own[...]
     for distance, received in ((1, r1), (2, r2), (3, r3)):
         place[lax.rem(mine + 4 - distance, 4)] = received[...]
@@ -123,30 +123,18 @@
     lead_out[...] = jnp.broadcast_to(lead, (8, E))
 
 
-def solve_body(
-    pos, q, kv, gates, first, state, lead, t1, t2, t3, out, left, keys_t, mix, mix_v, xs, rs, ds, rr
-):
-    line = pos[1]
-    start = jnp.zeros((2 * E, E), f32)
-    passed = jnp.zeros((1, E), f32)
-    for distance, received in ((1, t1), (2, t2), (3, t3)):
-        block = received[: 2 * E, :].astype(f32)
-        start = jnp.where(line >= distance, start + jnp.exp(passed) * block, start)
-        passed = passed + decay_row(received[2 * E :, :])
-    start = jnp.exp(lead[0:1, :]) * start + state[...]
-    starts = [start, jnp.exp(gates[0:1, HALF - 1 :]) * start + first[...]]
+def prepare_body(q, kv, gates, mix, mix_v, keys_t, values_t, queries_t, leads):
     row, col = iotas((HALF, HALF))
     causal = row <= col
-    leads = []
+    line_of, _ = iotas((E, HALF))
     for j in range(2):
         own = slice(j * HALF, (j + 1) * HALF)
-        k = kv[0, own, :]
-        kt = jnp.transpose(k.astype(f32))
+        kt = jnp.transpose(kv[0, own, :].astype(f32))
         keys_t[j] = kt.astype(bf16)
+        values_t[j] = jnp.transpose(kv[1, own, :].astype(f32)).astype(bf16)
         r = lax.rsqrt(jnp.sum(kt * kt, axis=0, keepdims=True) + 1e-6)
         c = gates[j : j + 1, :]
         strength = gates[2 + j : 3 + j, :]
-        line_of, _ = iotas((E, HALF))
         columns = jnp.transpose(
             jnp.where(
                 line_of == 0, c, jnp.where(line_of == 1, strength * r * r, strength * r)
@@ -156,16 +144,38 @@
         decay = jnp.where(causal, jnp.exp(gap), 0.0)
         mix[j] = decay * columns[:, 1:2]
         mix_v[j] = decay * columns[:, 2:3]
-        leads.append(jnp.exp(c))
+        qt = jnp.transpose(q[own, :].astype(f32))
+        queries_t[j] = qt * lax.rsqrt(jnp.sum(qt * qt, axis=0, keepdims=True) + 1e-6)
+    leads[...] = jnp.exp(gates[...])
+
+
+def place_state(left, j, state):
+    high, low = split(state)
+    left[j, HALF : HALF + E, :E] = high
+    left[j, HALF : HALF + E, E:] = high
+    left[j, HALF + E :, :E] = low
+    left[j, HALF + E :, E:] = jnp.zeros((E, E), bf16)
+
+
+def solve_body(
+    kv, gates, first, state, lead, mix, mix_v, keys_t, values_t, queries_t, leads, t1, t2, t3,
+    out, left, xs, rs, ds, rr,
+):
+    line = lax.axis_index("x")
+    start = jnp.zeros((2 * E, E), f32)
+    passed = jnp.zeros((1, E), f32)
+    for distance, received in ((1, t1), (2, t2), (3, t3)):
+        block = received[: 2 * E, :].astype(f32)
+        start = jnp.where(line >= distance, start + jnp.exp(passed) * block, start)
+        passed = passed + decay_row(received[2 * E :, :])
+    start = jnp.exp(lead[0:1, :]) * start + state[...]
+    starts = [start, jnp.exp(gates[0:1, HALF - 1 :]) * start + first[...]]
+    for j in range(2):
+        k = kv[0, j * HALF : (j + 1) * HALF, :]
         left[j, :HALF, :E] = k
         left[j, :HALF, E:] = k
-        high, low = split(starts[j][:E])
-        left[j, HALF : HALF + E, :E] = high
-        left[j, HALF : HALF + E, E:] = high
-        left[j, HALF + E :, :E] = low
-        left[j, HALF + E :, E:] = jnp.zeros((E, E), bf16)
-        qt = jnp.transpose(q[own, :].astype(f32))
-        qn = qt * lax.rsqrt(jnp.sum(qt * qt, axis=0, keepdims=True) + 1e-6)
+        place_state(left, j, starts[j][:E])
+        qn = queries_t[j]
         xs[j] = jnp.zeros((E, HALF), f32)
         rs[j] = qn
         ds[j] = qn
@@ -175,7 +185,7 @@
         high, low = split(vector)
         y = dot(left[j], jnp.concatenate((high, low), axis=0))
         inside = two_part(right, weights * y[:HALF])
-        return leads[j] * (y[HALF : HALF + E] + y[HALF + E :]) + inside
+        return leads[j : j + 1, :] * (y[HALF : HALF + E] + y[HALF + E :]) + inside
 
     def iteration(_, carry):
         for j in range(2):
@@ -193,17 +203,13 @@
 
     lax.fori_loop(0, CG_STEPS, iteration, 0)
     for j in range(2):
-        own = slice(j * HALF, (j + 1) * HALF)
-        high, low = split(starts[j][E:])
-        left[j, HALF : HALF + E, :E] = high
-        left[j, HALF : HALF + E, E:] = high
-        left[j, HALF + E :, :E] = low
-        vt = jnp.transpose(kv[1, own, :].astype(f32)).astype(bf16)
-        out[:, own] = products(j, xs[j], mix_v[j], vt)
-
-
-def attend_body(pos, q, kv, near, far, mesa, keep_out, c_out, z_out, cz_out, place):
-    core, chip = pos[0], pos[1] * 4 + pos[2]
+        place_state(left, j, starts[j][E:])
+        out[:, j * HALF : (j + 1) * HALF] = products(j, xs[j], mix_v[j], values_t[j])
+
+
+def attend_body(q, kv, near, far, mesa, keep_out, c_out, z_out, cz_out, place):
+    core = lax.axis_index("c")
+    chip = lax.axis_index("x") * 4 + lax.axis_index("y")
     scale = E ** (-0.5)
     row, col = iotas((HALF, HALF))
     parts = [(far, 0, 2), (far, 1, 2), (near, 0, 1), (near, 1, 1), (kv, 0, 0), (kv, 1, 0)]
@@ -252,7 +258,7 @@
             axis=0,
         )
 
-    here = pos[3]
+    here = lax.axis_index("z")
     there = here + 1 - 2 * lax.rem(here, 2)
     keep_out[...] = piece(core, here)
     c_out[...] = piece(1 - core, here)
@@ -260,8 +266,8 @@
     cz_out[...] = piece(1 - core, there)
 
 
-def project_body(pos, keep, from_c, from_z, from_cz, own_weight, pair_weight, mine, s1, s2, s3, wide):
-    core = pos[0]
+def project_body(keep, from_c, from_z, from_cz, own_weight, pair_weight, mine, s1, s2, s3, wide):
+    core = lax.axis_index("c")
     for piece, at in (
         (keep, core),
         (from_c, 1 - core),
@@ -289,7 +295,6 @@
 
 
 def on_device(queries, keys, values, log_forget, strength, out_weight):
-    pos = jnp.stack([lax.axis_index(a) for a in ("c", "x", "y", "z")]).astype(jnp.int32)
     front = lax.axis_index("c") == 0
     rows = jnp.stack((queries, keys, values))
     gates = jnp.stack((log_forget, strength), axis=1)
@@ -311,7 +316,6 @@
         ],
         [],
         1 << 26,
-        pos,
         keep,
         received,
         gate_keep,
@@ -324,32 +328,43 @@
         [((ROWS, E), bf16), ((2 * E, E), f32), ((8, E), f32)],
         [((4, ROWS, E), bf16)],
         1 << 20,
-        pos,
         local,
         *around_y,
     )
     around_x = [turned(row_total, "x", by) for by in (1, 2, 3)]
+    prepared = call(
+        prepare_body,
+        [
+            ((2, HALF, HALF), f32),
+            ((2, HALF, HALF), f32),
+            ((2, E, HALF), bf16),
+            ((2, E, HALF), bf16),
+            ((2, E, HALF), f32),
+            ((8, HALF), f32),
+        ],
+        [],
+        1 << 26,
+        q,
+        kv,
+        gates,
+    )
     (mesa,) = call(
         solve_body,
         [((E, CHIP), f32)],
         [
-            ((2, CHIP, CHIP // 2), bf16),
-            ((2, E, HALF), bf16),
-            ((2, HALF, HALF), f32),
-            ((2, HALF, HALF), f32),
+            ((2, CHIP, 2 * E), bf16),
             ((2, E, HALF), f32),
             ((2, E, HALF), f32),
             ((2, E, HALF), f32),
             ((2, 1, HALF), f32),
         ],
         1 << 30,
-        pos,
-        q,
         kv,
         gates,
         first,
         state,
         lead,
+        *prepared,
         *around_x,
     )
     kept, to_c, to_z, to_cz = call(
@@ -357,7 +372,6 @@
         [((HALF // 2, E), bf16)] * 4,
         [((2 * SLOTS, SLOT, E), bf16)],
         1 << 29,
-        pos,
         q,
         kv,
         *halos,
@@ -371,7 +385,6 @@
         [((SLOT, 2048), f32)] + [((SLOT, 2048), bf16)] * 3,
         [((HALF // 2, 4 * E), bf16)],
         1 << 28,
-        pos,
         kept,
         from_c,
         from_z,

time: 70.5 us -> 66.1 us (0.938)
  the two profiles are of different devices: /device:TPU:1 before, /device:TPU:63 now
where the time goes in v4:
time: 66.1 us; the launch traced here: 66 us
  waiting for transfers between devices  30.5 us (46%)
  starting transfers between devices  24.3 us (37%)
  Pallas kernels  9.16 us (14%)
  local copies, waits for them, and re-layouts  1.09 us (2%)
  other arithmetic  0.81 us (1%)
    ppermute x6, waiting for transfers between devices, turned(): return lax.ppermute(x, axis, [(i, (i + by) % 4) for i in range(4)])  15.7 us
    ppermute x3, waiting for transfers between devices, on_device(): total = total + lax.ppermute(share, 'z', pairs).astype(f32)  10.5 us
    pallas_call x6, Pallas kernels, call(): pl.pallas_call(body, out_shape=[jax.ShapeDtypeStruct(shape, kind) for sha...  9.16 us
    ppermute x6, starting transfers between devices, across(): return lax.ppermute(x, ('c', 'z'), pairs)  7.71 us
    ppermute x3, starting transfers between devices, on_device(): total = total + lax.ppermute(share, 'z', pairs).astype(f32)  7.57 us
    ppermute x6, starting transfers between devices, turned(): return lax.ppermute(x, axis, [(i, (i + by) % 4) for i in range(4)])  5.27 us
    ppermute x6, waiting for transfers between devices, across(): return lax.ppermute(x, ('c', 'z'), pairs)  4.27 us
    ppermute x2, starting transfers between devices, beyond(): return lax.ppermute(x, XY, [(i, (i + by) % 16) for i in range(16)])  3.75 us
  transfers between devices with their start and end apart: 17, of which 9 were waited for; matrix products, arithmetic and copies ran while one was open for 2% of the time, Pallas kernels for 13%

profile of v4, /device:TPU:63, one launch (start us, length us, event | category | flops | bytes accessed | tf_op | source)
XLA Modules:
  0.0 66.0 jit_solution(822480492828795839)
XLA Ops:
  0.0 0.0 copy-start.1
  0.0 0.0 collective-permute-start.13
  0.0 1.0 %copy_bitcast_fusion = (bf16[1,256,2,128]{3,1,0,2:T(8,128)(2,1)S(1)}, bf16[1,256,2,128]{3,1,0,2:T(8,128)(2,1)S(1)}) fusion(bf16[256,2,128]{2,1,0:T(2,128)(2,1)} %param.8, bf16[256,2,128]{2,1,0:T(2,128)(2,1)} %param.7), kind=kLoop, calls=%fused_computation.4 | loop fusion | bytes 524288 | tf_op jit(solution)/shard_map/stack | solution.py:299
  1.1 0.0 copy-done.1
  1.1 0.0 copy-start.2
  1.2 0.0 copy-start.3
  1.2 0.8 %collective-permute-start = (bf16[3,256,128]{2,1,0:T(8,128)(2,1)S(1)}, bf16[3,256,128]{2,1,0:T(8,128)(2,1)S(1)}, u32[]{:S(2)}, u32[]{:S(2)}) collective-permute-start(bf16[3,256,128]{2,1,0:T(8,128)(2,1)S(1)} %get-tuple-element.49), channel_id=1, source_target_pairs={{0,8},{1,9},{2,10},{3,11},{4,12},{5,13},{6,14},{7,15},{8,0},{9,1},... | collective-permute-start | bytes 589832 | tf_op jit(solution)/shard_map/ppermute | solution.py:294
  2.0 0.0 copy-done.2
  2.1 0.0 copy-done.3
  2.1 0.7 collective-permute-start.1
  2.7 0.8 %collective-permute-done.1.gate_recv = f32[2,256]{1,0:T(2,128)S(1)} collective-permute-done((f32[2,256]{1,0:T(2,128)S(1)}, f32[2,256]{1,0:T(2,128)S(1)}, u32[]{:S(2)}, u32[]{:S(2)}) %collective-permute-start.1) | collective-permute-done | bytes 2080 | tf_op jit(solution)/shard_map/ppermute | solution.py:294
  3.6 0.0 collective-permute-done.recv
  3.6 0.8 %shard_map.64 = (bf16[512,128]{1,0:T(8,128)(2,1)S(1)}, bf16[2,512,128]{2,1,0:T(8,128)(2,1)S(1)}, f32[8,256]{1,0:T(8,128)S(1)}, bf16[272,128]{1,0:T(8,128)(2,1)S(1)}, f32[256,128]{1,0:T(8,128)S(1)}) custom-call(bf16[3,256,128]{2,1,0:T(8,128)(2,1)S(1)} %get-tuple-element.50.keep, bf16[3,256,128]{2,1,0:T(8,128)(2,1)S(1)} %collective-permute-done.recv, ...), custom_call_target="tpu_custom_call" | custom-call | flops 67108864 | bytes 1048576 | tf_op jit(solution)/shard_map/pallas_call | solution.py:31
  4.3 0.1 collective-permute-start.4
  4.4 2.2 %collective-permute-start.5 = (bf16[272,128]{1,0:T(8,128)(2,1)S(1)}, bf16[272,128]{1,0:T(8,128)(2,1)S(1)}, u32[]{:S(2)}, u32[]{:S(2)}) collective-permute-start(bf16[272,128]{1,0:T(8,128)(2,1)S(1)} %get-tuple-element.31.own), channel_id=1, source_target_pairs={{0,32},{16,48},{32,0},{48,16},{1,33},{17,49},{33,1},{49,17},{2,34}... | collective-permute-start | bytes 208904 | tf_op jit(solution)/shard_map/ppermute | solution.py:289
  6.7 0.0 collective-permute-start.6
  6.7 2.6 %collective-permute-start.2 = (bf16[2,512,128]{2,1,0:T(8,128)(2,1)S(1)}, bf16[2,512,128]{2,1,0:T(8,128)(2,1)S(1)}, u32[]{:S(2)}, u32[]{:S(2)}) collective-permute-start(bf16[2,512,128]{2,1,0:T(8,128)(2,1)S(1)} %get-tuple-element.28.kv), channel_id=1, source_target_pairs={{0,16},{16,32},{32,48},{48,64},{64,80},{80,96},{96,112},{112,128},... | collective-permute-start | bytes 786440 | tf_op jit(solution)/shard_map/ppermute | solution.py:285
  9.3 0.0 collective-permute-done.4.r1
  9.3 1.2 %collective-permute-start.3 = (bf16[2,512,128]{2,1,0:T(8,128)(2,1)S(1)}, bf16[2,512,128]{2,1,0:T(8,128)(2,1)S(1)}, u32[]{:S(2)}, u32[]{:S(2)}) collective-permute-start(bf16[2,512,128]{2,1,0:T(8,128)(2,1)S(1)} %get-tuple-element.28.kv), channel_id=1, source_target_pairs={{0,32},{16,48},{32,64},{48,80},{64,96},{80,112},{96,128},{112,144}... | collective-permute-start | bytes 786440 | tf_op jit(solution)/shard_map/ppermute | solution.py:285
  10.4 0.0 collective-permute-done.5.r2
  10.4 0.6 collective-permute-done.6.r3
  11.0 0.2 shard_map.65
  11.2 1.9 %collective-permute-start.7 = (bf16[272,128]{1,0:T(8,128)(2,1)S(1)}, bf16[272,128]{1,0:T(8,128)(2,1)S(1)}, u32[]{:S(2)}, u32[]{:S(2)}) collective-permute-start(bf16[272,128]{1,0:T(8,128)(2,1)S(1)} %get-tuple-element.40), channel_id=1, source_target_pairs={{0,64},{64,128},{128,192},{192,0},{1,65},{65,129},{129,193},{193,1... | collective-permute-start | bytes 208904 | tf_op jit(solution)/shard_map/ppermute | solution.py:289
  13.1 0.5 collective-permute-start.8
  13.6 11.9 %collective-permute-done.7.t1 = bf16[272,128]{1,0:T(8,128)(2,1)S(1)} collective-permute-done((bf16[272,128]{1,0:T(8,128)(2,1)S(1)}, bf16[272,128]{1,0:T(8,128)(2,1)S(1)}, u32[]{:S(2)}, u32[]{:S(2)}) %collective-permute-start.7) | collective-permute-done | bytes 69664 | tf_op jit(solution)/shard_map/ppermute | solution.py:289
  25.5 0.5 collective-permute-start.9
  26.0 0.6 shard_map.66
  26.6 0.0 collective-permute-done.8.t2
  26.6 3.2 %collective-permute-done.9.t3 = bf16[272,128]{1,0:T(8,128)(2,1)S(1)} collective-permute-done((bf16[272,128]{1,0:T(8,128)(2,1)S(1)}, bf16[272,128]{1,0:T(8,128)(2,1)S(1)}, u32[]{:S(2)}, u32[]{:S(2)}) %collective-permute-start.9) | collective-permute-done | bytes 69664 | tf_op jit(solution)/shard_map/ppermute | solution.py:289
  29.8 5.6 %shard_map.67.mesa = f32[128,512]{1,0:T(8,128)S(1)} custom-call(bf16[2,512,128]{2,1,0:T(8,128)(2,1)S(1)} %get-tuple-element.28.kv, f32[8,256]{1,0:T(8,128)S(1)} %get-tuple-element.29.gates, f32[256,128]{1,0:T(8,128)S(1)} %get-tuple-element.30.first, f32[256,128]{1,0:T(8,128)S(1)} %get-tuple-element.32.state, f32[8,128]{1,0:T(8,128)S(1)} %get-tuple-element.33.lead, ...), custom_call_target="tpu_custom_call" | custom-call | flops 1073741824 | bytes 1048576 | tf_op jit(solution)/shard_map/pallas_call | solution.py:31
  35.5 0.0 copy-start
  35.5 0.0 collective-permute-done.2.near
  35.5 0.0 collective-permute-done.3.far
  35.5 1.6 %shard_map.68 = (bf16[128,128]{1,0:T(8,128)(2,1)S(1)}, bf16[128,128]{1,0:T(8,128)(2,1)S(1)}, bf16[128,128]{1,0:T(8,128)(2,1)S(1)}, bf16[128,128]{1,0:T(8,128)(2,1)S(1)}) custom-call(bf16[512,128]{1,0:T(8,128)(2,1)S(1)} %get-tuple-element.27.q, bf16[2,512,128]{2,1,0:T(8,128)(2,1)S(1)} %get-tuple-element.28.kv, ...), custom_call_target="tpu_custom_call" | custom-call | flops 536870912 | bytes 1048576 | tf_op jit(solution)/shard_map/pallas_call | solution.py:31
  37.1 4.3 %collective-permute-start.10 = (bf16[128,128]{1,0:T(8,128)(2,1)S(1)}, bf16[128,128]{1,0:T(8,128)(2,1)S(1)}, u32[]{:S(2)}, u32[]{:S(2)}) collective-permute-start(bf16[128,128]{1,0:T(8,128)(2,1)S(1)} %get-tuple-element.42), channel_id=1, source_target_pairs={{0,8},{1,9},{2,10},{3,11},{4,12},{5,13},{6,14},{7,15},{8,0},{9,1},... | collective-permute-start | bytes 98312 | tf_op jit(solution)/shard_map/ppermute | solution.py:294
  41.4 1.6 %collective-permute-start.11 = (bf16[128,128]{1,0:T(8,128)(2,1)S(1)}, bf16[128,128]{1,0:T(8,128)(2,1)S(1)}, u32[]{:S(2)}, u32[]{:S(2)}) collective-permute-start(bf16[128,128]{1,0:T(8,128)(2,1)S(1)} %get-tuple-element.43), channel_id=1, source_target_pairs={{0,1},{1,0},{2,3},{3,2},{4,5},{5,4},{6,7},{7,6},{8,9},{9,8},{10,11... | collective-permute-start | bytes 98312 | tf_op jit(solution)/shard_map/ppermute | solution.py:294
  43.1 0.3 collective-permute-start.12
  43.3 0.0 collective-permute-done.10.from_c
  43.3 1.0 %collective-permute-done.11.from_z = bf16[128,128]{1,0:T(8,128)(2,1)S(1)} collective-permute-done((bf16[128,128]{1,0:T(8,128)(2,1)S(1)}, bf16[128,128]{1,0:T(8,128)(2,1)S(1)}, u32[]{:S(2)}, u32[]{:S(2)}) %collective-permute-start.11) | collective-permute-done | bytes 32800 | tf_op jit(solution)/shard_map/ppermute | solution.py:294
  44.4 2.4 %collective-permute-done.12.from_cz = bf16[128,128]{1,0:T(8,128)(2,1)S(1)} collective-permute-done((bf16[128,128]{1,0:T(8,128)(2,1)S(1)}, bf16[128,128]{1,0:T(8,128)(2,1)S(1)}, u32[]{:S(2)}, u32[]{:S(2)}) %collective-permute-start.12) | collective-permute-done | bytes 32800 | tf_op jit(solution)/shard_map/ppermute | solution.py:294
  46.8 0.0 collective-permute-done.13.pair_weight
  46.8 0.0 copy-done
  46.8 0.4 shard_map.69
  47.2 5.6 %collective-permute-start.14 = (bf16[32,2048]{1,0:T(8,128)(2,1)S(1)}, bf16[32,2048]{1,0:T(8,128)(2,1)S(1)}, u32[]{:S(2)}, u32[]{:S(2)}) collective-permute-start(bf16[32,2048]{1,0:T(8,128)(2,1)S(1)} %get-tuple-element.46), channel_id=1, source_target_pairs={{0,5},{1,4},{2,7},{3,6},{4,1},{5,0},{6,3},{7,2},{8,13},{9,12},{10,... | collective-permute-start | bytes 393224 | tf_op jit(solution)/shard_map/ppermute | solution.py:398
  52.9 1.2 %collective-permute-start.15 = (bf16[32,2048]{1,0:T(8,128)(2,1)S(1)}, bf16[32,2048]{1,0:T(8,128)(2,1)S(1)}, u32[]{:S(2)}, u32[]{:S(2)}) collective-permute-start(bf16[32,2048]{1,0:T(8,128)(2,1)S(1)} %get-tuple-element.47), channel_id=1, source_target_pairs={{0,6},{1,3},{2,0},{3,5},{4,2},{5,7},{6,4},{7,1},{8,14},{9,11},{10,... | collective-permute-start | bytes 393224 | tf_op jit(solution)/shard_map/ppermute | solution.py:398
  54.1 0.7 %collective-permute-start.16 = (bf16[32,2048]{1,0:T(8,128)(2,1)S(1)}, bf16[32,2048]{1,0:T(8,128)(2,1)S(1)}, u32[]{:S(2)}, u32[]{:S(2)}) collective-permute-start(bf16[32,2048]{1,0:T(8,128)(2,1)S(1)} %get-tuple-element.48), channel_id=1, source_target_pairs={{0,7},{1,2},{2,1},{3,4},{4,3},{5,6},{6,5},{7,0},{8,15},{9,10},{10,... | collective-permute-start | bytes 393224 | tf_op jit(solution)/shard_map/ppermute | solution.py:398
  54.8 4.1 %collective-permute-done.14 = bf16[32,2048]{1,0:T(8,128)(2,1)S(1)} collective-permute-done((bf16[32,2048]{1,0:T(8,128)(2,1)S(1)}, bf16[32,2048]{1,0:T(8,128)(2,1)S(1)}, u32[]{:S(2)}, u32[]{:S(2)}) %collective-permute-start.14) | collective-permute-done | bytes 131104 | tf_op jit(solution)/shard_map/ppermute | solution.py:398
  58.9 2.5 %collective-permute-done.15 = bf16[32,2048]{1,0:T(8,128)(2,1)S(1)} collective-permute-done((bf16[32,2048]{1,0:T(8,128)(2,1)S(1)}, bf16[32,2048]{1,0:T(8,128)(2,1)S(1)}, u32[]{:S(2)}, u32[]{:S(2)}) %collective-permute-start.15) | collective-permute-done | bytes 131104 | tf_op jit(solution)/shard_map/ppermute | solution.py:398
  61.4 3.9 %collective-permute-done.16 = bf16[32,2048]{1,0:T(8,128)(2,1)S(1)} collective-permute-done((bf16[32,2048]{1,0:T(8,128)(2,1)S(1)}, bf16[32,2048]{1,0:T(8,128)(2,1)S(1)}, u32[]{:S(2)}, u32[]{:S(2)}) %collective-permute-start.16) | collective-permute-done | bytes 131104 | tf_op jit(solution)/shard_map/ppermute | solution.py:398
  65.3 0.7 %add_convert_fusion = bf16[32,2048]{1,0:T(8,128)(2,1)} fusion(bf16[32,2048]{1,0:T(8,128)(2,1)S(1)} %collective-permute-done.16, bf16[32,2048]{1,0:T(8,128)(2,1)S(1)} %collective-permute-done.15, f32[32,2048]{1,0:T(8,128)S(1)} %get-tuple-element.45, bf16[32,2048]{1,0:T(8,128)(2,1)S(1)} %collective-permute-done.14), kind=kLoop, calls=%fused_computation.1 | loop fusion | flops 458752 | bytes 786432 | tf_op jit(solution)/shard_map/convert_element_type | solution.py:399
  (6 shorter events, 0.1 us)
Async XLA Ops:
  0.0 1.1 %copy-start.1 = (bf16[256,2,128]{2,1,0:T(2,128)(2,1)S(1)}, bf16[256,2,128]{2,1,0:T(2,128)(2,1)}, u32[]{:S(2)}) copy-start(bf16[256,2,128]{2,1,0:T(2,128)(2,1)} %param.6) | copy-start | bytes 393220
  0.0 46.8 %collective-permute-start.13 = (bf16[256,2048]{1,0:T(8,128)(2,1)}, bf16[256,2048]{1,0:T(8,128)(2,1)S(1)}, u32[]{:S(2)}, u32[]{:S(2)}) collective-permute-start(bf16[256,2048]{1,0:T(8,128)(2,1)} %own_weight.1), channel_id=1, source_target_pairs={{0,1},{1,0},{2,3},{3,2},{4,5},{5,4},{6,7},{7,6},{8,9},{9,8},{10,11... | collective-permute-start | bytes 3145736 | tf_op jit(solution)/shard_map/ppermute | solution.py:294
  1.1 0.9 %copy-start.2 = (f32[2,256]{1,0:T(2,128)S(1)}, f32[2,256]{1,0:T(2,128)}, u32[]{:S(2)}) copy-start(f32[2,256]{1,0:T(2,128)} %param.9) | copy-start | bytes 6148
  1.2 0.9 %copy-start.3 = (f32[2,256]{1,0:T(2,128)S(1)}, f32[2,256]{1,0:T(2,128)}, u32[]{:S(2)}) copy-start(f32[2,256]{1,0:T(2,128)} %param.10) | copy-start | bytes 6148
  1.2 2.3 %collective-permute-start = (bf16[3,256,128]{2,1,0:T(8,128)(2,1)S(1)}, bf16[3,256,128]{2,1,0:T(8,128)(2,1)S(1)}, u32[]{:S(2)}, u32[]{:S(2)}) collective-permute-start(bf16[3,256,128]{2,1,0:T(8,128)(2,1)S(1)} %get-tuple-element.49), channel_id=1, source_target_pairs={{0,8},{1,9},{2,10},{3,11},{4,12},{5,13},{6,14},{7,15},{8,0},{9,1},... | collective-permute-start | bytes 589832 | tf_op jit(solution)/shard_map/ppermute | solution.py:294
  2.1 1.5 %collective-permute-start.1 = (f32[2,256]{1,0:T(2,128)S(1)}, f32[2,256]{1,0:T(2,128)S(1)}, u32[]{:S(2)}, u32[]{:S(2)}) collective-permute-start(f32[2,256]{1,0:T(2,128)S(1)} %get-tuple-element.51), channel_id=1, source_target_pairs={{0,8},{1,9},{2,10},{3,11},{4,12},{5,13},{6,14},{7,15},{8,0},{9,1},... | collective-permute-start | bytes 6152 | tf_op jit(solution)/shard_map/ppermute | solution.py:294
  4.3 4.9 %collective-permute-start.4 = (bf16[272,128]{1,0:T(8,128)(2,1)S(1)}, bf16[272,128]{1,0:T(8,128)(2,1)S(1)}, u32[]{:S(2)}, u32[]{:S(2)}) collective-permute-start(bf16[272,128]{1,0:T(8,128)(2,1)S(1)} %get-tuple-element.31.own), channel_id=1, source_target_pairs={{0,16},{16,32},{32,48},{48,0},{1,17},{17,33},{33,49},{49,1},{2,18}... | collective-permute-start | bytes 208904 | tf_op jit(solution)/shard_map/ppermute | solution.py:289
  4.4 6.0 %collective-permute-start.5 = (bf16[272,128]{1,0:T(8,128)(2,1)S(1)}, bf16[272,128]{1,0:T(8,128)(2,1)S(1)}, u32[]{:S(2)}, u32[]{:S(2)}) collective-permute-start(bf16[272,128]{1,0:T(8,128)(2,1)S(1)} %get-tuple-element.31.own), channel_id=1, source_target_pairs={{0,32},{16,48},{32,0},{48,16},{1,33},{17,49},{33,1},{49,17},{2,34}... | collective-permute-start | bytes 208904 | tf_op jit(solution)/shard_map/ppermute | solution.py:289
  6.7 4.4 %collective-permute-start.6 = (bf16[272,128]{1,0:T(8,128)(2,1)S(1)}, bf16[272,128]{1,0:T(8,128)(2,1)S(1)}, u32[]{:S(2)}, u32[]{:S(2)}) collective-permute-start(bf16[272,128]{1,0:T(8,128)(2,1)S(1)} %get-tuple-element.31.own), channel_id=1, source_target_pairs={{0,48},{16,0},{32,16},{48,32},{1,49},{17,1},{33,17},{49,33},{2,50}... | collective-permute-start | bytes 208904 | tf_op jit(solution)/shard_map/ppermute | solution.py:289
  6.7 28.9 %collective-permute-start.2 = (bf16[2,512,128]{2,1,0:T(8,128)(2,1)S(1)}, bf16[2,512,128]{2,1,0:T(8,128)(2,1)S(1)}, u32[]{:S(2)}, u32[]{:S(2)}) collective-permute-start(bf16[2,512,128]{2,1,0:T(8,128)(2,1)S(1)} %get-tuple-element.28.kv), channel_id=1, source_target_pairs={{0,16},{16,32},{32,48},{48,64},{64,80},{80,96},{96,112},{112,128},... | collective-permute-start | bytes 786440 | tf_op jit(solution)/shard_map/ppermute | solution.py:285
  9.3 26.3 %collective-permute-start.3 = (bf16[2,512,128]{2,1,0:T(8,128)(2,1)S(1)}, bf16[2,512,128]{2,1,0:T(8,128)(2,1)S(1)}, u32[]{:S(2)}, u32[]{:S(2)}) collective-permute-start(bf16[2,512,128]{2,1,0:T(8,128)(2,1)S(1)} %get-tuple-element.28.kv), channel_id=1, source_target_pairs={{0,32},{16,48},{32,64},{48,80},{64,96},{80,112},{96,128},{112,144}... | collective-permute-start | bytes 786440 | tf_op jit(solution)/shard_map/ppermute | solution.py:285
  11.2 14.3 %collective-permute-start.7 = (bf16[272,128]{1,0:T(8,128)(2,1)S(1)}, bf16[272,128]{1,0:T(8,128)(2,1)S(1)}, u32[]{:S(2)}, u32[]{:S(2)}) collective-permute-start(bf16[272,128]{1,0:T(8,128)(2,1)S(1)} %get-tuple-element.40), channel_id=1, source_target_pairs={{0,64},{64,128},{128,192},{192,0},{1,65},{65,129},{129,193},{193,1... | collective-permute-start | bytes 208904 | tf_op jit(solution)/shard_map/ppermute | solution.py:289
  13.1 13.6 %collective-permute-start.8 = (bf16[272,128]{1,0:T(8,128)(2,1)S(1)}, bf16[272,128]{1,0:T(8,128)(2,1)S(1)}, u32[]{:S(2)}, u32[]{:S(2)}) collective-permute-start(bf16[272,128]{1,0:T(8,128)(2,1)S(1)} %get-tuple-element.40), channel_id=1, source_target_pairs={{0,128},{64,192},{128,0},{192,64},{1,129},{65,193},{129,1},{193,65... | collective-permute-start | bytes 208904 | tf_op jit(solution)/shard_map/ppermute | solution.py:289
  25.5 4.4 %collective-permute-start.9 = (bf16[272,128]{1,0:T(8,128)(2,1)S(1)}, bf16[272,128]{1,0:T(8,128)(2,1)S(1)}, u32[]{:S(2)}, u32[]{:S(2)}) collective-permute-start(bf16[272,128]{1,0:T(8,128)(2,1)S(1)} %get-tuple-element.40), channel_id=1, source_target_pairs={{0,192},{64,0},{128,64},{192,128},{1,193},{65,1},{129,65},{193,129... | collective-permute-start | bytes 208904 | tf_op jit(solution)/shard_map/ppermute | solution.py:289
  35.5 11.3 %copy-start = (bf16[256,2048]{1,0:T(8,128)(2,1)S(1)}, bf16[256,2048]{1,0:T(8,128)(2,1)}, u32[]{:S(2)}) copy-start(bf16[256,2048]{1,0:T(8,128)(2,1)} %own_weight.1) | copy-start | bytes 3145732
  37.1 6.2 %collective-permute-start.10 = (bf16[128,128]{1,0:T(8,128)(2,1)S(1)}, bf16[128,128]{1,0:T(8,128)(2,1)S(1)}, u32[]{:S(2)}, u32[]{:S(2)}) collective-permute-start(bf16[128,128]{1,0:T(8,128)(2,1)S(1)} %get-tuple-element.42), channel_id=1, source_target_pairs={{0,8},{1,9},{2,10},{3,11},{4,12},{5,13},{6,14},{7,15},{8,0},{9,1},... | collective-permute-start | bytes 98312 | tf_op jit(solution)/shard_map/ppermute | solution.py:294
  41.4 2.9 %collective-permute-start.11 = (bf16[128,128]{1,0:T(8,128)(2,1)S(1)}, bf16[128,128]{1,0:T(8,128)(2,1)S(1)}, u32[]{:S(2)}, u32[]{:S(2)}) collective-permute-start(bf16[128,128]{1,0:T(8,128)(2,1)S(1)} %get-tuple-element.43), channel_id=1, source_target_pairs={{0,1},{1,0},{2,3},{3,2},{4,5},{5,4},{6,7},{7,6},{8,9},{9,8},{10,11... | collective-permute-start | bytes 98312 | tf_op jit(solution)/shard_map/ppermute | solution.py:294
  43.1 3.7 %collective-permute-start.12 = (bf16[128,128]{1,0:T(8,128)(2,1)S(1)}, bf16[128,128]{1,0:T(8,128)(2,1)S(1)}, u32[]{:S(2)}, u32[]{:S(2)}) collective-permute-start(bf16[128,128]{1,0:T(8,128)(2,1)S(1)} %get-tuple-element.44), channel_id=1, source_target_pairs={{0,9},{1,8},{2,11},{3,10},{4,13},{5,12},{6,15},{7,14},{8,1},{9,0},... | collective-permute-start | bytes 98312 | tf_op jit(solution)/shard_map/ppermute | solution.py:294
  47.2 11.6 %collective-permute-start.14 = (bf16[32,2048]{1,0:T(8,128)(2,1)S(1)}, bf16[32,2048]{1,0:T(8,128)(2,1)S(1)}, u32[]{:S(2)}, u32[]{:S(2)}) collective-permute-start(bf16[32,2048]{1,0:T(8,128)(2,1)S(1)} %get-tuple-element.46), channel_id=1, source_target_pairs={{0,5},{1,4},{2,7},{3,6},{4,1},{5,0},{6,3},{7,2},{8,13},{9,12},{10,... | collective-permute-start | bytes 393224 | tf_op jit(solution)/shard_map/ppermute | solution.py:398
  52.9 8.5 %collective-permute-start.15 = (bf16[32,2048]{1,0:T(8,128)(2,1)S(1)}, bf16[32,2048]{1,0:T(8,128)(2,1)S(1)}, u32[]{:S(2)}, u32[]{:S(2)}) collective-permute-start(bf16[32,2048]{1,0:T(8,128)(2,1)S(1)} %get-tuple-element.47), channel_id=1, source_target_pairs={{0,6},{1,3},{2,0},{3,5},{4,2},{5,7},{6,4},{7,1},{8,14},{9,11},{10,... | collective-permute-start | bytes 393224 | tf_op jit(solution)/shard_map/ppermute | solution.py:398
  54.1 11.2 %collective-permute-start.16 = (bf16[32,2048]{1,0:T(8,128)(2,1)S(1)}, bf16[32,2048]{1,0:T(8,128)(2,1)S(1)}, u32[]{:S(2)}, u32[]{:S(2)}) collective-permute-start(bf16[32,2048]{1,0:T(8,128)(2,1)S(1)} %get-tuple-element.48), channel_id=1, source_target_pairs={{0,7},{1,2},{2,1},{3,4},{4,3},{5,6},{6,5},{7,0},{8,15},{9,10},{10,... | collective-permute-start | bytes 393224 | tf_op jit(solution)/shard_map/ppermute | solution.py:398

commit v5 on v4

--- a/solution.py
+++ b/solution.py
@@ -159,7 +159,7 @@
 
 def solve_body(
     kv, gates, first, state, lead, mix, mix_v, keys_t, values_t, queries_t, leads, t1, t2, t3,
-    out, left, xs, rs, ds, rr,
+    out, left,
 ):
     line = lax.axis_index("x")
     start = jnp.zeros((2 * E, E), f32)
@@ -175,11 +175,6 @@
         left[j, :HALF, :E] = k
         left[j, :HALF, E:] = k
         place_state(left, j, starts[j][:E])
-        qn = queries_t[j]
-        xs[j] = jnp.zeros((E, HALF), f32)
-        rs[j] = qn
-        ds[j] = qn
-        rr[j] = jnp.sum(qn * qn, axis=0, keepdims=True)
 
     def products(j, vector, weights, right):
         high, low = split(vector)
@@ -187,21 +182,20 @@
         inside = two_part(right, weights * y[:HALF])
         return leads[j : j + 1, :] * (y[HALF : HALF + E] + y[HALF + E :]) + inside
 
-    def iteration(_, carry):
+    xs = [jnp.zeros((E, HALF), f32)] * 2
+    rs = [queries_t[j] for j in range(2)]
+    ds = list(rs)
+    norms = [jnp.sum(r * r, axis=0, keepdims=True) for r in rs]
+    for _ in range(CG_STEPS):
         for j in range(2):
             d = ds[j]
             image = products(j, d, mix[j], keys_t[j]) + RIDGE * d
-            now = rr[j]
-            alpha = now / jnp.maximum(jnp.sum(d * image, axis=0, keepdims=True), TINY)
+            alpha = norms[j] / jnp.maximum(jnp.sum(d * image, axis=0, keepdims=True), TINY)
             xs[j] = xs[j] + alpha * d
-            r = rs[j] - alpha * image
-            rs[j] = r
-            new = jnp.sum(r * r, axis=0, keepdims=True)
-            ds[j] = r + new / jnp.maximum(now, TINY) * d
-            rr[j] = new
-        return carry
-
-    lax.fori_loop(0, CG_STEPS, iteration, 0)
+            rs[j] = rs[j] - alpha * image
+            new = jnp.sum(rs[j] * rs[j], axis=0, keepdims=True)
+            ds[j] = rs[j] + new / jnp.maximum(norms[j], TINY) * d
+            norms[j] = new
     for j in range(2):
         place_state(left, j, starts[j][E:])
         out[:, j * HALF : (j + 1) * HALF] = products(j, xs[j], mix_v[j], values_t[j])
@@ -281,6 +275,12 @@
         out[...] = y[d * SLOT : (d + 1) * SLOT].astype(bf16)
 
 
+def sum_body(mine, a, b, c, out):
+    out[...] = (mine[...] + a[...].astype(f32) + b[...].astype(f32) + c[...].astype(f32)).astype(
+        bf16
+    )
+
+
 def beyond(x, by):
     return lax.ppermute(x, XY, [(i, (i + by) % 16) for i in range(16)])
 
@@ -353,10 +353,6 @@
         [((E, CHIP), f32)],
         [
             ((2, CHIP, 2 * E), bf16),
-            ((2, E, HALF), f32),
-            ((2, E, HALF), f32),
-            ((2, E, HALF), f32),
-            ((2, 1, HALF), f32),
         ],
         1 << 30,
         kv,
@@ -392,11 +388,12 @@
         out_weight,
         pair_weight,
     )
-    total = mine
+    got = []
     for away, share in reversed(list(enumerate(sent, 1))):
         pairs = [(z, (z + (2 * (z % 2) - 1) * away) % SLOTS) for z in range(SLOTS)]
-        total = total + lax.ppermute(share, "z", pairs).astype(f32)
-    return total.astype(bf16)
+        got.append(lax.ppermute(share, "z", pairs))
+    (total,) = call(sum_body, [((SLOT, 2048), bf16)], [], 1 << 18, mine, *got)
+    return total
 
 
 def solution(mesh):

time: 66.1 us -> 64.2 us (0.971)
  the two profiles are of different devices: /device:TPU:63 before, /device:TPU:30 now
where the time goes in v5:
time: 64.2 us; the launch traced here: 64.1 us
  waiting for transfers between devices  30.2 us (47%)
  starting transfers between devices  23.9 us (37%)
  Pallas kernels  8.05 us (13%)
  local copies, waits for them, and re-layouts  1.61 us (3%)
    ppermute x6, waiting for transfers between devices, turned(): return lax.ppermute(x, axis, [(i, (i + by) % 4) for i in range(4)])  18.7 us
    ppermute x3, starting transfers between devices, on_device(): got.append(lax.ppermute(share, 'z', pairs))  9.93 us
    ppermute x3, waiting for transfers between devices, on_device(): got.append(lax.ppermute(share, 'z', pairs))  8.06 us
    pallas_call x7, Pallas kernels, call(): pl.pallas_call(body, out_shape=[jax.ShapeDtypeStruct(shape, kind) for sha...  8.05 us
    ppermute x6, starting transfers between devices, turned(): return lax.ppermute(x, axis, [(i, (i + by) % 4) for i in range(4)])  6.7 us
    ppermute x6, starting transfers between devices, across(): return lax.ppermute(x, ('c', 'z'), pairs)  4.04 us
    ppermute x6, waiting for transfers between devices, across(): return lax.ppermute(x, ('c', 'z'), pairs)  3.45 us
    ppermute x2, starting transfers between devices, beyond(): return lax.ppermute(x, XY, [(i, (i + by) % 16) for i in range(16)])  3.27 us
  transfers between devices with their start and end apart: 17, of which 8 were waited for; matrix products, arithmetic and copies ran while one was open for 2% of the time, Pallas kernels for 11%

profile of v5, /device:TPU:30, one launch (start us, length us, event | category | flops | bytes accessed | tf_op | source)
XLA Modules:
  0.0 64.1 jit_solution(18178567548042104461)
XLA Ops:
  0.0 0.0 copy-start.1
  0.0 1.9 %collective-permute-start.13 = (bf16[256,2048]{1,0:T(8,128)(2,1)}, bf16[256,2048]{1,0:T(8,128)(2,1)S(1)}, u32[]{:S(2)}, u32[]{:S(2)}) collective-permute-start(bf16[256,2048]{1,0:T(8,128)(2,1)} %own_weight.1), channel_id=1, source_target_pairs={{0,1},{1,0},{2,3},{3,2},{4,5},{5,4},{6,7},{7,6},{8,9},{9,8},{10,11... | collective-permute-start | bytes 3145736 | tf_op jit(solution)/shard_map/ppermute | solution.py:294
  1.9 1.0 %copy_bitcast_fusion = (bf16[1,256,2,128]{3,1,0,2:T(8,128)(2,1)S(1)}, bf16[1,256,2,128]{3,1,0,2:T(8,128)(2,1)S(1)}) fusion(bf16[256,2,128]{2,1,0:T(2,128)(2,1)} %param.8, bf16[256,2,128]{2,1,0:T(2,128)(2,1)} %param.7), kind=kLoop, calls=%fused_computation.3 | loop fusion | bytes 524288 | tf_op jit(solution)/shard_map/stack | solution.py:299
  2.9 0.0 copy-done.1
  3.0 0.0 copy-start.2
  3.1 0.0 copy-start.3
  3.1 0.1 collective-permute-start
  3.2 0.5 copy-done.2
  3.7 0.0 copy-done.3
  3.8 0.1 collective-permute-start.1
  3.9 1.1 %collective-permute-done.1.gate_recv = f32[2,256]{1,0:T(2,128)S(1)} collective-permute-done((f32[2,256]{1,0:T(2,128)S(1)}, f32[2,256]{1,0:T(2,128)S(1)}, u32[]{:S(2)}, u32[]{:S(2)}) %collective-permute-start.1) | collective-permute-done | bytes 2080 | tf_op jit(solution)/shard_map/ppermute | solution.py:294
  5.0 0.0 collective-permute-done.recv
  5.0 0.8 %shard_map.64 = (bf16[512,128]{1,0:T(8,128)(2,1)S(1)}, bf16[2,512,128]{2,1,0:T(8,128)(2,1)S(1)}, f32[8,256]{1,0:T(8,128)S(1)}, bf16[272,128]{1,0:T(8,128)(2,1)S(1)}, f32[256,128]{1,0:T(8,128)S(1)}) custom-call(bf16[3,256,128]{2,1,0:T(8,128)(2,1)S(1)} %get-tuple-element.50.keep, bf16[3,256,128]{2,1,0:T(8,128)(2,1)S(1)} %collective-permute-done.recv, ...), custom_call_target="tpu_custom_call" | custom-call | flops 67108864 | bytes 1048576 | tf_op jit(solution)/shard_map/pallas_call | solution.py:31
  5.8 0.3 collective-permute-start.4
  6.1 2.6 %collective-permute-start.5 = (bf16[272,128]{1,0:T(8,128)(2,1)S(1)}, bf16[272,128]{1,0:T(8,128)(2,1)S(1)}, u32[]{:S(2)}, u32[]{:S(2)}) collective-permute-start(bf16[272,128]{1,0:T(8,128)(2,1)S(1)} %get-tuple-element.31.own), channel_id=1, source_target_pairs={{0,32},{16,48},{32,0},{48,16},{1,33},{17,49},{33,1},{49,17},{2,34}... | collective-permute-start | bytes 208904 | tf_op jit(solution)/shard_map/ppermute | solution.py:289
  8.7 0.0 collective-permute-start.6
  8.7 3.1 %collective-permute-start.2 = (bf16[2,512,128]{2,1,0:T(8,128)(2,1)S(1)}, bf16[2,512,128]{2,1,0:T(8,128)(2,1)S(1)}, u32[]{:S(2)}, u32[]{:S(2)}) collective-permute-start(bf16[2,512,128]{2,1,0:T(8,128)(2,1)S(1)} %get-tuple-element.28.kv), channel_id=1, source_target_pairs={{0,16},{16,32},{32,48},{48,64},{64,80},{80,96},{96,112},{112,128},... | collective-permute-start | bytes 786440 | tf_op jit(solution)/shard_map/ppermute | solution.py:285
  11.8 0.0 collective-permute-done.4.r1
  11.9 0.1 collective-permute-start.3
  12.0 0.0 collective-permute-done.5.r2
  12.0 2.2 %collective-permute-done.6.r3 = bf16[272,128]{1,0:T(8,128)(2,1)S(1)} collective-permute-done((bf16[272,128]{1,0:T(8,128)(2,1)S(1)}, bf16[272,128]{1,0:T(8,128)(2,1)S(1)}, u32[]{:S(2)}, u32[]{:S(2)}) %collective-permute-start.6) | collective-permute-done | bytes 69664 | tf_op jit(solution)/shard_map/ppermute | solution.py:289
  14.2 0.2 shard_map.65
  14.4 0.6 collective-permute-start.7
  14.9 2.4 %collective-permute-start.8 = (bf16[272,128]{1,0:T(8,128)(2,1)S(1)}, bf16[272,128]{1,0:T(8,128)(2,1)S(1)}, u32[]{:S(2)}, u32[]{:S(2)}) collective-permute-start(bf16[272,128]{1,0:T(8,128)(2,1)S(1)} %get-tuple-element.40), channel_id=1, source_target_pairs={{0,128},{64,192},{128,0},{192,64},{1,129},{65,193},{129,1},{193,65... | collective-permute-start | bytes 208904 | tf_op jit(solution)/shard_map/ppermute | solution.py:289
  17.3 12.3 %collective-permute-done.7.t1 = bf16[272,128]{1,0:T(8,128)(2,1)S(1)} collective-permute-done((bf16[272,128]{1,0:T(8,128)(2,1)S(1)}, bf16[272,128]{1,0:T(8,128)(2,1)S(1)}, u32[]{:S(2)}, u32[]{:S(2)}) %collective-permute-start.7) | collective-permute-done | bytes 69664 | tf_op jit(solution)/shard_map/ppermute | solution.py:289
  29.7 0.8 %collective-permute-start.9 = (bf16[272,128]{1,0:T(8,128)(2,1)S(1)}, bf16[272,128]{1,0:T(8,128)(2,1)S(1)}, u32[]{:S(2)}, u32[]{:S(2)}) collective-permute-start(bf16[272,128]{1,0:T(8,128)(2,1)S(1)} %get-tuple-element.40), channel_id=1, source_target_pairs={{0,192},{64,0},{128,64},{192,128},{1,193},{65,1},{129,65},{193,129... | collective-permute-start | bytes 208904 | tf_op jit(solution)/shard_map/ppermute | solution.py:289
  30.5 0.6 shard_map.66
  31.1 0.0 collective-permute-done.8.t2
  31.1 4.1 %collective-permute-done.9.t3 = bf16[272,128]{1,0:T(8,128)(2,1)S(1)} collective-permute-done((bf16[272,128]{1,0:T(8,128)(2,1)S(1)}, bf16[272,128]{1,0:T(8,128)(2,1)S(1)}, u32[]{:S(2)}, u32[]{:S(2)}) %collective-permute-start.9) | collective-permute-done | bytes 69664 | tf_op jit(solution)/shard_map/ppermute | solution.py:289
  35.2 3.8 %shard_map.67.mesa = f32[128,512]{1,0:T(8,128)S(1)} custom-call(bf16[2,512,128]{2,1,0:T(8,128)(2,1)S(1)} %get-tuple-element.28.kv, f32[8,256]{1,0:T(8,128)S(1)} %get-tuple-element.29.gates, f32[256,128]{1,0:T(8,128)S(1)} %get-tuple-element.30.first, f32[256,128]{1,0:T(8,128)S(1)} %get-tuple-element.32.state, f32[8,128]{1,0:T(8,128)S(1)} %get-tuple-element.33.lead, ...), custom_call_target="tpu_custom_call" | custom-call | flops 1073741824 | bytes 1048576 | tf_op jit(solution)/shard_map/pallas_call | solution.py:31
  39.0 0.0 copy-start
  39.0 0.0 collective-permute-done.2.near
  39.1 0.0 collective-permute-done.3.far
  39.1 1.6 %shard_map.68 = (bf16[128,128]{1,0:T(8,128)(2,1)S(1)}, bf16[128,128]{1,0:T(8,128)(2,1)S(1)}, bf16[128,128]{1,0:T(8,128)(2,1)S(1)}, bf16[128,128]{1,0:T(8,128)(2,1)S(1)}) custom-call(bf16[512,128]{1,0:T(8,128)(2,1)S(1)} %get-tuple-element.27.q, bf16[2,512,128]{2,1,0:T(8,128)(2,1)S(1)} %get-tuple-element.28.kv, ...), custom_call_target="tpu_custom_call" | custom-call | flops 536870912 | bytes 1048576 | tf_op jit(solution)/shard_map/pallas_call | solution.py:31
  40.6 0.1 collective-permute-start.10
  40.7 0.2 collective-permute-start.11
  40.9 1.6 %collective-permute-start.12 = (bf16[128,128]{1,0:T(8,128)(2,1)S(1)}, bf16[128,128]{1,0:T(8,128)(2,1)S(1)}, u32[]{:S(2)}, u32[]{:S(2)}) collective-permute-start(bf16[128,128]{1,0:T(8,128)(2,1)S(1)} %get-tuple-element.44), channel_id=1, source_target_pairs={{0,9},{1,8},{2,11},{3,10},{4,13},{5,12},{6,15},{7,14},{8,1},{9,0},... | collective-permute-start | bytes 98312 | tf_op jit(solution)/shard_map/ppermute | solution.py:294
  42.6 0.0 collective-permute-done.10.from_c
  42.6 2.3 %collective-permute-done.11.from_z = bf16[128,128]{1,0:T(8,128)(2,1)S(1)} collective-permute-done((bf16[128,128]{1,0:T(8,128)(2,1)S(1)}, bf16[128,128]{1,0:T(8,128)(2,1)S(1)}, u32[]{:S(2)}, u32[]{:S(2)}) %collective-permute-start.11) | collective-permute-done | bytes 32800 | tf_op jit(solution)/shard_map/ppermute | solution.py:294
  44.9 0.0 collective-permute-done.12.from_cz
  44.9 0.0 collective-permute-done.13.pair_weight
  44.9 0.0 copy-done
  44.9 0.4 shard_map.69
  45.3 6.3 %collective-permute-start.14 = (bf16[32,2048]{1,0:T(8,128)(2,1)S(1)}, bf16[32,2048]{1,0:T(8,128)(2,1)S(1)}, u32[]{:S(2)}, u32[]{:S(2)}) collective-permute-start(bf16[32,2048]{1,0:T(8,128)(2,1)S(1)} %get-tuple-element.46), channel_id=1, source_target_pairs={{0,5},{1,4},{2,7},{3,6},{4,1},{5,0},{6,3},{7,2},{8,13},{9,12},{10,... | collective-permute-start | bytes 393224 | tf_op jit(solution)/shard_map/ppermute | solution.py:394
  51.6 0.5 collective-permute-start.15
  52.1 3.1 %collective-permute-start.16 = (bf16[32,2048]{1,0:T(8,128)(2,1)S(1)}, bf16[32,2048]{1,0:T(8,128)(2,1)S(1)}, u32[]{:S(2)}, u32[]{:S(2)}) collective-permute-start(bf16[32,2048]{1,0:T(8,128)(2,1)S(1)} %get-tuple-element.48), channel_id=1, source_target_pairs={{0,7},{1,2},{2,1},{3,4},{4,3},{5,6},{6,5},{7,0},{8,15},{9,10},{10,... | collective-permute-start | bytes 393224 | tf_op jit(solution)/shard_map/ppermute | solution.py:394
  55.3 2.9 %collective-permute-done.14.a = bf16[32,2048]{1,0:T(8,128)(2,1)S(1)} collective-permute-done((bf16[32,2048]{1,0:T(8,128)(2,1)S(1)}, bf16[32,2048]{1,0:T(8,128)(2,1)S(1)}, u32[]{:S(2)}, u32[]{:S(2)}) %collective-permute-start.14) | collective-permute-done | bytes 131104 | tf_op jit(solution)/shard_map/ppermute | solution.py:394
  58.1 3.4 %collective-permute-done.15.b = bf16[32,2048]{1,0:T(8,128)(2,1)S(1)} collective-permute-done((bf16[32,2048]{1,0:T(8,128)(2,1)S(1)}, bf16[32,2048]{1,0:T(8,128)(2,1)S(1)}, u32[]{:S(2)}, u32[]{:S(2)}) %collective-permute-start.15) | collective-permute-done | bytes 131104 | tf_op jit(solution)/shard_map/ppermute | solution.py:394
  61.5 1.8 %collective-permute-done.16.c = bf16[32,2048]{1,0:T(8,128)(2,1)S(1)} collective-permute-done((bf16[32,2048]{1,0:T(8,128)(2,1)S(1)}, bf16[32,2048]{1,0:T(8,128)(2,1)S(1)}, u32[]{:S(2)}, u32[]{:S(2)}) %collective-permute-start.16) | collective-permute-done | bytes 131104 | tf_op jit(solution)/shard_map/ppermute | solution.py:394
  63.3 0.7 %shard_map.70 = bf16[32,2048]{1,0:T(8,128)(2,1)} custom-call(f32[32,2048]{1,0:T(8,128)S(1)} %get-tuple-element.45.mine, bf16[32,2048]{1,0:T(8,128)(2,1)S(1)} %collective-permute-done.14.a, bf16[32,2048]{1,0:T(8,128)(2,1)S(1)} %collective-permute-done.15.b, bf16[32,2048]{1,0:T(8,128)(2,1)S(1)} %collective-permute-done.16.c), custom_call_target="tpu_custom_call" | custom-call | flops 262144 | bytes 1048576 | tf_op jit(solution)/shard_map/pallas_call | solution.py:31
  (6 shorter events, 0.1 us)
Async XLA Ops:
  0.0 2.9 %copy-start.1 = (bf16[256,2,128]{2,1,0:T(2,128)(2,1)S(1)}, bf16[256,2,128]{2,1,0:T(2,128)(2,1)}, u32[]{:S(2)}) copy-start(bf16[256,2,128]{2,1,0:T(2,128)(2,1)} %param.6) | copy-start | bytes 393220
  0.0 44.9 %collective-permute-start.13 = (bf16[256,2048]{1,0:T(8,128)(2,1)}, bf16[256,2048]{1,0:T(8,128)(2,1)S(1)}, u32[]{:S(2)}, u32[]{:S(2)}) collective-permute-start(bf16[256,2048]{1,0:T(8,128)(2,1)} %own_weight.1), channel_id=1, source_target_pairs={{0,1},{1,0},{2,3},{3,2},{4,5},{5,4},{6,7},{7,6},{8,9},{9,8},{10,11... | collective-permute-start | bytes 3145736 | tf_op jit(solution)/shard_map/ppermute | solution.py:294
  3.0 0.7 %copy-start.2 = (f32[2,256]{1,0:T(2,128)S(1)}, f32[2,256]{1,0:T(2,128)}, u32[]{:S(2)}) copy-start(f32[2,256]{1,0:T(2,128)} %param.9) | copy-start | bytes 6148
  3.1 0.7 %copy-start.3 = (f32[2,256]{1,0:T(2,128)S(1)}, f32[2,256]{1,0:T(2,128)}, u32[]{:S(2)}) copy-start(f32[2,256]{1,0:T(2,128)} %param.10) | copy-start | bytes 6148
  3.1 1.9 %collective-permute-start = (bf16[3,256,128]{2,1,0:T(8,128)(2,1)S(1)}, bf16[3,256,128]{2,1,0:T(8,128)(2,1)S(1)}, u32[]{:S(2)}, u32[]{:S(2)}) collective-permute-start(bf16[3,256,128]{2,1,0:T(8,128)(2,1)S(1)} %get-tuple-element.49), channel_id=1, source_target_pairs={{0,8},{1,9},{2,10},{3,11},{4,12},{5,13},{6,14},{7,15},{8,0},{9,1},... | collective-permute-start | bytes 589832 | tf_op jit(solution)/shard_map/ppermute | solution.py:294
  3.8 1.2 %collective-permute-start.1 = (f32[2,256]{1,0:T(2,128)S(1)}, f32[2,256]{1,0:T(2,128)S(1)}, u32[]{:S(2)}, u32[]{:S(2)}) collective-permute-start(f32[2,256]{1,0:T(2,128)S(1)} %get-tuple-element.51), channel_id=1, source_target_pairs={{0,8},{1,9},{2,10},{3,11},{4,12},{5,13},{6,14},{7,15},{8,0},{9,1},... | collective-permute-start | bytes 6152 | tf_op jit(solution)/shard_map/ppermute | solution.py:294
  5.8 6.0 %collective-permute-start.4 = (bf16[272,128]{1,0:T(8,128)(2,1)S(1)}, bf16[272,128]{1,0:T(8,128)(2,1)S(1)}, u32[]{:S(2)}, u32[]{:S(2)}) collective-permute-start(bf16[272,128]{1,0:T(8,128)(2,1)S(1)} %get-tuple-element.31.own), channel_id=1, source_target_pairs={{0,16},{16,32},{32,48},{48,0},{1,17},{17,33},{33,49},{49,1},{2,18}... | collective-permute-start | bytes 208904 | tf_op jit(solution)/shard_map/ppermute | solution.py:289
  6.1 5.9 %collective-permute-start.5 = (bf16[272,128]{1,0:T(8,128)(2,1)S(1)}, bf16[272,128]{1,0:T(8,128)(2,1)S(1)}, u32[]{:S(2)}, u32[]{:S(2)}) collective-permute-start(bf16[272,128]{1,0:T(8,128)(2,1)S(1)} %get-tuple-element.31.own), channel_id=1, source_target_pairs={{0,32},{16,48},{32,0},{48,16},{1,33},{17,49},{33,1},{49,17},{2,34}... | collective-permute-start | bytes 208904 | tf_op jit(solution)/shard_map/ppermute | solution.py:289
  8.7 5.5 %collective-permute-start.6 = (bf16[272,128]{1,0:T(8,128)(2,1)S(1)}, bf16[272,128]{1,0:T(8,128)(2,1)S(1)}, u32[]{:S(2)}, u32[]{:S(2)}) collective-permute-start(bf16[272,128]{1,0:T(8,128)(2,1)S(1)} %get-tuple-element.31.own), channel_id=1, source_target_pairs={{0,48},{16,0},{32,16},{48,32},{1,49},{17,1},{33,17},{49,33},{2,50}... | collective-permute-start | bytes 208904 | tf_op jit(solution)/shard_map/ppermute | solution.py:289
  8.7 30.3 %collective-permute-start.2 = (bf16[2,512,128]{2,1,0:T(8,128)(2,1)S(1)}, bf16[2,512,128]{2,1,0:T(8,128)(2,1)S(1)}, u32[]{:S(2)}, u32[]{:S(2)}) collective-permute-start(bf16[2,512,128]{2,1,0:T(8,128)(2,1)S(1)} %get-tuple-element.28.kv), channel_id=1, source_target_pairs={{0,16},{16,32},{32,48},{48,64},{64,80},{80,96},{96,112},{112,128},... | collective-permute-start | bytes 786440 | tf_op jit(solution)/shard_map/ppermute | solution.py:285
  11.9 27.2 %collective-permute-start.3 = (bf16[2,512,128]{2,1,0:T(8,128)(2,1)S(1)}, bf16[2,512,128]{2,1,0:T(8,128)(2,1)S(1)}, u32[]{:S(2)}, u32[]{:S(2)}) collective-permute-start(bf16[2,512,128]{2,1,0:T(8,128)(2,1)S(1)} %get-tuple-element.28.kv), channel_id=1, source_target_pairs={{0,32},{16,48},{32,64},{48,80},{64,96},{80,112},{96,128},{112,144}... | collective-permute-start | bytes 786440 | tf_op jit(solution)/shard_map/ppermute | solution.py:285
  14.4 15.3 %collective-permute-start.7 = (bf16[272,128]{1,0:T(8,128)(2,1)S(1)}, bf16[272,128]{1,0:T(8,128)(2,1)S(1)}, u32[]{:S(2)}, u32[]{:S(2)}) collective-permute-start(bf16[272,128]{1,0:T(8,128)(2,1)S(1)} %get-tuple-element.40), channel_id=1, source_target_pairs={{0,64},{64,128},{128,192},{192,0},{1,65},{65,129},{129,193},{193,1... | collective-permute-start | bytes 208904 | tf_op jit(solution)/shard_map/ppermute | solution.py:289
  14.9 16.2 %collective-permute-start.8 = (bf16[272,128]{1,0:T(8,128)(2,1)S(1)}, bf16[272,128]{1,0:T(8,128)(2,1)S(1)}, u32[]{:S(2)}, u32[]{:S(2)}) collective-permute-start(bf16[272,128]{1,0:T(8,128)(2,1)S(1)} %get-tuple-element.40), channel_id=1, source_target_pairs={{0,128},{64,192},{128,0},{192,64},{1,129},{65,193},{129,1},{193,65... | collective-permute-start | bytes 208904 | tf_op jit(solution)/shard_map/ppermute | solution.py:289
  29.7 5.5 %collective-permute-start.9 = (bf16[272,128]{1,0:T(8,128)(2,1)S(1)}, bf16[272,128]{1,0:T(8,128)(2,1)S(1)}, u32[]{:S(2)}, u32[]{:S(2)}) collective-permute-start(bf16[272,128]{1,0:T(8,128)(2,1)S(1)} %get-tuple-element.40), channel_id=1, source_target_pairs={{0,192},{64,0},{128,64},{192,128},{1,193},{65,1},{129,65},{193,129... | collective-permute-start | bytes 208904 | tf_op jit(solution)/shard_map/ppermute | solution.py:289
  39.0 5.9 %copy-start = (bf16[256,2048]{1,0:T(8,128)(2,1)S(1)}, bf16[256,2048]{1,0:T(8,128)(2,1)}, u32[]{:S(2)}) copy-start(bf16[256,2048]{1,0:T(8,128)(2,1)} %own_weight.1) | copy-start | bytes 3145732
  40.6 2.0 %collective-permute-start.10 = (bf16[128,128]{1,0:T(8,128)(2,1)S(1)}, bf16[128,128]{1,0:T(8,128)(2,1)S(1)}, u32[]{:S(2)}, u32[]{:S(2)}) collective-permute-start(bf16[128,128]{1,0:T(8,128)(2,1)S(1)} %get-tuple-element.42), channel_id=1, source_target_pairs={{0,8},{1,9},{2,10},{3,11},{4,12},{5,13},{6,14},{7,15},{8,0},{9,1},... | collective-permute-start | bytes 98312 | tf_op jit(solution)/shard_map/ppermute | solution.py:294
  40.7 4.1 %collective-permute-start.11 = (bf16[128,128]{1,0:T(8,128)(2,1)S(1)}, bf16[128,128]{1,0:T(8,128)(2,1)S(1)}, u32[]{:S(2)}, u32[]{:S(2)}) collective-permute-start(bf16[128,128]{1,0:T(8,128)(2,1)S(1)} %get-tuple-element.43), channel_id=1, source_target_pairs={{0,1},{1,0},{2,3},{3,2},{4,5},{5,4},{6,7},{7,6},{8,9},{9,8},{10,11... | collective-permute-start | bytes 98312 | tf_op jit(solution)/shard_map/ppermute | solution.py:294
  40.9 3.9 %collective-permute-start.12 = (bf16[128,128]{1,0:T(8,128)(2,1)S(1)}, bf16[128,128]{1,0:T(8,128)(2,1)S(1)}, u32[]{:S(2)}, u32[]{:S(2)}) collective-permute-start(bf16[128,128]{1,0:T(8,128)(2,1)S(1)} %get-tuple-element.44), channel_id=1, source_target_pairs={{0,9},{1,8},{2,11},{3,10},{4,13},{5,12},{6,15},{7,14},{8,1},{9,0},... | collective-permute-start | bytes 98312 | tf_op jit(solution)/shard_map/ppermute | solution.py:294
  45.3 12.8 %collective-permute-start.14 = (bf16[32,2048]{1,0:T(8,128)(2,1)S(1)}, bf16[32,2048]{1,0:T(8,128)(2,1)S(1)}, u32[]{:S(2)}, u32[]{:S(2)}) collective-permute-start(bf16[32,2048]{1,0:T(8,128)(2,1)S(1)} %get-tuple-element.46), channel_id=1, source_target_pairs={{0,5},{1,4},{2,7},{3,6},{4,1},{5,0},{6,3},{7,2},{8,13},{9,12},{10,... | collective-permute-start | bytes 393224 | tf_op jit(solution)/shard_map/ppermute | solution.py:394
  51.6 9.9 %collective-permute-start.15 = (bf16[32,2048]{1,0:T(8,128)(2,1)S(1)}, bf16[32,2048]{1,0:T(8,128)(2,1)S(1)}, u32[]{:S(2)}, u32[]{:S(2)}) collective-permute-start(bf16[32,2048]{1,0:T(8,128)(2,1)S(1)} %get-tuple-element.47), channel_id=1, source_target_pairs={{0,6},{1,3},{2,0},{3,5},{4,2},{5,7},{6,4},{7,1},{8,14},{9,11},{10,... | collective-permute-start | bytes 393224 | tf_op jit(solution)/shard_map/ppermute | solution.py:394
  52.1 11.2 %collective-permute-start.16 = (bf16[32,2048]{1,0:T(8,128)(2,1)S(1)}, bf16[32,2048]{1,0:T(8,128)(2,1)S(1)}, u32[]{:S(2)}, u32[]{:S(2)}) collective-permute-start(bf16[32,2048]{1,0:T(8,128)(2,1)S(1)} %get-tuple-element.48), channel_id=1, source_target_pairs={{0,7},{1,2},{2,1},{3,4},{4,3},{5,6},{6,5},{7,0},{8,15},{9,10},{10,... | collective-permute-start | bytes 393224 | tf_op jit(solution)/shard_map/ppermute | solution.py:394

commit v6 on v5

--- a/solution.py
+++ b/solution.py
@@ -13,7 +13,9 @@
 HALF = 256
 E = 128
 CHIP = 2 * HALF
-ROWS = 2 * E + 16
+SIDE = E // 2
+BODY = SIDE + E
+ROWS = BODY + 16
 SLOT = 32
 SLOTS = 8
 GRANT = 16 << 20
@@ -57,11 +59,33 @@
     return lax.broadcasted_iota(jnp.int32, shape, 0), lax.broadcasted_iota(jnp.int32, shape, 1)
 
 
+def packed(state):
+    top, bottom = state[:SIDE], pltpu.roll(state[SIDE:E], SIDE, 1)
+    row, col = iotas((SIDE, E))
+    square = jnp.where((col < SIDE) & (row < col), bottom, top)
+    diagonal = jnp.sum(jnp.where(row == col, bottom, 0.0), axis=0, keepdims=True)
+    line, _ = iotas((16, E))
+    return jnp.concatenate((square, state[E:], jnp.where(line == 2, diagonal, 0.0)), axis=0)
+
+
+def unpacked(state):
+    square, diagonal = state[:SIDE], state[BODY + 2 : BODY + 3]
+    turned_square = jnp.transpose(jnp.concatenate((square, jnp.zeros((SIDE, E), f32)), axis=0))
+    other = turned_square[:SIDE]
+    row, col = iotas((SIDE, E))
+    top = jnp.where((col < SIDE) & (row < col), other, square)
+    corner = jnp.where(row < col, square, jnp.where(row > col, other, diagonal))
+    bottom = jnp.where(col < SIDE, turned_square[SIDE:], pltpu.roll(corner, SIDE, 1))
+    return jnp.concatenate((top, bottom, state[SIDE:BODY]), axis=0)
+
+
 def payload(state, total):
     high, low = split(total)
     row, _ = iotas((16, E))
-    tail = jnp.where(row == 0, high.astype(f32), jnp.where(row == 1, low.astype(f32), 0.0))
-    return jnp.concatenate((state, tail), axis=0).astype(bf16)
+    tail = jnp.where(
+        row == 0, high.astype(f32), jnp.where(row == 1, low.astype(f32), state[BODY:])
+    )
+    return jnp.concatenate((state[:BODY], tail), axis=0).astype(bf16)
 
 
 def decay_row(tail):
@@ -99,7 +123,7 @@
     first_out[...] = grams[0]
     later = sums[1:2, HALF - 1 :]
     local = jnp.exp(later) * grams[0] + grams[1]
-    pay_out[...] = payload(local, jnp.broadcast_to(sums[0:1, HALF - 1 :] + later, (1, E)))
+    pay_out[...] = payload(packed(local), jnp.broadcast_to(sums[0:1, HALF - 1 :] + later, (1, E)))
 
 
 def row_body(own, r1, r2, r3, pay_out, state_out, lead_out, place):
@@ -107,12 +131,12 @@
     place[mine] = own[...]
     for distance, received in ((1, r1), (2, r2), (3, r3)):
         place[lax.rem(mine + 4 - distance, 4)] = received[...]
-    decays = [decay_row(place[m, 2 * E :, :]) for m in range(4)]
+    decays = [decay_row(place[m, BODY:, :]) for m in range(4)]
     zero = jnp.zeros((1, E), f32)
-    total = before = jnp.zeros((2 * E, E), f32)
+    total = before = jnp.zeros((ROWS, E), f32)
     lead = zero
     for m in range(4):
-        block = place[m, : 2 * E, :].astype(f32)
+        block = place[m].astype(f32)
         step = jnp.exp(decays[m])
         total = step * total + block
         earlier = m < mine
@@ -162,13 +186,13 @@
     out, left,
 ):
     line = lax.axis_index("x")
-    start = jnp.zeros((2 * E, E), f32)
+    start = jnp.zeros((ROWS, E), f32)
     passed = jnp.zeros((1, E), f32)
     for distance, received in ((1, t1), (2, t2), (3, t3)):
-        block = received[: 2 * E, :].astype(f32)
+        block = received[...].astype(f32)
         start = jnp.where(line >= distance, start + jnp.exp(passed) * block, start)
-        passed = passed + decay_row(received[2 * E :, :])
-    start = jnp.exp(lead[0:1, :]) * start + state[...]
+        passed = passed + decay_row(received[BODY:, :])
+    start = unpacked(jnp.exp(lead[0:1, :]) * start + state[...])
     starts = [start, jnp.exp(gates[0:1, HALF - 1 :]) * start + first[...]]
     for j in range(2):
         k = kv[0, j * HALF : (j + 1) * HALF, :]
@@ -325,7 +349,7 @@
     halos = [beyond(kv, 1), beyond(kv, 2)]
     row_total, state, lead = call(
         row_body,
-        [((ROWS, E), bf16), ((2 * E, E), f32), ((8, E), f32)],
+        [((ROWS, E), bf16), ((ROWS, E), f32), ((8, E), f32)],
         [((4, ROWS, E), bf16)],
         1 << 20,
         local,

time: 64.2 us -> 65.6 us (1.022)
  the two profiles are of different devices: /device:TPU:30 before, /device:TPU:1 now
where the time goes in v6:
time: 65.6 us; the launch traced here: 65.5 us
  waiting for transfers between devices  28.2 us (43%)
  starting transfers between devices  28 us (43%)
  Pallas kernels  8.08 us (12%)
  local copies, waits for them, and re-layouts  1.05 us (2%)
    ppermute x6, waiting for transfers between devices, turned(): return lax.ppermute(x, axis, [(i, (i + by) % 4) for i in range(4)])  16.2 us
    ppermute x6, starting transfers between devices, across(): return lax.ppermute(x, ('c', 'z'), pairs)  9.2 us
    ppermute x3, starting transfers between devices, on_device(): got.append(lax.ppermute(share, 'z', pairs))  8.34 us
    ppermute x3, waiting for transfers between devices, on_device(): got.append(lax.ppermute(share, 'z', pairs))  8.29 us
    pallas_call x7, Pallas kernels, call(): pl.pallas_call(body, out_shape=[jax.ShapeDtypeStruct(shape, kind) for sha...  8.08 us
    ppermute x6, starting transfers between devices, turned(): return lax.ppermute(x, axis, [(i, (i + by) % 4) for i in range(4)])  7.71 us
    ppermute x6, waiting for transfers between devices, across(): return lax.ppermute(x, ('c', 'z'), pairs)  3.63 us
    ppermute x2, starting transfers between devices, beyond(): return lax.ppermute(x, XY, [(i, (i + by) % 16) for i in range(16)])  2.71 us
  transfers between devices with their start and end apart: 17, of which 9 were waited for; matrix products, arithmetic and copies ran while one was open for 2% of the time, Pallas kernels for 11%

profile of v6, /device:TPU:1, one launch (start us, length us, event | category | flops | bytes accessed | tf_op | source)
XLA Modules:
  0.0 65.5 jit_solution(18251703600305791465)
XLA Ops:
  0.0 0.0 copy-start.1
  0.0 2.5 %collective-permute-start.13 = (bf16[256,2048]{1,0:T(8,128)(2,1)}, bf16[256,2048]{1,0:T(8,128)(2,1)S(1)}, u32[]{:S(2)}, u32[]{:S(2)}) collective-permute-start(bf16[256,2048]{1,0:T(8,128)(2,1)} %own_weight.1), channel_id=1, source_target_pairs={{0,1},{1,0},{2,3},{3,2},{4,5},{5,4},{6,7},{7,6},{8,9},{9,8},{10,11... | collective-permute-start | bytes 3145736 | tf_op jit(solution)/shard_map/ppermute | solution.py:318
  2.5 1.0 %copy_bitcast_fusion = (bf16[1,256,2,128]{3,1,0,2:T(8,128)(2,1)S(1)}, bf16[1,256,2,128]{3,1,0,2:T(8,128)(2,1)S(1)}) fusion(bf16[256,2,128]{2,1,0:T(2,128)(2,1)} %param.8, bf16[256,2,128]{2,1,0:T(2,128)(2,1)} %param.7), kind=kLoop, calls=%fused_computation.3 | loop fusion | bytes 524288 | tf_op jit(solution)/shard_map/stack | solution.py:323
  3.5 0.0 copy-done.1
  3.6 0.0 copy-start.2
  3.6 0.0 copy-start.3
  3.6 1.0 %collective-permute-start = (bf16[3,256,128]{2,1,0:T(8,128)(2,1)S(1)}, bf16[3,256,128]{2,1,0:T(8,128)(2,1)S(1)}, u32[]{:S(2)}, u32[]{:S(2)}) collective-permute-start(bf16[3,256,128]{2,1,0:T(8,128)(2,1)S(1)} %get-tuple-element.49), channel_id=1, source_target_pairs={{0,8},{1,9},{2,10},{3,11},{4,12},{5,13},{6,14},{7,15},{8,0},{9,1},... | collective-permute-start | bytes 589832 | tf_op jit(solution)/shard_map/ppermute | solution.py:318
  4.7 0.0 copy-done.2
  4.7 0.0 copy-done.3
  4.7 0.7 collective-permute-start.1
  5.4 0.8 %collective-permute-done.1.gate_recv = f32[2,256]{1,0:T(2,128)S(1)} collective-permute-done((f32[2,256]{1,0:T(2,128)S(1)}, f32[2,256]{1,0:T(2,128)S(1)}, u32[]{:S(2)}, u32[]{:S(2)}) %collective-permute-start.1) | collective-permute-done | bytes 2080 | tf_op jit(solution)/shard_map/ppermute | solution.py:318
  6.2 0.0 collective-permute-done.recv
  6.2 0.8 %shard_map.64 = (bf16[512,128]{1,0:T(8,128)(2,1)S(1)}, bf16[2,512,128]{2,1,0:T(8,128)(2,1)S(1)}, f32[8,256]{1,0:T(8,128)S(1)}, bf16[208,128]{1,0:T(8,128)(2,1)S(1)}, f32[256,128]{1,0:T(8,128)S(1)}) custom-call(bf16[3,256,128]{2,1,0:T(8,128)(2,1)S(1)} %get-tuple-element.50.keep, bf16[3,256,128]{2,1,0:T(8,128)(2,1)S(1)} %collective-permute-done.recv, ...), custom_call_target="tpu_custom_call" | custom-call | flops 67108864 | bytes 1048576 | tf_op jit(solution)/shard_map/pallas_call | solution.py:33
  7.0 1.4 %collective-permute-start.4 = (bf16[208,128]{1,0:T(8,128)(2,1)S(1)}, bf16[208,128]{1,0:T(8,128)(2,1)S(1)}, u32[]{:S(2)}, u32[]{:S(2)}) collective-permute-start(bf16[208,128]{1,0:T(8,128)(2,1)S(1)} %get-tuple-element.31.own), channel_id=1, source_target_pairs={{0,16},{16,32},{32,48},{48,0},{1,17},{17,33},{33,49},{49,1},{2,18}... | collective-permute-start | bytes 159752 | tf_op jit(solution)/shard_map/ppermute | solution.py:313
  8.4 1.3 %collective-permute-start.2 = (bf16[2,512,128]{2,1,0:T(8,128)(2,1)S(1)}, bf16[2,512,128]{2,1,0:T(8,128)(2,1)S(1)}, u32[]{:S(2)}, u32[]{:S(2)}) collective-permute-start(bf16[2,512,128]{2,1,0:T(8,128)(2,1)S(1)} %get-tuple-element.28.kv), channel_id=1, source_target_pairs={{0,16},{16,32},{32,48},{48,64},{64,80},{80,96},{96,112},{112,128},... | collective-permute-start | bytes 786440 | tf_op jit(solution)/shard_map/ppermute | solution.py:309
  9.7 1.4 %collective-permute-start.3 = (bf16[2,512,128]{2,1,0:T(8,128)(2,1)S(1)}, bf16[2,512,128]{2,1,0:T(8,128)(2,1)S(1)}, u32[]{:S(2)}, u32[]{:S(2)}) collective-permute-start(bf16[2,512,128]{2,1,0:T(8,128)(2,1)S(1)} %get-tuple-element.28.kv), channel_id=1, source_target_pairs={{0,32},{16,48},{32,64},{48,80},{64,96},{80,112},{96,128},{112,144}... | collective-permute-start | bytes 786440 | tf_op jit(solution)/shard_map/ppermute | solution.py:309
  11.1 2.5 %collective-permute-start.5 = (bf16[208,128]{1,0:T(8,128)(2,1)S(1)}, bf16[208,128]{1,0:T(8,128)(2,1)S(1)}, u32[]{:S(2)}, u32[]{:S(2)}) collective-permute-start(bf16[208,128]{1,0:T(8,128)(2,1)S(1)} %get-tuple-element.31.own), channel_id=1, source_target_pairs={{0,32},{16,48},{32,0},{48,16},{1,33},{17,49},{33,1},{49,17},{2,34}... | collective-permute-start | bytes 159752 | tf_op jit(solution)/shard_map/ppermute | solution.py:313
  13.6 0.0 collective-permute-done.4.r1
  13.6 1.4 %collective-permute-start.6 = (bf16[208,128]{1,0:T(8,128)(2,1)S(1)}, bf16[208,128]{1,0:T(8,128)(2,1)S(1)}, u32[]{:S(2)}, u32[]{:S(2)}) collective-permute-start(bf16[208,128]{1,0:T(8,128)(2,1)S(1)} %get-tuple-element.31.own), channel_id=1, source_target_pairs={{0,48},{16,0},{32,16},{48,32},{1,49},{17,1},{33,17},{49,33},{2,50}... | collective-permute-start | bytes 159752 | tf_op jit(solution)/shard_map/ppermute | solution.py:313
  15.0 11.5 %collective-permute-done.5.r2 = bf16[208,128]{1,0:T(8,128)(2,1)S(1)} collective-permute-done((bf16[208,128]{1,0:T(8,128)(2,1)S(1)}, bf16[208,128]{1,0:T(8,128)(2,1)S(1)}, u32[]{:S(2)}, u32[]{:S(2)}) %collective-permute-start.5) | collective-permute-done | bytes 53280 | tf_op jit(solution)/shard_map/ppermute | solution.py:313
  26.4 0.0 collective-permute-done.6.r3
  26.4 0.1 shard_map.65
  26.6 0.1 collective-permute-start.7
  26.6 2.4 %collective-permute-start.8 = (bf16[208,128]{1,0:T(8,128)(2,1)S(1)}, bf16[208,128]{1,0:T(8,128)(2,1)S(1)}, u32[]{:S(2)}, u32[]{:S(2)}) collective-permute-start(bf16[208,128]{1,0:T(8,128)(2,1)S(1)} %get-tuple-element.40), channel_id=1, source_target_pairs={{0,128},{64,192},{128,0},{192,64},{1,129},{65,193},{129,1},{193,65... | collective-permute-start | bytes 159752 | tf_op jit(solution)/shard_map/ppermute | solution.py:313
  29.0 2.4 %collective-permute-done.7.t1 = bf16[208,128]{1,0:T(8,128)(2,1)S(1)} collective-permute-done((bf16[208,128]{1,0:T(8,128)(2,1)S(1)}, bf16[208,128]{1,0:T(8,128)(2,1)S(1)}, u32[]{:S(2)}, u32[]{:S(2)}) %collective-permute-start.7) | collective-permute-done | bytes 53280 | tf_op jit(solution)/shard_map/ppermute | solution.py:313
  31.4 0.0 collective-permute-start.9
  31.4 0.6 shard_map.66
  32.0 0.0 collective-permute-done.8.t2
  32.0 2.4 %collective-permute-done.9.t3 = bf16[208,128]{1,0:T(8,128)(2,1)S(1)} collective-permute-done((bf16[208,128]{1,0:T(8,128)(2,1)S(1)}, bf16[208,128]{1,0:T(8,128)(2,1)S(1)}, u32[]{:S(2)}, u32[]{:S(2)}) %collective-permute-start.9) | collective-permute-done | bytes 53280 | tf_op jit(solution)/shard_map/ppermute | solution.py:313
  34.4 3.8 %shard_map.67.mesa = f32[128,512]{1,0:T(8,128)S(1)} custom-call(bf16[2,512,128]{2,1,0:T(8,128)(2,1)S(1)} %get-tuple-element.28.kv, f32[8,256]{1,0:T(8,128)S(1)} %get-tuple-element.29.gates, f32[256,128]{1,0:T(8,128)S(1)} %get-tuple-element.30.first, f32[208,128]{1,0:T(8,128)S(1)} %get-tuple-element.32.state, f32[8,128]{1,0:T(8,128)S(1)} %get-tuple-element.33.lead, ...), custom_call_target="tpu_custom_call" | custom-call | flops 1073741824 | bytes 1048576 | tf_op jit(solution)/shard_map/pallas_call | solution.py:33
  38.2 0.0 copy-start
  38.2 0.0 collective-permute-done.2.near
  38.2 0.0 collective-permute-done.3.far
  38.2 1.6 %shard_map.68 = (bf16[128,128]{1,0:T(8,128)(2,1)S(1)}, bf16[128,128]{1,0:T(8,128)(2,1)S(1)}, bf16[128,128]{1,0:T(8,128)(2,1)S(1)}, bf16[128,128]{1,0:T(8,128)(2,1)S(1)}) custom-call(bf16[512,128]{1,0:T(8,128)(2,1)S(1)} %get-tuple-element.27.q, bf16[2,512,128]{2,1,0:T(8,128)(2,1)S(1)} %get-tuple-element.28.kv, ...), custom_call_target="tpu_custom_call" | custom-call | flops 536870912 | bytes 1048576 | tf_op jit(solution)/shard_map/pallas_call | solution.py:33
  39.8 3.3 %collective-permute-start.10 = (bf16[128,128]{1,0:T(8,128)(2,1)S(1)}, bf16[128,128]{1,0:T(8,128)(2,1)S(1)}, u32[]{:S(2)}, u32[]{:S(2)}) collective-permute-start(bf16[128,128]{1,0:T(8,128)(2,1)S(1)} %get-tuple-element.42), channel_id=1, source_target_pairs={{0,8},{1,9},{2,10},{3,11},{4,12},{5,13},{6,14},{7,15},{8,0},{9,1},... | collective-permute-start | bytes 98312 | tf_op jit(solution)/shard_map/ppermute | solution.py:318
  43.2 1.2 %collective-permute-start.11 = (bf16[128,128]{1,0:T(8,128)(2,1)S(1)}, bf16[128,128]{1,0:T(8,128)(2,1)S(1)}, u32[]{:S(2)}, u32[]{:S(2)}) collective-permute-start(bf16[128,128]{1,0:T(8,128)(2,1)S(1)} %get-tuple-element.43), channel_id=1, source_target_pairs={{0,1},{1,0},{2,3},{3,2},{4,5},{5,4},{6,7},{7,6},{8,9},{9,8},{10,11... | collective-permute-start | bytes 98312 | tf_op jit(solution)/shard_map/ppermute | solution.py:318
  44.3 0.6 collective-permute-start.12
  44.9 0.0 collective-permute-done.10.from_c
  44.9 1.0 %collective-permute-done.11.from_z = bf16[128,128]{1,0:T(8,128)(2,1)S(1)} collective-permute-done((bf16[128,128]{1,0:T(8,128)(2,1)S(1)}, bf16[128,128]{1,0:T(8,128)(2,1)S(1)}, u32[]{:S(2)}, u32[]{:S(2)}) %collective-permute-start.11) | collective-permute-done | bytes 32800 | tf_op jit(solution)/shard_map/ppermute | solution.py:318
  45.9 1.8 %collective-permute-done.12.from_cz = bf16[128,128]{1,0:T(8,128)(2,1)S(1)} collective-permute-done((bf16[128,128]{1,0:T(8,128)(2,1)S(1)}, bf16[128,128]{1,0:T(8,128)(2,1)S(1)}, u32[]{:S(2)}, u32[]{:S(2)}) %collective-permute-start.12) | collective-permute-done | bytes 32800 | tf_op jit(solution)/shard_map/ppermute | solution.py:318
  47.7 0.0 collective-permute-done.13.pair_weight
  47.7 0.0 copy-done
  47.7 0.4 shard_map.69
  48.2 5.2 %collective-permute-start.14 = (bf16[32,2048]{1,0:T(8,128)(2,1)S(1)}, bf16[32,2048]{1,0:T(8,128)(2,1)S(1)}, u32[]{:S(2)}, u32[]{:S(2)}) collective-permute-start(bf16[32,2048]{1,0:T(8,128)(2,1)S(1)} %get-tuple-element.46), channel_id=1, source_target_pairs={{0,5},{1,4},{2,7},{3,6},{4,1},{5,0},{6,3},{7,2},{8,13},{9,12},{10,... | collective-permute-start | bytes 393224 | tf_op jit(solution)/shard_map/ppermute | solution.py:418
  53.4 0.3 collective-permute-start.15
  53.6 2.9 %collective-permute-start.16 = (bf16[32,2048]{1,0:T(8,128)(2,1)S(1)}, bf16[32,2048]{1,0:T(8,128)(2,1)S(1)}, u32[]{:S(2)}, u32[]{:S(2)}) collective-permute-start(bf16[32,2048]{1,0:T(8,128)(2,1)S(1)} %get-tuple-element.48), channel_id=1, source_target_pairs={{0,7},{1,2},{2,1},{3,4},{4,3},{5,6},{6,5},{7,0},{8,15},{9,10},{10,... | collective-permute-start | bytes 393224 | tf_op jit(solution)/shard_map/ppermute | solution.py:418
  56.5 0.4 collective-permute-done.14.a
  56.9 6.5 %collective-permute-done.15.b = bf16[32,2048]{1,0:T(8,128)(2,1)S(1)} collective-permute-done((bf16[32,2048]{1,0:T(8,128)(2,1)S(1)}, bf16[32,2048]{1,0:T(8,128)(2,1)S(1)}, u32[]{:S(2)}, u32[]{:S(2)}) %collective-permute-start.15) | collective-permute-done | bytes 131104 | tf_op jit(solution)/shard_map/ppermute | solution.py:418
  63.4 1.4 %collective-permute-done.16.c = bf16[32,2048]{1,0:T(8,128)(2,1)S(1)} collective-permute-done((bf16[32,2048]{1,0:T(8,128)(2,1)S(1)}, bf16[32,2048]{1,0:T(8,128)(2,1)S(1)}, u32[]{:S(2)}, u32[]{:S(2)}) %collective-permute-start.16) | collective-permute-done | bytes 131104 | tf_op jit(solution)/shard_map/ppermute | solution.py:418
  64.8 0.7 %shard_map.70 = bf16[32,2048]{1,0:T(8,128)(2,1)} custom-call(f32[32,2048]{1,0:T(8,128)S(1)} %get-tuple-element.45.mine, bf16[32,2048]{1,0:T(8,128)(2,1)S(1)} %collective-permute-done.14.a, bf16[32,2048]{1,0:T(8,128)(2,1)S(1)} %collective-permute-done.15.b, bf16[32,2048]{1,0:T(8,128)(2,1)S(1)} %collective-permute-done.16.c), custom_call_target="tpu_custom_call" | custom-call | flops 262144 | bytes 1048576 | tf_op jit(solution)/shard_map/pallas_call | solution.py:33
  (6 shorter events, 0.1 us)
Async XLA Ops:
  0.0 3.5 %copy-start.1 = (bf16[256,2,128]{2,1,0:T(2,128)(2,1)S(1)}, bf16[256,2,128]{2,1,0:T(2,128)(2,1)}, u32[]{:S(2)}) copy-start(bf16[256,2,128]{2,1,0:T(2,128)(2,1)} %param.6) | copy-start | bytes 393220
  0.0 47.7 %collective-permute-start.13 = (bf16[256,2048]{1,0:T(8,128)(2,1)}, bf16[256,2048]{1,0:T(8,128)(2,1)S(1)}, u32[]{:S(2)}, u32[]{:S(2)}) collective-permute-start(bf16[256,2048]{1,0:T(8,128)(2,1)} %own_weight.1), channel_id=1, source_target_pairs={{0,1},{1,0},{2,3},{3,2},{4,5},{5,4},{6,7},{7,6},{8,9},{9,8},{10,11... | collective-permute-start | bytes 3145736 | tf_op jit(solution)/shard_map/ppermute | solution.py:318
  3.6 1.1 %copy-start.2 = (f32[2,256]{1,0:T(2,128)S(1)}, f32[2,256]{1,0:T(2,128)}, u32[]{:S(2)}) copy-start(f32[2,256]{1,0:T(2,128)} %param.9) | copy-start | bytes 6148
  3.6 1.1 %copy-start.3 = (f32[2,256]{1,0:T(2,128)S(1)}, f32[2,256]{1,0:T(2,128)}, u32[]{:S(2)}) copy-start(f32[2,256]{1,0:T(2,128)} %param.10) | copy-start | bytes 6148
  3.6 2.6 %collective-permute-start = (bf16[3,256,128]{2,1,0:T(8,128)(2,1)S(1)}, bf16[3,256,128]{2,1,0:T(8,128)(2,1)S(1)}, u32[]{:S(2)}, u32[]{:S(2)}) collective-permute-start(bf16[3,256,128]{2,1,0:T(8,128)(2,1)S(1)} %get-tuple-element.49), channel_id=1, source_target_pairs={{0,8},{1,9},{2,10},{3,11},{4,12},{5,13},{6,14},{7,15},{8,0},{9,1},... | collective-permute-start | bytes 589832 | tf_op jit(solution)/shard_map/ppermute | solution.py:318
  4.7 1.5 %collective-permute-start.1 = (f32[2,256]{1,0:T(2,128)S(1)}, f32[2,256]{1,0:T(2,128)S(1)}, u32[]{:S(2)}, u32[]{:S(2)}) collective-permute-start(f32[2,256]{1,0:T(2,128)S(1)} %get-tuple-element.51), channel_id=1, source_target_pairs={{0,8},{1,9},{2,10},{3,11},{4,12},{5,13},{6,14},{7,15},{8,0},{9,1},... | collective-permute-start | bytes 6152 | tf_op jit(solution)/shard_map/ppermute | solution.py:318
  7.0 6.6 %collective-permute-start.4 = (bf16[208,128]{1,0:T(8,128)(2,1)S(1)}, bf16[208,128]{1,0:T(8,128)(2,1)S(1)}, u32[]{:S(2)}, u32[]{:S(2)}) collective-permute-start(bf16[208,128]{1,0:T(8,128)(2,1)S(1)} %get-tuple-element.31.own), channel_id=1, source_target_pairs={{0,16},{16,32},{32,48},{48,0},{1,17},{17,33},{33,49},{49,1},{2,18}... | collective-permute-start | bytes 159752 | tf_op jit(solution)/shard_map/ppermute | solution.py:313
  8.4 29.9 %collective-permute-start.2 = (bf16[2,512,128]{2,1,0:T(8,128)(2,1)S(1)}, bf16[2,512,128]{2,1,0:T(8,128)(2,1)S(1)}, u32[]{:S(2)}, u32[]{:S(2)}) collective-permute-start(bf16[2,512,128]{2,1,0:T(8,128)(2,1)S(1)} %get-tuple-element.28.kv), channel_id=1, source_target_pairs={{0,16},{16,32},{32,48},{48,64},{64,80},{80,96},{96,112},{112,128},... | collective-permute-start | bytes 786440 | tf_op jit(solution)/shard_map/ppermute | solution.py:309
  9.7 28.6 %collective-permute-start.3 = (bf16[2,512,128]{2,1,0:T(8,128)(2,1)S(1)}, bf16[2,512,128]{2,1,0:T(8,128)(2,1)S(1)}, u32[]{:S(2)}, u32[]{:S(2)}) collective-permute-start(bf16[2,512,128]{2,1,0:T(8,128)(2,1)S(1)} %get-tuple-element.28.kv), channel_id=1, source_target_pairs={{0,32},{16,48},{32,64},{48,80},{64,96},{80,112},{96,128},{112,144}... | collective-permute-start | bytes 786440 | tf_op jit(solution)/shard_map/ppermute | solution.py:309
  11.1 15.3 %collective-permute-start.5 = (bf16[208,128]{1,0:T(8,128)(2,1)S(1)}, bf16[208,128]{1,0:T(8,128)(2,1)S(1)}, u32[]{:S(2)}, u32[]{:S(2)}) collective-permute-start(bf16[208,128]{1,0:T(8,128)(2,1)S(1)} %get-tuple-element.31.own), channel_id=1, source_target_pairs={{0,32},{16,48},{32,0},{48,16},{1,33},{17,49},{33,1},{49,17},{2,34}... | collective-permute-start | bytes 159752 | tf_op jit(solution)/shard_map/ppermute | solution.py:313
  13.6 12.9 %collective-permute-start.6 = (bf16[208,128]{1,0:T(8,128)(2,1)S(1)}, bf16[208,128]{1,0:T(8,128)(2,1)S(1)}, u32[]{:S(2)}, u32[]{:S(2)}) collective-permute-start(bf16[208,128]{1,0:T(8,128)(2,1)S(1)} %get-tuple-element.31.own), channel_id=1, source_target_pairs={{0,48},{16,0},{32,16},{48,32},{1,49},{17,1},{33,17},{49,33},{2,50}... | collective-permute-start | bytes 159752 | tf_op jit(solution)/shard_map/ppermute | solution.py:313
  26.6 4.8 %collective-permute-start.7 = (bf16[208,128]{1,0:T(8,128)(2,1)S(1)}, bf16[208,128]{1,0:T(8,128)(2,1)S(1)}, u32[]{:S(2)}, u32[]{:S(2)}) collective-permute-start(bf16[208,128]{1,0:T(8,128)(2,1)S(1)} %get-tuple-element.40), channel_id=1, source_target_pairs={{0,64},{64,128},{128,192},{192,0},{1,65},{65,129},{129,193},{193,1... | collective-permute-start | bytes 159752 | tf_op jit(solution)/shard_map/ppermute | solution.py:313
  26.6 5.4 %collective-permute-start.8 = (bf16[208,128]{1,0:T(8,128)(2,1)S(1)}, bf16[208,128]{1,0:T(8,128)(2,1)S(1)}, u32[]{:S(2)}, u32[]{:S(2)}) collective-permute-start(bf16[208,128]{1,0:T(8,128)(2,1)S(1)} %get-tuple-element.40), channel_id=1, source_target_pairs={{0,128},{64,192},{128,0},{192,64},{1,129},{65,193},{129,1},{193,65... | collective-permute-start | bytes 159752 | tf_op jit(solution)/shard_map/ppermute | solution.py:313
  31.4 3.0 %collective-permute-start.9 = (bf16[208,128]{1,0:T(8,128)(2,1)S(1)}, bf16[208,128]{1,0:T(8,128)(2,1)S(1)}, u32[]{:S(2)}, u32[]{:S(2)}) collective-permute-start(bf16[208,128]{1,0:T(8,128)(2,1)S(1)} %get-tuple-element.40), channel_id=1, source_target_pairs={{0,192},{64,0},{128,64},{192,128},{1,193},{65,1},{129,65},{193,129... | collective-permute-start | bytes 159752 | tf_op jit(solution)/shard_map/ppermute | solution.py:313
  38.2 9.5 %copy-start = (bf16[256,2048]{1,0:T(8,128)(2,1)S(1)}, bf16[256,2048]{1,0:T(8,128)(2,1)}, u32[]{:S(2)}) copy-start(bf16[256,2048]{1,0:T(8,128)(2,1)} %own_weight.1) | copy-start | bytes 3145732
  39.8 5.1 %collective-permute-start.10 = (bf16[128,128]{1,0:T(8,128)(2,1)S(1)}, bf16[128,128]{1,0:T(8,128)(2,1)S(1)}, u32[]{:S(2)}, u32[]{:S(2)}) collective-permute-start(bf16[128,128]{1,0:T(8,128)(2,1)S(1)} %get-tuple-element.42), channel_id=1, source_target_pairs={{0,8},{1,9},{2,10},{3,11},{4,12},{5,13},{6,14},{7,15},{8,0},{9,1},... | collective-permute-start | bytes 98312 | tf_op jit(solution)/shard_map/ppermute | solution.py:318
  43.2 2.8 %collective-permute-start.11 = (bf16[128,128]{1,0:T(8,128)(2,1)S(1)}, bf16[128,128]{1,0:T(8,128)(2,1)S(1)}, u32[]{:S(2)}, u32[]{:S(2)}) collective-permute-start(bf16[128,128]{1,0:T(8,128)(2,1)S(1)} %get-tuple-element.43), channel_id=1, source_target_pairs={{0,1},{1,0},{2,3},{3,2},{4,5},{5,4},{6,7},{7,6},{8,9},{9,8},{10,11... | collective-permute-start | bytes 98312 | tf_op jit(solution)/shard_map/ppermute | solution.py:318
  44.3 3.4 %collective-permute-start.12 = (bf16[128,128]{1,0:T(8,128)(2,1)S(1)}, bf16[128,128]{1,0:T(8,128)(2,1)S(1)}, u32[]{:S(2)}, u32[]{:S(2)}) collective-permute-start(bf16[128,128]{1,0:T(8,128)(2,1)S(1)} %get-tuple-element.44), channel_id=1, source_target_pairs={{0,9},{1,8},{2,11},{3,10},{4,13},{5,12},{6,15},{7,14},{8,1},{9,0},... | collective-permute-start | bytes 98312 | tf_op jit(solution)/shard_map/ppermute | solution.py:318
  48.2 8.7 %collective-permute-start.14 = (bf16[32,2048]{1,0:T(8,128)(2,1)S(1)}, bf16[32,2048]{1,0:T(8,128)(2,1)S(1)}, u32[]{:S(2)}, u32[]{:S(2)}) collective-permute-start(bf16[32,2048]{1,0:T(8,128)(2,1)S(1)} %get-tuple-element.46), channel_id=1, source_target_pairs={{0,5},{1,4},{2,7},{3,6},{4,1},{5,0},{6,3},{7,2},{8,13},{9,12},{10,... | collective-permute-start | bytes 393224 | tf_op jit(solution)/shard_map/ppermute | solution.py:418
  53.4 10.0 %collective-permute-start.15 = (bf16[32,2048]{1,0:T(8,128)(2,1)S(1)}, bf16[32,2048]{1,0:T(8,128)(2,1)S(1)}, u32[]{:S(2)}, u32[]{:S(2)}) collective-permute-start(bf16[32,2048]{1,0:T(8,128)(2,1)S(1)} %get-tuple-element.47), channel_id=1, source_target_pairs={{0,6},{1,3},{2,0},{3,5},{4,2},{5,7},{6,4},{7,1},{8,14},{9,11},{10,... | collective-permute-start | bytes 393224 | tf_op jit(solution)/shard_map/ppermute | solution.py:418
  53.6 11.2 %collective-permute-start.16 = (bf16[32,2048]{1,0:T(8,128)(2,1)S(1)}, bf16[32,2048]{1,0:T(8,128)(2,1)S(1)}, u32[]{:S(2)}, u32[]{:S(2)}) collective-permute-start(bf16[32,2048]{1,0:T(8,128)(2,1)S(1)} %get-tuple-element.48), channel_id=1, source_target_pairs={{0,7},{1,2},{2,1},{3,4},{4,3},{5,6},{6,5},{7,0},{8,15},{9,10},{10,... | collective-permute-start | bytes 393224 | tf_op jit(solution)/shard_map/ppermute | solution.py:418

commit v7 on v6

--- a/solution.py
+++ b/solution.py
@@ -225,44 +225,63 @@
         out[:, j * HALF : (j + 1) * HALF] = products(j, xs[j], mix_v[j], values_t[j])
 
 
-def attend_body(q, kv, near, far, mesa, keep_out, c_out, z_out, cz_out, place):
+def products_of(parts, qj, largest, total, result):
+    scale = E ** (-0.5)
+    scores = []
+    for keys, _, mask in parts:
+        s = lax.dot_general(keys, qj, (((1,), (1,)), ((), ())), preferred_element_type=f32)
+        scores.append(s if mask is None else jnp.where(mask, s, LOW))
+    top = scores[0]
+    for s in scores[1:]:
+        top = jnp.maximum(top, s)
+    top = jnp.max(top, axis=0, keepdims=True)
+    if largest is not None:
+        top = jnp.maximum(top, largest)
+        shrink = jnp.exp((largest - top) * scale)
+        total, result = total * shrink, result * shrink
+    for (_, values_t, _), s in zip(parts, scores):
+        expo = jnp.exp((s - top) * scale)
+        total = total + jnp.sum(expo, axis=0, keepdims=True)
+        result = result + dot(values_t, expo.astype(bf16))
+    return top, total, result
+
+
+def blocks_of(source):
+    rows = [slice(half * HALF, (half + 1) * HALF) for half in range(2)]
+    return [(source[0, r, :], jnp.transpose(source[1, r, :].astype(f32)).astype(bf16)) for r in rows]
+
+
+def attend_a_body(q, kv, far, rows_out, result_out):
+    chip = lax.axis_index("x") * 4 + lax.axis_index("y")
+    row, col = iotas((HALF, HALF))
+    old, own = blocks_of(far), blocks_of(kv)
+    held = chip >= 2
+    lines = []
+    for j in range(2):
+        parts = [(*old[j], (row > col) & held)]
+        if j == 0:
+            parts.append((*old[1], held))
+        else:
+            parts.append((*own[0], None))
+        parts.append((*own[j], row <= col))
+        at = slice(j * HALF, (j + 1) * HALF)
+        top, total, result = products_of(
+            parts, q[at, :], None, jnp.zeros((1, HALF), f32), jnp.zeros((E, HALF), f32)
+        )
+        lines += [top, total]
+        result_out[:, at] = result
+    rows_out[...] = jnp.concatenate((*lines, jnp.zeros((4, HALF), f32)), axis=0)
+
+
+def attend_body(q, near, rows, first, mesa, keep_out, c_out, z_out, cz_out, place):
     core = lax.axis_index("c")
-    chip = lax.axis_index("x") * 4 + lax.axis_index("y")
-    scale = E ** (-0.5)
-    row, col = iotas((HALF, HALF))
-    parts = [(far, 0, 2), (far, 1, 2), (near, 0, 1), (near, 1, 1), (kv, 0, 0), (kv, 1, 0)]
-
-    def rows_of(b, which):
-        source, half, _ = parts[b]
-        return source[which, half * HALF : (half + 1) * HALF, :]
-
-    values_t = [jnp.transpose(rows_of(b, 1).astype(f32)).astype(bf16) for b in range(6)]
-    for j in range(2):
-        own = slice(j * HALF, (j + 1) * HALF)
-        qj = q[own, :]
-        scores = []
-        for b in range(j, j + 5):
-            s = lax.dot_general(
-                rows_of(b, 0), qj, (((1,), (1,)), ((), ())), preferred_element_type=f32
-            )
-            if b == j:
-                s = jnp.where(row > col, s, LOW)
-            if b == j + 4:
-                s = jnp.where(row <= col, s, LOW)
-            if parts[b][2]:
-                s = jnp.where(chip >= parts[b][2], s, LOW)
-            scores.append(s)
-        largest = scores[0]
-        for s in scores[1:]:
-            largest = jnp.maximum(largest, s)
-        largest = jnp.max(largest, axis=0, keepdims=True)
-        total = jnp.zeros((1, HALF), f32)
-        result = jnp.zeros((E, HALF), f32)
-        for b, s in zip(range(j, j + 5), scores):
-            expo = jnp.exp((s - largest) * scale)
-            total = total + jnp.sum(expo, axis=0, keepdims=True)
-            result = result + dot(values_t[b], expo.astype(bf16))
-        both = jnp.transpose(result / total + mesa[:, own]).astype(bf16)
+    held = lax.axis_index("x") * 4 + lax.axis_index("y") >= 1
+    parts = [(*block, held) for block in blocks_of(near)]
+    for j in range(2):
+        at = slice(j * HALF, (j + 1) * HALF)
+        top, total = rows[2 * j : 2 * j + 1, :], rows[2 * j + 1 : 2 * j + 2, :]
+        _, total, result = products_of(parts, q[at, :], top, total, first[:, at])
+        both = jnp.transpose(result / total + mesa[:, at]).astype(bf16)
         for slot in range(SLOTS):
             place[SLOTS * j + slot] = both[slot * SLOT : (slot + 1) * SLOT]
 
@@ -387,14 +406,16 @@
         *prepared,
         *around_x,
     )
+    near, far = halos
+    partial = call(attend_a_body, [((8, HALF), f32), ((E, CHIP), f32)], [], 1 << 28, q, kv, far)
     kept, to_c, to_z, to_cz = call(
         attend_body,
         [((HALF // 2, E), bf16)] * 4,
         [((2 * SLOTS, SLOT, E), bf16)],
         1 << 29,
         q,
-        kv,
-        *halos,
+        near,
+        *partial,
         mesa,
     )
     from_cz = across(to_cz, 1, 1)

time: 65.6 us -> 60.9 us (0.928)
  waiting for transfers between devices: 28.2 us -> 23.8 us
  starting transfers between devices: 28 us -> 27.1 us
    ppermute x6, waiting for transfers between devices: 16.2 us -> 11.8 us  [turned(): return lax.ppermute(x, axis, [(i, (i + by) % 4) for i in range(4)])]
    ppermute x6, starting transfers between devices: 7.71 us -> 6.52 us  [turned(): return lax.ppermute(x, axis, [(i, (i + by) % 4) for i in range(4)])]
    pallas_call x7 -> x8, Pallas kernels: 8.08 us -> 8.63 us  [call(): pl.pallas_call(body, out_shape=[jax.ShapeDtypeStruct(shape, kind) for sha...]
  transfers between devices with their start and end apart: 17 -> 17, of which waited for: 9 -> 9; matrix products, arithmetic and copies ran while one was open for 2% -> 2% of each run, Pallas kernels for 11% -> 12%
where the time goes in v7:
time: 60.9 us; the launch traced here: 60.8 us
  starting transfers between devices  27.1 us (44%)
  waiting for transfers between devices  23.8 us (39%)
  Pallas kernels  8.63 us (14%)
  local copies, waits for them, and re-layouts  1.05 us (2%)
    ppermute x6, waiting for transfers between devices, turned(): return lax.ppermute(x, axis, [(i, (i + by) % 4) for i in range(4)])  11.8 us
    ppermute x6, starting transfers between devices, across(): return lax.ppermute(x, ('c', 'z'), pairs)  8.86 us
    pallas_call x8, Pallas kernels, call(): pl.pallas_call(body, out_shape=[jax.ShapeDtypeStruct(shape, kind) for sha...  8.63 us
    ppermute x3, starting transfers between devices, on_device(): got.append(lax.ppermute(share, 'z', pairs))  8.33 us
    ppermute x3, waiting for transfers between devices, on_device(): got.append(lax.ppermute(share, 'z', pairs))  8.28 us
    ppermute x6, starting transfers between devices, turned(): return lax.ppermute(x, axis, [(i, (i + by) % 4) for i in range(4)])  6.52 us
    ppermute x6, waiting for transfers between devices, across(): return lax.ppermute(x, ('c', 'z'), pairs)  3.65 us
    ppermute x2, starting transfers between devices, beyond(): return lax.ppermute(x, XY, [(i, (i + by) % 16) for i in range(16)])  3.37 us
  transfers between devices with their start and end apart: 17, of which 9 were waited for; matrix products, arithmetic and copies ran while one was open for 2% of the time, Pallas kernels for 12%

profile of v7, /device:TPU:1, one launch (start us, length us, event | category | flops | bytes accessed | tf_op | source)
XLA Modules:
  0.0 60.8 jit_solution(13700058810775582926)
XLA Ops:
  0.0 0.0 copy-start.1
  0.0 2.5 %collective-permute-start.13 = (bf16[256,2048]{1,0:T(8,128)(2,1)}, bf16[256,2048]{1,0:T(8,128)(2,1)S(1)}, u32[]{:S(2)}, u32[]{:S(2)}) collective-permute-start(bf16[256,2048]{1,0:T(8,128)(2,1)} %own_weight.1), channel_id=1, source_target_pairs={{0,1},{1,0},{2,3},{3,2},{4,5},{5,4},{6,7},{7,6},{8,9},{9,8},{10,11... | collective-permute-start | bytes 3145736 | tf_op jit(solution)/shard_map/ppermute | solution.py:337
  2.5 1.0 %copy_bitcast_fusion = (bf16[1,256,2,128]{3,1,0,2:T(8,128)(2,1)S(1)}, bf16[1,256,2,128]{3,1,0,2:T(8,128)(2,1)S(1)}) fusion(bf16[256,2,128]{2,1,0:T(2,128)(2,1)} %param.8, bf16[256,2,128]{2,1,0:T(2,128)(2,1)} %param.7), kind=kLoop, calls=%fused_computation.3 | loop fusion | bytes 524288 | tf_op jit(solution)/shard_map/stack | solution.py:342
  3.5 0.0 copy-done.1
  3.6 0.0 copy-start.2
  3.6 0.0 copy-start.3
  3.6 1.0 %collective-permute-start = (bf16[3,256,128]{2,1,0:T(8,128)(2,1)S(1)}, bf16[3,256,128]{2,1,0:T(8,128)(2,1)S(1)}, u32[]{:S(2)}, u32[]{:S(2)}) collective-permute-start(bf16[3,256,128]{2,1,0:T(8,128)(2,1)S(1)} %get-tuple-element.53), channel_id=1, source_target_pairs={{0,8},{1,9},{2,10},{3,11},{4,12},{5,13},{6,14},{7,15},{8,0},{9,1},... | collective-permute-start | bytes 589832 | tf_op jit(solution)/shard_map/ppermute | solution.py:337
  4.7 0.0 copy-done.2
  4.7 0.0 copy-done.3
  4.7 0.7 %collective-permute-start.1 = (f32[2,256]{1,0:T(2,128)S(1)}, f32[2,256]{1,0:T(2,128)S(1)}, u32[]{:S(2)}, u32[]{:S(2)}) collective-permute-start(f32[2,256]{1,0:T(2,128)S(1)} %get-tuple-element.55), channel_id=1, source_target_pairs={{0,8},{1,9},{2,10},{3,11},{4,12},{5,13},{6,14},{7,15},{8,0},{9,1},... | collective-permute-start | bytes 6152 | tf_op jit(solution)/shard_map/ppermute | solution.py:337
  5.4 0.8 %collective-permute-done.1.gate_recv = f32[2,256]{1,0:T(2,128)S(1)} collective-permute-done((f32[2,256]{1,0:T(2,128)S(1)}, f32[2,256]{1,0:T(2,128)S(1)}, u32[]{:S(2)}, u32[]{:S(2)}) %collective-permute-start.1) | collective-permute-done | bytes 2080 | tf_op jit(solution)/shard_map/ppermute | solution.py:337
  6.2 0.0 collective-permute-done.recv
  6.2 0.8 %shard_map.64 = (bf16[512,128]{1,0:T(8,128)(2,1)S(1)}, bf16[2,512,128]{2,1,0:T(8,128)(2,1)S(1)}, f32[8,256]{1,0:T(8,128)S(1)}, bf16[208,128]{1,0:T(8,128)(2,1)S(1)}, f32[256,128]{1,0:T(8,128)S(1)}) custom-call(bf16[3,256,128]{2,1,0:T(8,128)(2,1)S(1)} %get-tuple-element.54.keep, bf16[3,256,128]{2,1,0:T(8,128)(2,1)S(1)} %collective-permute-done.recv, ...), custom_call_target="tpu_custom_call" | custom-call | flops 67108864 | bytes 1048576 | tf_op jit(solution)/shard_map/pallas_call | solution.py:33
  7.0 1.4 %collective-permute-start.4 = (bf16[208,128]{1,0:T(8,128)(2,1)S(1)}, bf16[208,128]{1,0:T(8,128)(2,1)S(1)}, u32[]{:S(2)}, u32[]{:S(2)}) collective-permute-start(bf16[208,128]{1,0:T(8,128)(2,1)S(1)} %get-tuple-element.35.own), channel_id=1, source_target_pairs={{0,16},{16,32},{32,48},{48,0},{1,17},{17,33},{33,49},{49,1},{2,18}... | collective-permute-start | bytes 159752 | tf_op jit(solution)/shard_map/ppermute | solution.py:332
  8.4 2.6 %collective-permute-start.3 = (bf16[2,512,128]{2,1,0:T(8,128)(2,1)S(1)}, bf16[2,512,128]{2,1,0:T(8,128)(2,1)S(1)}, u32[]{:S(2)}, u32[]{:S(2)}) collective-permute-start(bf16[2,512,128]{2,1,0:T(8,128)(2,1)S(1)} %get-tuple-element.30.kv), channel_id=1, source_target_pairs={{0,32},{16,48},{32,64},{48,80},{64,96},{80,112},{96,128},{112,144}... | collective-permute-start | bytes 786440 | tf_op jit(solution)/shard_map/ppermute | solution.py:328
  11.0 1.3 %collective-permute-start.5 = (bf16[208,128]{1,0:T(8,128)(2,1)S(1)}, bf16[208,128]{1,0:T(8,128)(2,1)S(1)}, u32[]{:S(2)}, u32[]{:S(2)}) collective-permute-start(bf16[208,128]{1,0:T(8,128)(2,1)S(1)} %get-tuple-element.35.own), channel_id=1, source_target_pairs={{0,32},{16,48},{32,0},{48,16},{1,33},{17,49},{33,1},{49,17},{2,34}... | collective-permute-start | bytes 159752 | tf_op jit(solution)/shard_map/ppermute | solution.py:332
  12.3 0.7 %collective-permute-start.6 = (bf16[208,128]{1,0:T(8,128)(2,1)S(1)}, bf16[208,128]{1,0:T(8,128)(2,1)S(1)}, u32[]{:S(2)}, u32[]{:S(2)}) collective-permute-start(bf16[208,128]{1,0:T(8,128)(2,1)S(1)} %get-tuple-element.35.own), channel_id=1, source_target_pairs={{0,48},{16,0},{32,16},{48,32},{1,49},{17,1},{33,17},{49,33},{2,50}... | collective-permute-start | bytes 159752 | tf_op jit(solution)/shard_map/ppermute | solution.py:332
  13.0 0.0 collective-permute-done.4.r1
  13.0 0.7 %collective-permute-start.2 = (bf16[2,512,128]{2,1,0:T(8,128)(2,1)S(1)}, bf16[2,512,128]{2,1,0:T(8,128)(2,1)S(1)}, u32[]{:S(2)}, u32[]{:S(2)}) collective-permute-start(bf16[2,512,128]{2,1,0:T(8,128)(2,1)S(1)} %get-tuple-element.30.kv), channel_id=1, source_target_pairs={{0,16},{16,32},{32,48},{48,64},{64,80},{80,96},{96,112},{112,128},... | collective-permute-start | bytes 786440 | tf_op jit(solution)/shard_map/ppermute | solution.py:328
  13.7 8.0 %collective-permute-done.5.r2 = bf16[208,128]{1,0:T(8,128)(2,1)S(1)} collective-permute-done((bf16[208,128]{1,0:T(8,128)(2,1)S(1)}, bf16[208,128]{1,0:T(8,128)(2,1)S(1)}, u32[]{:S(2)}, u32[]{:S(2)}) %collective-permute-start.5) | collective-permute-done | bytes 53280 | tf_op jit(solution)/shard_map/ppermute | solution.py:332
  21.8 0.0 collective-permute-done.6.r3
  21.8 0.1 shard_map.66
  21.9 0.4 collective-permute-start.7
  22.3 2.4 %collective-permute-start.8 = (bf16[208,128]{1,0:T(8,128)(2,1)S(1)}, bf16[208,128]{1,0:T(8,128)(2,1)S(1)}, u32[]{:S(2)}, u32[]{:S(2)}) collective-permute-start(bf16[208,128]{1,0:T(8,128)(2,1)S(1)} %get-tuple-element.44), channel_id=1, source_target_pairs={{0,128},{64,192},{128,0},{192,64},{1,129},{65,193},{129,1},{193,65... | collective-permute-start | bytes 159752 | tf_op jit(solution)/shard_map/ppermute | solution.py:332
  24.7 1.8 %collective-permute-done.7.t1 = bf16[208,128]{1,0:T(8,128)(2,1)S(1)} collective-permute-done((bf16[208,128]{1,0:T(8,128)(2,1)S(1)}, bf16[208,128]{1,0:T(8,128)(2,1)S(1)}, u32[]{:S(2)}, u32[]{:S(2)}) %collective-permute-start.7) | collective-permute-done | bytes 53280 | tf_op jit(solution)/shard_map/ppermute | solution.py:332
  26.5 0.3 collective-permute-start.9
  26.8 0.6 shard_map.67
  27.4 0.0 collective-permute-done.8.t2
  27.4 2.0 %collective-permute-done.9.t3 = bf16[208,128]{1,0:T(8,128)(2,1)S(1)} collective-permute-done((bf16[208,128]{1,0:T(8,128)(2,1)S(1)}, bf16[208,128]{1,0:T(8,128)(2,1)S(1)}, u32[]{:S(2)}, u32[]{:S(2)}) %collective-permute-start.9) | collective-permute-done | bytes 53280 | tf_op jit(solution)/shard_map/ppermute | solution.py:332
  29.5 3.8 %shard_map.68.mesa = f32[128,512]{1,0:T(8,128)S(1)} custom-call(bf16[2,512,128]{2,1,0:T(8,128)(2,1)S(1)} %get-tuple-element.30.kv, f32[8,256]{1,0:T(8,128)S(1)} %get-tuple-element.33.gates, f32[256,128]{1,0:T(8,128)S(1)} %get-tuple-element.34.first, f32[208,128]{1,0:T(8,128)S(1)} %get-tuple-element.36.state, f32[8,128]{1,0:T(8,128)S(1)} %get-tuple-element.37.lead, ...), custom_call_target="tpu_custom_call" | custom-call | flops 1073741824 | bytes 1048576 | tf_op jit(solution)/shard_map/pallas_call | solution.py:33
  33.3 0.0 collective-permute-done.3.far
  33.3 1.1 %shard_map.65 = (f32[8,256]{1,0:T(8,128)S(1)}, f32[128,512]{1,0:T(8,128)S(1)}) custom-call(bf16[512,128]{1,0:T(8,128)(2,1)S(1)} %get-tuple-element.29.q, bf16[2,512,128]{2,1,0:T(8,128)(2,1)S(1)} %get-tuple-element.30.kv, bf16[2,512,128]{2,1,0:T(8,128)(2,1)S(1)} %collective-permute-done.3.far), custom_call_target="tpu_custom_call" | custom-call | flops 268435456 | bytes 1048576 | tf_op jit(solution)/shard_map/pallas_call | solution.py:33
  34.4 0.0 copy-start
  34.4 0.0 collective-permute-done.2.near
  34.4 1.0 %shard_map.69 = (bf16[128,128]{1,0:T(8,128)(2,1)S(1)}, bf16[128,128]{1,0:T(8,128)(2,1)S(1)}, bf16[128,128]{1,0:T(8,128)(2,1)S(1)}, bf16[128,128]{1,0:T(8,128)(2,1)S(1)}) custom-call(bf16[512,128]{1,0:T(8,128)(2,1)S(1)} %get-tuple-element.29.q, bf16[2,512,128]{2,1,0:T(8,128)(2,1)S(1)} %collective-permute-done.2.near, f32[8,256]{1,0:T(8,128)S(1)} %get-tuple-element.31.rows, ...), custom_call_target="tpu_custom_call" | custom-call | flops 536870912 | bytes 1048576 | tf_op jit(solution)/shard_map/pallas_call | solution.py:33
  35.5 3.0 %collective-permute-start.10 = (bf16[128,128]{1,0:T(8,128)(2,1)S(1)}, bf16[128,128]{1,0:T(8,128)(2,1)S(1)}, u32[]{:S(2)}, u32[]{:S(2)}) collective-permute-start(bf16[128,128]{1,0:T(8,128)(2,1)S(1)} %get-tuple-element.46), channel_id=1, source_target_pairs={{0,8},{1,9},{2,10},{3,11},{4,12},{5,13},{6,14},{7,15},{8,0},{9,1},... | collective-permute-start | bytes 98312 | tf_op jit(solution)/shard_map/ppermute | solution.py:337
  38.5 1.2 %collective-permute-start.11 = (bf16[128,128]{1,0:T(8,128)(2,1)S(1)}, bf16[128,128]{1,0:T(8,128)(2,1)S(1)}, u32[]{:S(2)}, u32[]{:S(2)}) collective-permute-start(bf16[128,128]{1,0:T(8,128)(2,1)S(1)} %get-tuple-element.47), channel_id=1, source_target_pairs={{0,1},{1,0},{2,3},{3,2},{4,5},{5,4},{6,7},{7,6},{8,9},{9,8},{10,11... | collective-permute-start | bytes 98312 | tf_op jit(solution)/shard_map/ppermute | solution.py:337
  39.6 0.6 collective-permute-start.12
  40.2 0.0 collective-permute-done.10.from_c
  40.2 1.0 %collective-permute-done.11.from_z = bf16[128,128]{1,0:T(8,128)(2,1)S(1)} collective-permute-done((bf16[128,128]{1,0:T(8,128)(2,1)S(1)}, bf16[128,128]{1,0:T(8,128)(2,1)S(1)}, u32[]{:S(2)}, u32[]{:S(2)}) %collective-permute-start.11) | collective-permute-done | bytes 32800 | tf_op jit(solution)/shard_map/ppermute | solution.py:337
  41.2 1.8 %collective-permute-done.12.from_cz = bf16[128,128]{1,0:T(8,128)(2,1)S(1)} collective-permute-done((bf16[128,128]{1,0:T(8,128)(2,1)S(1)}, bf16[128,128]{1,0:T(8,128)(2,1)S(1)}, u32[]{:S(2)}, u32[]{:S(2)}) %collective-permute-start.12) | collective-permute-done | bytes 32800 | tf_op jit(solution)/shard_map/ppermute | solution.py:337
  43.0 0.0 collective-permute-done.13.pair_weight
  43.0 0.0 copy-done
  43.0 0.4 shard_map.70
  43.5 5.2 %collective-permute-start.14 = (bf16[32,2048]{1,0:T(8,128)(2,1)S(1)}, bf16[32,2048]{1,0:T(8,128)(2,1)S(1)}, u32[]{:S(2)}, u32[]{:S(2)}) collective-permute-start(bf16[32,2048]{1,0:T(8,128)(2,1)S(1)} %get-tuple-element.50), channel_id=1, source_target_pairs={{0,5},{1,4},{2,7},{3,6},{4,1},{5,0},{6,3},{7,2},{8,13},{9,12},{10,... | collective-permute-start | bytes 393224 | tf_op jit(solution)/shard_map/ppermute | solution.py:439
  48.7 0.3 collective-permute-start.15
  48.9 2.9 %collective-permute-start.16 = (bf16[32,2048]{1,0:T(8,128)(2,1)S(1)}, bf16[32,2048]{1,0:T(8,128)(2,1)S(1)}, u32[]{:S(2)}, u32[]{:S(2)}) collective-permute-start(bf16[32,2048]{1,0:T(8,128)(2,1)S(1)} %get-tuple-element.52), channel_id=1, source_target_pairs={{0,7},{1,2},{2,1},{3,4},{4,3},{5,6},{6,5},{7,0},{8,15},{9,10},{10,... | collective-permute-start | bytes 393224 | tf_op jit(solution)/shard_map/ppermute | solution.py:439
  51.8 0.4 collective-permute-done.14.a
  52.2 6.5 %collective-permute-done.15.b = bf16[32,2048]{1,0:T(8,128)(2,1)S(1)} collective-permute-done((bf16[32,2048]{1,0:T(8,128)(2,1)S(1)}, bf16[32,2048]{1,0:T(8,128)(2,1)S(1)}, u32[]{:S(2)}, u32[]{:S(2)}) %collective-permute-start.15) | collective-permute-done | bytes 131104 | tf_op jit(solution)/shard_map/ppermute | solution.py:439
  58.7 1.4 %collective-permute-done.16.c = bf16[32,2048]{1,0:T(8,128)(2,1)S(1)} collective-permute-done((bf16[32,2048]{1,0:T(8,128)(2,1)S(1)}, bf16[32,2048]{1,0:T(8,128)(2,1)S(1)}, u32[]{:S(2)}, u32[]{:S(2)}) %collective-permute-start.16) | collective-permute-done | bytes 131104 | tf_op jit(solution)/shard_map/ppermute | solution.py:439
  60.1 0.7 %shard_map.71 = bf16[32,2048]{1,0:T(8,128)(2,1)} custom-call(f32[32,2048]{1,0:T(8,128)S(1)} %get-tuple-element.49.mine, bf16[32,2048]{1,0:T(8,128)(2,1)S(1)} %collective-permute-done.14.a, bf16[32,2048]{1,0:T(8,128)(2,1)S(1)} %collective-permute-done.15.b, bf16[32,2048]{1,0:T(8,128)(2,1)S(1)} %collective-permute-done.16.c), custom_call_target="tpu_custom_call" | custom-call | flops 262144 | bytes 1048576 | tf_op jit(solution)/shard_map/pallas_call | solution.py:33
  (6 shorter events, 0.1 us)
Async XLA Ops:
  0.0 3.5 %copy-start.1 = (bf16[256,2,128]{2,1,0:T(2,128)(2,1)S(1)}, bf16[256,2,128]{2,1,0:T(2,128)(2,1)}, u32[]{:S(2)}) copy-start(bf16[256,2,128]{2,1,0:T(2,128)(2,1)} %param.6) | copy-start | bytes 393220
  0.0 43.0 %collective-permute-start.13 = (bf16[256,2048]{1,0:T(8,128)(2,1)}, bf16[256,2048]{1,0:T(8,128)(2,1)S(1)}, u32[]{:S(2)}, u32[]{:S(2)}) collective-permute-start(bf16[256,2048]{1,0:T(8,128)(2,1)} %own_weight.1), channel_id=1, source_target_pairs={{0,1},{1,0},{2,3},{3,2},{4,5},{5,4},{6,7},{7,6},{8,9},{9,8},{10,11... | collective-permute-start | bytes 3145736 | tf_op jit(solution)/shard_map/ppermute | solution.py:337
  3.6 1.1 %copy-start.2 = (f32[2,256]{1,0:T(2,128)S(1)}, f32[2,256]{1,0:T(2,128)}, u32[]{:S(2)}) copy-start(f32[2,256]{1,0:T(2,128)} %param.9) | copy-start | bytes 6148
  3.6 1.1 %copy-start.3 = (f32[2,256]{1,0:T(2,128)S(1)}, f32[2,256]{1,0:T(2,128)}, u32[]{:S(2)}) copy-start(f32[2,256]{1,0:T(2,128)} %param.10) | copy-start | bytes 6148
  3.6 2.6 %collective-permute-start = (bf16[3,256,128]{2,1,0:T(8,128)(2,1)S(1)}, bf16[3,256,128]{2,1,0:T(8,128)(2,1)S(1)}, u32[]{:S(2)}, u32[]{:S(2)}) collective-permute-start(bf16[3,256,128]{2,1,0:T(8,128)(2,1)S(1)} %get-tuple-element.53), channel_id=1, source_target_pairs={{0,8},{1,9},{2,10},{3,11},{4,12},{5,13},{6,14},{7,15},{8,0},{9,1},... | collective-permute-start | bytes 589832 | tf_op jit(solution)/shard_map/ppermute | solution.py:337
  4.7 1.5 %collective-permute-start.1 = (f32[2,256]{1,0:T(2,128)S(1)}, f32[2,256]{1,0:T(2,128)S(1)}, u32[]{:S(2)}, u32[]{:S(2)}) collective-permute-start(f32[2,256]{1,0:T(2,128)S(1)} %get-tuple-element.55), channel_id=1, source_target_pairs={{0,8},{1,9},{2,10},{3,11},{4,12},{5,13},{6,14},{7,15},{8,0},{9,1},... | collective-permute-start | bytes 6152 | tf_op jit(solution)/shard_map/ppermute | solution.py:337
  7.0 6.0 %collective-permute-start.4 = (bf16[208,128]{1,0:T(8,128)(2,1)S(1)}, bf16[208,128]{1,0:T(8,128)(2,1)S(1)}, u32[]{:S(2)}, u32[]{:S(2)}) collective-permute-start(bf16[208,128]{1,0:T(8,128)(2,1)S(1)} %get-tuple-element.35.own), channel_id=1, source_target_pairs={{0,16},{16,32},{32,48},{48,0},{1,17},{17,33},{33,49},{49,1},{2,18}... | collective-permute-start | bytes 159752 | tf_op jit(solution)/shard_map/ppermute | solution.py:332
  8.4 24.9 %collective-permute-start.3 = (bf16[2,512,128]{2,1,0:T(8,128)(2,1)S(1)}, bf16[2,512,128]{2,1,0:T(8,128)(2,1)S(1)}, u32[]{:S(2)}, u32[]{:S(2)}) collective-permute-start(bf16[2,512,128]{2,1,0:T(8,128)(2,1)S(1)} %get-tuple-element.30.kv), channel_id=1, source_target_pairs={{0,32},{16,48},{32,64},{48,80},{64,96},{80,112},{96,128},{112,144}... | collective-permute-start | bytes 786440 | tf_op jit(solution)/shard_map/ppermute | solution.py:328
  11.0 10.8 %collective-permute-start.5 = (bf16[208,128]{1,0:T(8,128)(2,1)S(1)}, bf16[208,128]{1,0:T(8,128)(2,1)S(1)}, u32[]{:S(2)}, u32[]{:S(2)}) collective-permute-start(bf16[208,128]{1,0:T(8,128)(2,1)S(1)} %get-tuple-element.35.own), channel_id=1, source_target_pairs={{0,32},{16,48},{32,0},{48,16},{1,33},{17,49},{33,1},{49,17},{2,34}... | collective-permute-start | bytes 159752 | tf_op jit(solution)/shard_map/ppermute | solution.py:332
  12.3 9.5 %collective-permute-start.6 = (bf16[208,128]{1,0:T(8,128)(2,1)S(1)}, bf16[208,128]{1,0:T(8,128)(2,1)S(1)}, u32[]{:S(2)}, u32[]{:S(2)}) collective-permute-start(bf16[208,128]{1,0:T(8,128)(2,1)S(1)} %get-tuple-element.35.own), channel_id=1, source_target_pairs={{0,48},{16,0},{32,16},{48,32},{1,49},{17,1},{33,17},{49,33},{2,50}... | collective-permute-start | bytes 159752 | tf_op jit(solution)/shard_map/ppermute | solution.py:332
  13.0 21.4 %collective-permute-start.2 = (bf16[2,512,128]{2,1,0:T(8,128)(2,1)S(1)}, bf16[2,512,128]{2,1,0:T(8,128)(2,1)S(1)}, u32[]{:S(2)}, u32[]{:S(2)}) collective-permute-start(bf16[2,512,128]{2,1,0:T(8,128)(2,1)S(1)} %get-tuple-element.30.kv), channel_id=1, source_target_pairs={{0,16},{16,32},{32,48},{48,64},{64,80},{80,96},{96,112},{112,128},... | collective-permute-start | bytes 786440 | tf_op jit(solution)/shard_map/ppermute | solution.py:328
  21.9 4.6 %collective-permute-start.7 = (bf16[208,128]{1,0:T(8,128)(2,1)S(1)}, bf16[208,128]{1,0:T(8,128)(2,1)S(1)}, u32[]{:S(2)}, u32[]{:S(2)}) collective-permute-start(bf16[208,128]{1,0:T(8,128)(2,1)S(1)} %get-tuple-element.44), channel_id=1, source_target_pairs={{0,64},{64,128},{128,192},{192,0},{1,65},{65,129},{129,193},{193,1... | collective-permute-start | bytes 159752 | tf_op jit(solution)/shard_map/ppermute | solution.py:332
  22.3 5.1 %collective-permute-start.8 = (bf16[208,128]{1,0:T(8,128)(2,1)S(1)}, bf16[208,128]{1,0:T(8,128)(2,1)S(1)}, u32[]{:S(2)}, u32[]{:S(2)}) collective-permute-start(bf16[208,128]{1,0:T(8,128)(2,1)S(1)} %get-tuple-element.44), channel_id=1, source_target_pairs={{0,128},{64,192},{128,0},{192,64},{1,129},{65,193},{129,1},{193,65... | collective-permute-start | bytes 159752 | tf_op jit(solution)/shard_map/ppermute | solution.py:332
  26.5 3.0 %collective-permute-start.9 = (bf16[208,128]{1,0:T(8,128)(2,1)S(1)}, bf16[208,128]{1,0:T(8,128)(2,1)S(1)}, u32[]{:S(2)}, u32[]{:S(2)}) collective-permute-start(bf16[208,128]{1,0:T(8,128)(2,1)S(1)} %get-tuple-element.44), channel_id=1, source_target_pairs={{0,192},{64,0},{128,64},{192,128},{1,193},{65,1},{129,65},{193,129... | collective-permute-start | bytes 159752 | tf_op jit(solution)/shard_map/ppermute | solution.py:332
  34.4 8.6 %copy-start = (bf16[256,2048]{1,0:T(8,128)(2,1)S(1)}, bf16[256,2048]{1,0:T(8,128)(2,1)}, u32[]{:S(2)}) copy-start(bf16[256,2048]{1,0:T(8,128)(2,1)} %own_weight.1) | copy-start | bytes 3145732
  35.5 4.7 %collective-permute-start.10 = (bf16[128,128]{1,0:T(8,128)(2,1)S(1)}, bf16[128,128]{1,0:T(8,128)(2,1)S(1)}, u32[]{:S(2)}, u32[]{:S(2)}) collective-permute-start(bf16[128,128]{1,0:T(8,128)(2,1)S(1)} %get-tuple-element.46), channel_id=1, source_target_pairs={{0,8},{1,9},{2,10},{3,11},{4,12},{5,13},{6,14},{7,15},{8,0},{9,1},... | collective-permute-start | bytes 98312 | tf_op jit(solution)/shard_map/ppermute | solution.py:337
  38.5 2.8 %collective-permute-start.11 = (bf16[128,128]{1,0:T(8,128)(2,1)S(1)}, bf16[128,128]{1,0:T(8,128)(2,1)S(1)}, u32[]{:S(2)}, u32[]{:S(2)}) collective-permute-start(bf16[128,128]{1,0:T(8,128)(2,1)S(1)} %get-tuple-element.47), channel_id=1, source_target_pairs={{0,1},{1,0},{2,3},{3,2},{4,5},{5,4},{6,7},{7,6},{8,9},{9,8},{10,11... | collective-permute-start | bytes 98312 | tf_op jit(solution)/shard_map/ppermute | solution.py:337
  39.6 3.4 %collective-permute-start.12 = (bf16[128,128]{1,0:T(8,128)(2,1)S(1)}, bf16[128,128]{1,0:T(8,128)(2,1)S(1)}, u32[]{:S(2)}, u32[]{:S(2)}) collective-permute-start(bf16[128,128]{1,0:T(8,128)(2,1)S(1)} %get-tuple-element.48), channel_id=1, source_target_pairs={{0,9},{1,8},{2,11},{3,10},{4,13},{5,12},{6,15},{7,14},{8,1},{9,0},... | collective-permute-start | bytes 98312 | tf_op jit(solution)/shard_map/ppermute | solution.py:337
  43.5 8.7 %collective-permute-start.14 = (bf16[32,2048]{1,0:T(8,128)(2,1)S(1)}, bf16[32,2048]{1,0:T(8,128)(2,1)S(1)}, u32[]{:S(2)}, u32[]{:S(2)}) collective-permute-start(bf16[32,2048]{1,0:T(8,128)(2,1)S(1)} %get-tuple-element.50), channel_id=1, source_target_pairs={{0,5},{1,4},{2,7},{3,6},{4,1},{5,0},{6,3},{7,2},{8,13},{9,12},{10,... | collective-permute-start | bytes 393224 | tf_op jit(solution)/shard_map/ppermute | solution.py:439
  48.7 10.0 %collective-permute-start.15 = (bf16[32,2048]{1,0:T(8,128)(2,1)S(1)}, bf16[32,2048]{1,0:T(8,128)(2,1)S(1)}, u32[]{:S(2)}, u32[]{:S(2)}) collective-permute-start(bf16[32,2048]{1,0:T(8,128)(2,1)S(1)} %get-tuple-element.51), channel_id=1, source_target_pairs={{0,6},{1,3},{2,0},{3,5},{4,2},{5,7},{6,4},{7,1},{8,14},{9,11},{10,... | collective-permute-start | bytes 393224 | tf_op jit(solution)/shard_map/ppermute | solution.py:439
  48.9 11.1 %collective-permute-start.16 = (bf16[32,2048]{1,0:T(8,128)(2,1)S(1)}, bf16[32,2048]{1,0:T(8,128)(2,1)S(1)}, u32[]{:S(2)}, u32[]{:S(2)}) collective-permute-start(bf16[32,2048]{1,0:T(8,128)(2,1)S(1)} %get-tuple-element.52), channel_id=1, source_target_pairs={{0,7},{1,2},{2,1},{3,4},{4,3},{5,6},{6,5},{7,0},{8,15},{9,10},{10,... | collective-permute-start | bytes 393224 | tf_op jit(solution)/shard_map/ppermute | solution.py:439

commit v8 on v7

--- a/solution.py
+++ b/solution.py
@@ -251,26 +251,34 @@
     return [(source[0, r, :], jnp.transpose(source[1, r, :].astype(f32)).astype(bf16)) for r in rows]
 
 
-def attend_a_body(q, kv, far, rows_out, result_out):
-    chip = lax.axis_index("x") * 4 + lax.axis_index("y")
+def store_partial(rows_out, result_out, found):
+    lines = []
+    for j, (top, total, result) in enumerate(found):
+        lines += [top, total]
+        result_out[:, j * HALF : (j + 1) * HALF] = result
+    rows_out[...] = jnp.concatenate((*lines, jnp.zeros((4, HALF), f32)), axis=0)
+
+
+def attend_own_body(q, kv, rows_out, result_out):
     row, col = iotas((HALF, HALF))
-    old, own = blocks_of(far), blocks_of(kv)
-    held = chip >= 2
-    lines = []
-    for j in range(2):
-        parts = [(*old[j], (row > col) & held)]
-        if j == 0:
-            parts.append((*old[1], held))
-        else:
-            parts.append((*own[0], None))
-        parts.append((*own[j], row <= col))
+    own, found = blocks_of(kv), []
+    for j in range(2):
+        parts = [(*own[0], None)] * j + [(*own[j], row <= col)]
+        start = None, jnp.zeros((1, HALF), f32), jnp.zeros((E, HALF), f32)
+        found.append(products_of(parts, q[j * HALF : (j + 1) * HALF, :], *start))
+    store_partial(rows_out, result_out, found)
+
+
+def attend_a_body(q, far, rows, first, rows_out, result_out):
+    held = lax.axis_index("x") * 4 + lax.axis_index("y") >= 2
+    row, col = iotas((HALF, HALF))
+    old, found = blocks_of(far), []
+    for j in range(2):
         at = slice(j * HALF, (j + 1) * HALF)
-        top, total, result = products_of(
-            parts, q[at, :], None, jnp.zeros((1, HALF), f32), jnp.zeros((E, HALF), f32)
-        )
-        lines += [top, total]
-        result_out[:, at] = result
-    rows_out[...] = jnp.concatenate((*lines, jnp.zeros((4, HALF), f32)), axis=0)
+        parts = [(*old[j], (row > col) & held)] + [(*old[1], held)] * (1 - j)
+        top, total = rows[2 * j : 2 * j + 1, :], rows[2 * j + 1 : 2 * j + 2, :]
+        found.append(products_of(parts, q[at, :], top, total, first[:, at]))
+    store_partial(rows_out, result_out, found)
 
 
 def attend_body(q, near, rows, first, mesa, keep_out, c_out, z_out, cz_out, place):
@@ -407,7 +415,10 @@
         *around_x,
     )
     near, far = halos
-    partial = call(attend_a_body, [((8, HALF), f32), ((E, CHIP), f32)], [], 1 << 28, q, kv, far)
+    partial = call(attend_own_body, [((8, HALF), f32), ((E, CHIP), f32)], [], 1 << 27, q, kv)
+    partial = call(
+        attend_a_body, [((8, HALF), f32), ((E, CHIP), f32)], [], 1 << 28, q, far, *partial
+    )
     kept, to_c, to_z, to_cz = call(
         attend_body,
         [((HALF // 2, E), bf16)] * 4,

time: 60.9 us -> 60.4 us (level)
  waiting for transfers between devices: 23.8 us -> 23 us
    ppermute x6, waiting for transfers between devices: 11.8 us -> 11 us  [turned(): return lax.ppermute(x, axis, [(i, (i + by) % 4) for i in range(4)])]
    pallas_call x8 -> x9, Pallas kernels: 8.63 us -> 8.89 us  [call(): pl.pallas_call(body, out_shape=[jax.ShapeDtypeStruct(shape, kind) for sha...]
  transfers between devices with their start and end apart: 17 -> 17, of which waited for: 9 -> 9; matrix products, arithmetic and copies ran while one was open for 2% -> 2% of each run, Pallas kernels for 12% -> 13%
where the time goes in v8:
time: 60.4 us; the launch traced here: 60.3 us
  starting transfers between devices  27.1 us (45%)
  waiting for transfers between devices  23 us (38%)
  Pallas kernels  8.89 us (15%)
  local copies, waits for them, and re-layouts  1.05 us (2%)
    ppermute x6, waiting for transfers between devices, turned(): return lax.ppermute(x, axis, [(i, (i + by) % 4) for i in range(4)])  11 us
    pallas_call x9, Pallas kernels, call(): pl.pallas_call(body, out_shape=[jax.ShapeDtypeStruct(shape, kind) for sha...  8.89 us
    ppermute x6, starting transfers between devices, across(): return lax.ppermute(x, ('c', 'z'), pairs)  8.86 us
    ppermute x3, starting transfers between devices, on_device(): got.append(lax.ppermute(share, 'z', pairs))  8.33 us
    ppermute x3, waiting for transfers between devices, on_device(): got.append(lax.ppermute(share, 'z', pairs))  8.29 us
    ppermute x6, starting transfers between devices, turned(): return lax.ppermute(x, axis, [(i, (i + by) % 4) for i in range(4)])  6.52 us
    ppermute x6, waiting for transfers between devices, across(): return lax.ppermute(x, ('c', 'z'), pairs)  3.65 us
    ppermute x2, starting transfers between devices, beyond(): return lax.ppermute(x, XY, [(i, (i + by) % 16) for i in range(16)])  3.37 us
  transfers between devices with their start and end apart: 17, of which 9 were waited for; matrix products, arithmetic and copies ran while one was open for 2% of the time, Pallas kernels for 13%

profile of v8, /device:TPU:1, one launch (start us, length us, event | category | flops | bytes accessed | tf_op | source)
XLA Modules:
  0.0 60.3 jit_solution(5555739688260855339)
XLA Ops:
  0.0 0.0 copy-start.1
  0.0 2.5 %collective-permute-start.13 = (bf16[256,2048]{1,0:T(8,128)(2,1)}, bf16[256,2048]{1,0:T(8,128)(2,1)S(1)}, u32[]{:S(2)}, u32[]{:S(2)}) collective-permute-start(bf16[256,2048]{1,0:T(8,128)(2,1)} %own_weight.1), channel_id=1, source_target_pairs={{0,1},{1,0},{2,3},{3,2},{4,5},{5,4},{6,7},{7,6},{8,9},{9,8},{10,11... | collective-permute-start | bytes 3145736 | tf_op jit(solution)/shard_map/ppermute | solution.py:345
  2.5 1.0 %copy_bitcast_fusion = (bf16[1,256,2,128]{3,1,0,2:T(8,128)(2,1)S(1)}, bf16[1,256,2,128]{3,1,0,2:T(8,128)(2,1)S(1)}) fusion(bf16[256,2,128]{2,1,0:T(2,128)(2,1)} %param.8, bf16[256,2,128]{2,1,0:T(2,128)(2,1)} %param.7), kind=kLoop, calls=%fused_computation.3 | loop fusion | bytes 524288 | tf_op jit(solution)/shard_map/stack | solution.py:350
  3.5 0.0 copy-done.1
  3.6 0.0 copy-start.2
  3.6 0.0 copy-start.3
  3.6 1.0 %collective-permute-start = (bf16[3,256,128]{2,1,0:T(8,128)(2,1)S(1)}, bf16[3,256,128]{2,1,0:T(8,128)(2,1)S(1)}, u32[]{:S(2)}, u32[]{:S(2)}) collective-permute-start(bf16[3,256,128]{2,1,0:T(8,128)(2,1)S(1)} %get-tuple-element.57), channel_id=1, source_target_pairs={{0,8},{1,9},{2,10},{3,11},{4,12},{5,13},{6,14},{7,15},{8,0},{9,1},... | collective-permute-start | bytes 589832 | tf_op jit(solution)/shard_map/ppermute | solution.py:345
  4.7 0.0 copy-done.2
  4.7 0.0 copy-done.3
  4.7 0.7 %collective-permute-start.1 = (f32[2,256]{1,0:T(2,128)S(1)}, f32[2,256]{1,0:T(2,128)S(1)}, u32[]{:S(2)}, u32[]{:S(2)}) collective-permute-start(f32[2,256]{1,0:T(2,128)S(1)} %get-tuple-element.59), channel_id=1, source_target_pairs={{0,8},{1,9},{2,10},{3,11},{4,12},{5,13},{6,14},{7,15},{8,0},{9,1},... | collective-permute-start | bytes 6152 | tf_op jit(solution)/shard_map/ppermute | solution.py:345
  5.4 0.8 %collective-permute-done.1.gate_recv = f32[2,256]{1,0:T(2,128)S(1)} collective-permute-done((f32[2,256]{1,0:T(2,128)S(1)}, f32[2,256]{1,0:T(2,128)S(1)}, u32[]{:S(2)}, u32[]{:S(2)}) %collective-permute-start.1) | collective-permute-done | bytes 2080 | tf_op jit(solution)/shard_map/ppermute | solution.py:345
  6.2 0.0 collective-permute-done.recv
  6.2 0.8 %shard_map.64 = (bf16[512,128]{1,0:T(8,128)(2,1)S(1)}, bf16[2,512,128]{2,1,0:T(8,128)(2,1)S(1)}, f32[8,256]{1,0:T(8,128)S(1)}, bf16[208,128]{1,0:T(8,128)(2,1)S(1)}, f32[256,128]{1,0:T(8,128)S(1)}) custom-call(bf16[3,256,128]{2,1,0:T(8,128)(2,1)S(1)} %get-tuple-element.58.keep, bf16[3,256,128]{2,1,0:T(8,128)(2,1)S(1)} %collective-permute-done.recv, ...), custom_call_target="tpu_custom_call" | custom-call | flops 67108864 | bytes 1048576 | tf_op jit(solution)/shard_map/pallas_call | solution.py:33
  7.0 1.4 %collective-permute-start.4 = (bf16[208,128]{1,0:T(8,128)(2,1)S(1)}, bf16[208,128]{1,0:T(8,128)(2,1)S(1)}, u32[]{:S(2)}, u32[]{:S(2)}) collective-permute-start(bf16[208,128]{1,0:T(8,128)(2,1)S(1)} %get-tuple-element.39.own), channel_id=1, source_target_pairs={{0,16},{16,32},{32,48},{48,0},{1,17},{17,33},{33,49},{49,1},{2,18}... | collective-permute-start | bytes 159752 | tf_op jit(solution)/shard_map/ppermute | solution.py:340
  8.4 2.6 %collective-permute-start.3 = (bf16[2,512,128]{2,1,0:T(8,128)(2,1)S(1)}, bf16[2,512,128]{2,1,0:T(8,128)(2,1)S(1)}, u32[]{:S(2)}, u32[]{:S(2)}) collective-permute-start(bf16[2,512,128]{2,1,0:T(8,128)(2,1)S(1)} %get-tuple-element.32.kv), channel_id=1, source_target_pairs={{0,32},{16,48},{32,64},{48,80},{64,96},{80,112},{96,128},{112,144}... | collective-permute-start | bytes 786440 | tf_op jit(solution)/shard_map/ppermute | solution.py:336
  11.0 1.3 %collective-permute-start.5 = (bf16[208,128]{1,0:T(8,128)(2,1)S(1)}, bf16[208,128]{1,0:T(8,128)(2,1)S(1)}, u32[]{:S(2)}, u32[]{:S(2)}) collective-permute-start(bf16[208,128]{1,0:T(8,128)(2,1)S(1)} %get-tuple-element.39.own), channel_id=1, source_target_pairs={{0,32},{16,48},{32,0},{48,16},{1,33},{17,49},{33,1},{49,17},{2,34}... | collective-permute-start | bytes 159752 | tf_op jit(solution)/shard_map/ppermute | solution.py:340
  12.3 0.7 %collective-permute-start.6 = (bf16[208,128]{1,0:T(8,128)(2,1)S(1)}, bf16[208,128]{1,0:T(8,128)(2,1)S(1)}, u32[]{:S(2)}, u32[]{:S(2)}) collective-permute-start(bf16[208,128]{1,0:T(8,128)(2,1)S(1)} %get-tuple-element.39.own), channel_id=1, source_target_pairs={{0,48},{16,0},{32,16},{48,32},{1,49},{17,1},{33,17},{49,33},{2,50}... | collective-permute-start | bytes 159752 | tf_op jit(solution)/shard_map/ppermute | solution.py:340
  13.0 0.0 collective-permute-done.4.r1
  13.0 0.7 %collective-permute-start.2 = (bf16[2,512,128]{2,1,0:T(8,128)(2,1)S(1)}, bf16[2,512,128]{2,1,0:T(8,128)(2,1)S(1)}, u32[]{:S(2)}, u32[]{:S(2)}) collective-permute-start(bf16[2,512,128]{2,1,0:T(8,128)(2,1)S(1)} %get-tuple-element.32.kv), channel_id=1, source_target_pairs={{0,16},{16,32},{32,48},{48,64},{64,80},{80,96},{96,112},{112,128},... | collective-permute-start | bytes 786440 | tf_op jit(solution)/shard_map/ppermute | solution.py:336
  13.7 8.0 %collective-permute-done.5.r2 = bf16[208,128]{1,0:T(8,128)(2,1)S(1)} collective-permute-done((bf16[208,128]{1,0:T(8,128)(2,1)S(1)}, bf16[208,128]{1,0:T(8,128)(2,1)S(1)}, u32[]{:S(2)}, u32[]{:S(2)}) %collective-permute-start.5) | collective-permute-done | bytes 53280 | tf_op jit(solution)/shard_map/ppermute | solution.py:340
  21.8 0.0 collective-permute-done.6.r3
  21.8 0.1 shard_map.67
  21.9 0.4 collective-permute-start.7
  22.3 2.4 %collective-permute-start.8 = (bf16[208,128]{1,0:T(8,128)(2,1)S(1)}, bf16[208,128]{1,0:T(8,128)(2,1)S(1)}, u32[]{:S(2)}, u32[]{:S(2)}) collective-permute-start(bf16[208,128]{1,0:T(8,128)(2,1)S(1)} %get-tuple-element.48), channel_id=1, source_target_pairs={{0,128},{64,192},{128,0},{192,64},{1,129},{65,193},{129,1},{193,65... | collective-permute-start | bytes 159752 | tf_op jit(solution)/shard_map/ppermute | solution.py:340
  24.7 1.8 %collective-permute-done.7.t1 = bf16[208,128]{1,0:T(8,128)(2,1)S(1)} collective-permute-done((bf16[208,128]{1,0:T(8,128)(2,1)S(1)}, bf16[208,128]{1,0:T(8,128)(2,1)S(1)}, u32[]{:S(2)}, u32[]{:S(2)}) %collective-permute-start.7) | collective-permute-done | bytes 53280 | tf_op jit(solution)/shard_map/ppermute | solution.py:340
  26.5 0.3 collective-permute-start.9
  26.8 0.6 shard_map.68
  27.4 0.8 %shard_map.65 = (f32[8,256]{1,0:T(8,128)S(1)}, f32[128,512]{1,0:T(8,128)S(1)}) custom-call(bf16[512,128]{1,0:T(8,128)(2,1)S(1)} %get-tuple-element.31.q, bf16[2,512,128]{2,1,0:T(8,128)(2,1)S(1)} %get-tuple-element.32.kv), custom_call_target="tpu_custom_call" | custom-call | flops 134217728 | bytes 1048576 | tf_op jit(solution)/shard_map/pallas_call | solution.py:33
  28.2 0.0 collective-permute-done.8.t2
  28.2 1.2 %collective-permute-done.9.t3 = bf16[208,128]{1,0:T(8,128)(2,1)S(1)} collective-permute-done((bf16[208,128]{1,0:T(8,128)(2,1)S(1)}, bf16[208,128]{1,0:T(8,128)(2,1)S(1)}, u32[]{:S(2)}, u32[]{:S(2)}) %collective-permute-start.9) | collective-permute-done | bytes 53280 | tf_op jit(solution)/shard_map/ppermute | solution.py:340
  29.5 3.8 %shard_map.69.mesa = f32[128,512]{1,0:T(8,128)S(1)} custom-call(bf16[2,512,128]{2,1,0:T(8,128)(2,1)S(1)} %get-tuple-element.32.kv, f32[8,256]{1,0:T(8,128)S(1)} %get-tuple-element.37.gates, f32[256,128]{1,0:T(8,128)S(1)} %get-tuple-element.38.first, f32[208,128]{1,0:T(8,128)S(1)} %get-tuple-element.40.state, f32[8,128]{1,0:T(8,128)S(1)} %get-tuple-element.41.lead, ...), custom_call_target="tpu_custom_call" | custom-call | flops 1073741824 | bytes 1048576 | tf_op jit(solution)/shard_map/pallas_call | solution.py:33
  33.3 0.0 collective-permute-done.3.far
  33.3 0.6 shard_map.66
  33.9 0.0 copy-start
  33.9 0.0 collective-permute-done.2.near
  33.9 1.0 %shard_map.70 = (bf16[128,128]{1,0:T(8,128)(2,1)S(1)}, bf16[128,128]{1,0:T(8,128)(2,1)S(1)}, bf16[128,128]{1,0:T(8,128)(2,1)S(1)}, bf16[128,128]{1,0:T(8,128)(2,1)S(1)}) custom-call(bf16[512,128]{1,0:T(8,128)(2,1)S(1)} %get-tuple-element.31.q, bf16[2,512,128]{2,1,0:T(8,128)(2,1)S(1)} %collective-permute-done.2.near, f32[8,256]{1,0:T(8,128)S(1)} %get-tuple-element.35.rows, ...), custom_call_target="tpu_custom_call" | custom-call | flops 536870912 | bytes 1048576 | tf_op jit(solution)/shard_map/pallas_call | solution.py:33
  35.0 3.0 %collective-permute-start.10 = (bf16[128,128]{1,0:T(8,128)(2,1)S(1)}, bf16[128,128]{1,0:T(8,128)(2,1)S(1)}, u32[]{:S(2)}, u32[]{:S(2)}) collective-permute-start(bf16[128,128]{1,0:T(8,128)(2,1)S(1)} %get-tuple-element.50), channel_id=1, source_target_pairs={{0,8},{1,9},{2,10},{3,11},{4,12},{5,13},{6,14},{7,15},{8,0},{9,1},... | collective-permute-start | bytes 98312 | tf_op jit(solution)/shard_map/ppermute | solution.py:345
  37.9 1.2 %collective-permute-start.11 = (bf16[128,128]{1,0:T(8,128)(2,1)S(1)}, bf16[128,128]{1,0:T(8,128)(2,1)S(1)}, u32[]{:S(2)}, u32[]{:S(2)}) collective-permute-start(bf16[128,128]{1,0:T(8,128)(2,1)S(1)} %get-tuple-element.51), channel_id=1, source_target_pairs={{0,1},{1,0},{2,3},{3,2},{4,5},{5,4},{6,7},{7,6},{8,9},{9,8},{10,11... | collective-permute-start | bytes 98312 | tf_op jit(solution)/shard_map/ppermute | solution.py:345
  39.1 0.6 collective-permute-start.12
  39.7 0.0 collective-permute-done.10.from_c
  39.7 1.0 %collective-permute-done.11.from_z = bf16[128,128]{1,0:T(8,128)(2,1)S(1)} collective-permute-done((bf16[128,128]{1,0:T(8,128)(2,1)S(1)}, bf16[128,128]{1,0:T(8,128)(2,1)S(1)}, u32[]{:S(2)}, u32[]{:S(2)}) %collective-permute-start.11) | collective-permute-done | bytes 32800 | tf_op jit(solution)/shard_map/ppermute | solution.py:345
  40.7 1.8 %collective-permute-done.12.from_cz = bf16[128,128]{1,0:T(8,128)(2,1)S(1)} collective-permute-done((bf16[128,128]{1,0:T(8,128)(2,1)S(1)}, bf16[128,128]{1,0:T(8,128)(2,1)S(1)}, u32[]{:S(2)}, u32[]{:S(2)}) %collective-permute-start.12) | collective-permute-done | bytes 32800 | tf_op jit(solution)/shard_map/ppermute | solution.py:345
  42.5 0.0 collective-permute-done.13.pair_weight
  42.5 0.0 copy-done
  42.5 0.4 shard_map.71
  42.9 5.2 %collective-permute-start.14 = (bf16[32,2048]{1,0:T(8,128)(2,1)S(1)}, bf16[32,2048]{1,0:T(8,128)(2,1)S(1)}, u32[]{:S(2)}, u32[]{:S(2)}) collective-permute-start(bf16[32,2048]{1,0:T(8,128)(2,1)S(1)} %get-tuple-element.54), channel_id=1, source_target_pairs={{0,5},{1,4},{2,7},{3,6},{4,1},{5,0},{6,3},{7,2},{8,13},{9,12},{10,... | collective-permute-start | bytes 393224 | tf_op jit(solution)/shard_map/ppermute | solution.py:450
  48.1 0.3 collective-permute-start.15
  48.4 2.9 %collective-permute-start.16 = (bf16[32,2048]{1,0:T(8,128)(2,1)S(1)}, bf16[32,2048]{1,0:T(8,128)(2,1)S(1)}, u32[]{:S(2)}, u32[]{:S(2)}) collective-permute-start(bf16[32,2048]{1,0:T(8,128)(2,1)S(1)} %get-tuple-element.56), channel_id=1, source_target_pairs={{0,7},{1,2},{2,1},{3,4},{4,3},{5,6},{6,5},{7,0},{8,15},{9,10},{10,... | collective-permute-start | bytes 393224 | tf_op jit(solution)/shard_map/ppermute | solution.py:450
  51.3 0.4 collective-permute-done.14.a
  51.6 6.5 %collective-permute-done.15.b = bf16[32,2048]{1,0:T(8,128)(2,1)S(1)} collective-permute-done((bf16[32,2048]{1,0:T(8,128)(2,1)S(1)}, bf16[32,2048]{1,0:T(8,128)(2,1)S(1)}, u32[]{:S(2)}, u32[]{:S(2)}) %collective-permute-start.15) | collective-permute-done | bytes 131104 | tf_op jit(solution)/shard_map/ppermute | solution.py:450
  58.2 1.4 %collective-permute-done.16.c = bf16[32,2048]{1,0:T(8,128)(2,1)S(1)} collective-permute-done((bf16[32,2048]{1,0:T(8,128)(2,1)S(1)}, bf16[32,2048]{1,0:T(8,128)(2,1)S(1)}, u32[]{:S(2)}, u32[]{:S(2)}) %collective-permute-start.16) | collective-permute-done | bytes 131104 | tf_op jit(solution)/shard_map/ppermute | solution.py:450
  59.6 0.7 %shard_map.72 = bf16[32,2048]{1,0:T(8,128)(2,1)} custom-call(f32[32,2048]{1,0:T(8,128)S(1)} %get-tuple-element.53.mine, bf16[32,2048]{1,0:T(8,128)(2,1)S(1)} %collective-permute-done.14.a, bf16[32,2048]{1,0:T(8,128)(2,1)S(1)} %collective-permute-done.15.b, bf16[32,2048]{1,0:T(8,128)(2,1)S(1)} %collective-permute-done.16.c), custom_call_target="tpu_custom_call" | custom-call | flops 262144 | bytes 1048576 | tf_op jit(solution)/shard_map/pallas_call | solution.py:33
  (6 shorter events, 0.1 us)
Async XLA Ops:
  0.0 3.5 %copy-start.1 = (bf16[256,2,128]{2,1,0:T(2,128)(2,1)S(1)}, bf16[256,2,128]{2,1,0:T(2,128)(2,1)}, u32[]{:S(2)}) copy-start(bf16[256,2,128]{2,1,0:T(2,128)(2,1)} %param.6) | copy-start | bytes 393220
  0.0 42.5 %collective-permute-start.13 = (bf16[256,2048]{1,0:T(8,128)(2,1)}, bf16[256,2048]{1,0:T(8,128)(2,1)S(1)}, u32[]{:S(2)}, u32[]{:S(2)}) collective-permute-start(bf16[256,2048]{1,0:T(8,128)(2,1)} %own_weight.1), channel_id=1, source_target_pairs={{0,1},{1,0},{2,3},{3,2},{4,5},{5,4},{6,7},{7,6},{8,9},{9,8},{10,11... | collective-permute-start | bytes 3145736 | tf_op jit(solution)/shard_map/ppermute | solution.py:345
  3.6 1.1 %copy-start.2 = (f32[2,256]{1,0:T(2,128)S(1)}, f32[2,256]{1,0:T(2,128)}, u32[]{:S(2)}) copy-start(f32[2,256]{1,0:T(2,128)} %param.9) | copy-start | bytes 6148
  3.6 1.1 %copy-start.3 = (f32[2,256]{1,0:T(2,128)S(1)}, f32[2,256]{1,0:T(2,128)}, u32[]{:S(2)}) copy-start(f32[2,256]{1,0:T(2,128)} %param.10) | copy-start | bytes 6148
  3.6 2.6 %collective-permute-start = (bf16[3,256,128]{2,1,0:T(8,128)(2,1)S(1)}, bf16[3,256,128]{2,1,0:T(8,128)(2,1)S(1)}, u32[]{:S(2)}, u32[]{:S(2)}) collective-permute-start(bf16[3,256,128]{2,1,0:T(8,128)(2,1)S(1)} %get-tuple-element.57), channel_id=1, source_target_pairs={{0,8},{1,9},{2,10},{3,11},{4,12},{5,13},{6,14},{7,15},{8,0},{9,1},... | collective-permute-start | bytes 589832 | tf_op jit(solution)/shard_map/ppermute | solution.py:345
  4.7 1.5 %collective-permute-start.1 = (f32[2,256]{1,0:T(2,128)S(1)}, f32[2,256]{1,0:T(2,128)S(1)}, u32[]{:S(2)}, u32[]{:S(2)}) collective-permute-start(f32[2,256]{1,0:T(2,128)S(1)} %get-tuple-element.59), channel_id=1, source_target_pairs={{0,8},{1,9},{2,10},{3,11},{4,12},{5,13},{6,14},{7,15},{8,0},{9,1},... | collective-permute-start | bytes 6152 | tf_op jit(solution)/shard_map/ppermute | solution.py:345
  7.0 6.0 %collective-permute-start.4 = (bf16[208,128]{1,0:T(8,128)(2,1)S(1)}, bf16[208,128]{1,0:T(8,128)(2,1)S(1)}, u32[]{:S(2)}, u32[]{:S(2)}) collective-permute-start(bf16[208,128]{1,0:T(8,128)(2,1)S(1)} %get-tuple-element.39.own), channel_id=1, source_target_pairs={{0,16},{16,32},{32,48},{48,0},{1,17},{17,33},{33,49},{49,1},{2,18}... | collective-permute-start | bytes 159752 | tf_op jit(solution)/shard_map/ppermute | solution.py:340
  8.4 24.9 %collective-permute-start.3 = (bf16[2,512,128]{2,1,0:T(8,128)(2,1)S(1)}, bf16[2,512,128]{2,1,0:T(8,128)(2,1)S(1)}, u32[]{:S(2)}, u32[]{:S(2)}) collective-permute-start(bf16[2,512,128]{2,1,0:T(8,128)(2,1)S(1)} %get-tuple-element.32.kv), channel_id=1, source_target_pairs={{0,32},{16,48},{32,64},{48,80},{64,96},{80,112},{96,128},{112,144}... | collective-permute-start | bytes 786440 | tf_op jit(solution)/shard_map/ppermute | solution.py:336
  11.0 10.8 %collective-permute-start.5 = (bf16[208,128]{1,0:T(8,128)(2,1)S(1)}, bf16[208,128]{1,0:T(8,128)(2,1)S(1)}, u32[]{:S(2)}, u32[]{:S(2)}) collective-permute-start(bf16[208,128]{1,0:T(8,128)(2,1)S(1)} %get-tuple-element.39.own), channel_id=1, source_target_pairs={{0,32},{16,48},{32,0},{48,16},{1,33},{17,49},{33,1},{49,17},{2,34}... | collective-permute-start | bytes 159752 | tf_op jit(solution)/shard_map/ppermute | solution.py:340
  12.3 9.5 %collective-permute-start.6 = (bf16[208,128]{1,0:T(8,128)(2,1)S(1)}, bf16[208,128]{1,0:T(8,128)(2,1)S(1)}, u32[]{:S(2)}, u32[]{:S(2)}) collective-permute-start(bf16[208,128]{1,0:T(8,128)(2,1)S(1)} %get-tuple-element.39.own), channel_id=1, source_target_pairs={{0,48},{16,0},{32,16},{48,32},{1,49},{17,1},{33,17},{49,33},{2,50}... | collective-permute-start | bytes 159752 | tf_op jit(solution)/shard_map/ppermute | solution.py:340
  13.0 20.9 %collective-permute-start.2 = (bf16[2,512,128]{2,1,0:T(8,128)(2,1)S(1)}, bf16[2,512,128]{2,1,0:T(8,128)(2,1)S(1)}, u32[]{:S(2)}, u32[]{:S(2)}) collective-permute-start(bf16[2,512,128]{2,1,0:T(8,128)(2,1)S(1)} %get-tuple-element.32.kv), channel_id=1, source_target_pairs={{0,16},{16,32},{32,48},{48,64},{64,80},{80,96},{96,112},{112,128},... | collective-permute-start | bytes 786440 | tf_op jit(solution)/shard_map/ppermute | solution.py:336
  21.9 4.6 %collective-permute-start.7 = (bf16[208,128]{1,0:T(8,128)(2,1)S(1)}, bf16[208,128]{1,0:T(8,128)(2,1)S(1)}, u32[]{:S(2)}, u32[]{:S(2)}) collective-permute-start(bf16[208,128]{1,0:T(8,128)(2,1)S(1)} %get-tuple-element.48), channel_id=1, source_target_pairs={{0,64},{64,128},{128,192},{192,0},{1,65},{65,129},{129,193},{193,1... | collective-permute-start | bytes 159752 | tf_op jit(solution)/shard_map/ppermute | solution.py:340
  22.3 5.9 %collective-permute-start.8 = (bf16[208,128]{1,0:T(8,128)(2,1)S(1)}, bf16[208,128]{1,0:T(8,128)(2,1)S(1)}, u32[]{:S(2)}, u32[]{:S(2)}) collective-permute-start(bf16[208,128]{1,0:T(8,128)(2,1)S(1)} %get-tuple-element.48), channel_id=1, source_target_pairs={{0,128},{64,192},{128,0},{192,64},{1,129},{65,193},{129,1},{193,65... | collective-permute-start | bytes 159752 | tf_op jit(solution)/shard_map/ppermute | solution.py:340
  26.5 3.0 %collective-permute-start.9 = (bf16[208,128]{1,0:T(8,128)(2,1)S(1)}, bf16[208,128]{1,0:T(8,128)(2,1)S(1)}, u32[]{:S(2)}, u32[]{:S(2)}) collective-permute-start(bf16[208,128]{1,0:T(8,128)(2,1)S(1)} %get-tuple-element.48), channel_id=1, source_target_pairs={{0,192},{64,0},{128,64},{192,128},{1,193},{65,1},{129,65},{193,129... | collective-permute-start | bytes 159752 | tf_op jit(solution)/shard_map/ppermute | solution.py:340
  33.9 8.6 %copy-start = (bf16[256,2048]{1,0:T(8,128)(2,1)S(1)}, bf16[256,2048]{1,0:T(8,128)(2,1)}, u32[]{:S(2)}) copy-start(bf16[256,2048]{1,0:T(8,128)(2,1)} %own_weight.1) | copy-start | bytes 3145732
  35.0 4.7 %collective-permute-start.10 = (bf16[128,128]{1,0:T(8,128)(2,1)S(1)}, bf16[128,128]{1,0:T(8,128)(2,1)S(1)}, u32[]{:S(2)}, u32[]{:S(2)}) collective-permute-start(bf16[128,128]{1,0:T(8,128)(2,1)S(1)} %get-tuple-element.50), channel_id=1, source_target_pairs={{0,8},{1,9},{2,10},{3,11},{4,12},{5,13},{6,14},{7,15},{8,0},{9,1},... | collective-permute-start | bytes 98312 | tf_op jit(solution)/shard_map/ppermute | solution.py:345
  37.9 2.8 %collective-permute-start.11 = (bf16[128,128]{1,0:T(8,128)(2,1)S(1)}, bf16[128,128]{1,0:T(8,128)(2,1)S(1)}, u32[]{:S(2)}, u32[]{:S(2)}) collective-permute-start(bf16[128,128]{1,0:T(8,128)(2,1)S(1)} %get-tuple-element.51), channel_id=1, source_target_pairs={{0,1},{1,0},{2,3},{3,2},{4,5},{5,4},{6,7},{7,6},{8,9},{9,8},{10,11... | collective-permute-start | bytes 98312 | tf_op jit(solution)/shard_map/ppermute | solution.py:345
  39.1 3.4 %collective-permute-start.12 = (bf16[128,128]{1,0:T(8,128)(2,1)S(1)}, bf16[128,128]{1,0:T(8,128)(2,1)S(1)}, u32[]{:S(2)}, u32[]{:S(2)}) collective-permute-start(bf16[128,128]{1,0:T(8,128)(2,1)S(1)} %get-tuple-element.52), channel_id=1, source_target_pairs={{0,9},{1,8},{2,11},{3,10},{4,13},{5,12},{6,15},{7,14},{8,1},{9,0},... | collective-permute-start | bytes 98312 | tf_op jit(solution)/shard_map/ppermute | solution.py:345
  42.9 8.7 %collective-permute-start.14 = (bf16[32,2048]{1,0:T(8,128)(2,1)S(1)}, bf16[32,2048]{1,0:T(8,128)(2,1)S(1)}, u32[]{:S(2)}, u32[]{:S(2)}) collective-permute-start(bf16[32,2048]{1,0:T(8,128)(2,1)S(1)} %get-tuple-element.54), channel_id=1, source_target_pairs={{0,5},{1,4},{2,7},{3,6},{4,1},{5,0},{6,3},{7,2},{8,13},{9,12},{10,... | collective-permute-start | bytes 393224 | tf_op jit(solution)/shard_map/ppermute | solution.py:450
  48.1 10.0 %collective-permute-start.15 = (bf16[32,2048]{1,0:T(8,128)(2,1)S(1)}, bf16[32,2048]{1,0:T(8,128)(2,1)S(1)}, u32[]{:S(2)}, u32[]{:S(2)}) collective-permute-start(bf16[32,2048]{1,0:T(8,128)(2,1)S(1)} %get-tuple-element.55), channel_id=1, source_target_pairs={{0,6},{1,3},{2,0},{3,5},{4,2},{5,7},{6,4},{7,1},{8,14},{9,11},{10,... | collective-permute-start | bytes 393224 | tf_op jit(solution)/shard_map/ppermute | solution.py:450
  48.4 11.2 %collective-permute-start.16 = (bf16[32,2048]{1,0:T(8,128)(2,1)S(1)}, bf16[32,2048]{1,0:T(8,128)(2,1)S(1)}, u32[]{:S(2)}, u32[]{:S(2)}) collective-permute-start(bf16[32,2048]{1,0:T(8,128)(2,1)S(1)} %get-tuple-element.56), channel_id=1, source_target_pairs={{0,7},{1,2},{2,1},{3,4},{4,3},{5,6},{6,5},{7,0},{8,15},{9,10},{10,... | collective-permute-start | bytes 393224 | tf_op jit(solution)/shard_map/ppermute | solution.py:450
